TPU v7x, 8 devices: a whole 2x2x1 slice. The times are simulated.
8 devices in a mesh: dp: 2 (over z, y), tp: 4 (over x, core).
Axes of the slice: x: 2, y: 2, z: 1, core: 2. Of those that a mesh axis runs over, the one named last changes fastest.
Arguments:
- x_stored: bfloat16 [6, 16, 1024, 1024], P(None, 'dp')
- u_stored: bfloat16 [6, 16, 1024, 4096], P(None, 'dp', None, 'tp')
- w_up: bfloat16 [6, 1024, 4096], P(None, None, 'tp')
- w_down: bfloat16 [6, 4096, 1024], P(None, 'tp')
- d_out: bfloat16 [16, 1024, 1024], P('dp')
- noise_up: float32 [6, 1024, 4096], P(None, 'dp', 'tp')
- noise_down: float32 [6, 4096, 1024], P(None, 'tp', 'dp')
- clip_up: float32 [6], replicated
- clip_down: float32 [6], replicated
- noise_mult: float32 [1], replicated
Outputs:
- output 1: float32 [6, 1024, 4096], P(None, 'dp', 'tp')
- output 2: float32 [6, 4096, 1024], P(None, 'tp', 'dp')
All inputs are finite; a program needn't handle non-finite values.
Results may differ from a plain program's by a relative error of at most 0.017855.
Values are sent between devices in bfloat16 or wider.
A program may use at most 1.25 GiB of HBM per device.

v0:
```python
import math
import jax
import jax.numpy as jnp
from jax import lax
from jax.sharding import PartitionSpec as P

GELU_SCALE = math.sqrt(2.0 / math.pi)


def gelu_pair(pre_act):
    tanh_val = jnp.tanh(GELU_SCALE * (pre_act + 0.044715 * pre_act * pre_act * pre_act))
    gelu_val = 0.5 * pre_act * (1.0 + tanh_val)
    gelu_slope = 0.5 * (1.0 + tanh_val) + 0.5 * pre_act * (1.0 - tanh_val * tanh_val) * GELU_SCALE * (1.0 + 0.134145 * pre_act * pre_act)
    return gelu_val, gelu_slope


def solution(mesh):
    data_size = mesh.shape["dp"]
    in_specs = (P(None, "dp", None, None), P(None, "dp", None, "tp"), P(None, None, "tp"), P(None, "tp", None), P("dp", None, None), P(None, "dp", "tp"), P(None, "tp", "dp"), P(), P(), P())
    out_specs = (P(None, "dp", "tp"), P(None, "tp", "dp"))

    def local_step(x_stored, u_stored, w_up, w_down, d_out, noise_up, noise_down, clip_up, clip_down, noise_mult):
        num_layers = x_stored.shape[0]
        total_examples = d_out.shape[0] * data_size
        grad_z = d_out
        grads_up = []
        grads_down = []
        for layer in reversed(range(num_layers)):
            x_layer = x_stored[layer]
            gelu_val, gelu_slope = gelu_pair(u_stored[layer].astype(jnp.float32))
            hidden = gelu_val.astype(jnp.bfloat16)
            back_h = jnp.einsum("btd,fd->btf", grad_z, w_down[layer], preferred_element_type=jnp.float32)
            grad_h = (gelu_slope * back_h).astype(jnp.bfloat16)
            part_x = jnp.einsum("btf,df->btd", grad_h, w_up[layer], preferred_element_type=jnp.float32).astype(jnp.bfloat16)
            full_x = lax.psum(part_x, "tp")
            gram_x = jnp.einsum("btd,bsd->bts", x_layer, x_layer, preferred_element_type=jnp.float32)
            gram_dh = jnp.einsum("btf,bsf->bts", grad_h, grad_h, preferred_element_type=jnp.float32)
            gram_h = jnp.einsum("btf,bsf->bts", hidden, hidden, preferred_element_type=jnp.float32)
            gram_dz = jnp.einsum("btd,bsd->bts", grad_z, grad_z, preferred_element_type=jnp.float32)
            part_norms = jnp.stack([jnp.sum(gram_x * gram_dh, axis=(1, 2)), jnp.sum(gram_h * gram_dz, axis=(1, 2))], axis=1)
            ghost_norms = lax.psum(part_norms, "tp")
            scale_up = jnp.minimum(1.0, clip_up[layer] / jnp.sqrt(ghost_norms[:, 0]))
            scale_down = jnp.minimum(1.0, clip_down[layer] / jnp.sqrt(ghost_norms[:, 1]))
            dh_clip = (grad_h * scale_up[:, None, None]).astype(jnp.bfloat16)
            dz_clip = (grad_z * scale_down[:, None, None]).astype(jnp.bfloat16)
            sum_up = jnp.einsum("btd,btf->df", x_layer, dh_clip, preferred_element_type=jnp.float32)
            sum_down = jnp.einsum("btf,btd->fd", hidden, dz_clip, preferred_element_type=jnp.float32)
            sum_up = lax.psum_scatter(sum_up, "dp", scatter_dimension=0, tiled=True)
            sum_down = lax.psum_scatter(sum_down, "dp", scatter_dimension=1, tiled=True)
            grads_up.append((sum_up + noise_mult[0] * clip_up[layer] * noise_up[layer]) / total_examples)
            grads_down.append((sum_down + noise_mult[0] * clip_down[layer] * noise_down[layer]) / total_examples)
            grad_z = (grad_z.astype(jnp.float32) + full_x.astype(jnp.float32)).astype(jnp.bfloat16)
        return jnp.stack(grads_up[::-1]), jnp.stack(grads_down[::-1])

    return jax.shard_map(local_step, mesh=mesh, in_specs=in_specs, out_specs=out_specs, check_vma=False)
```

profile of v0, /device:TPU:0, one launch (start us, length us, event | category | flops | bytes accessed | tf_op | source)
XLA Modules:
  0.0 2740.9 jit_solution(13080075438682540946)
XLA Ops:
  7.2 42.8 %fusion.40 = bf16[8,1024,1024]{2,1,0:T(8,128)(2,1)} fusion(bf16[8,1024,1024]{2,1,0:T(8,128)(2,1)} %param.14, bf16[6,8,1024,1024]{3,2,1,0:T(8,128)(2,1)} %param.11, bf16[6,1024,1024]{2,1,0:T(8,128)(2,1)} %param.13), kind=kOutput, calls=%fused_computation.92 | convolution fusion | flops 17347641344 | bytes 52428800 | tf_op jit(solution)/shard_map/btd,fd->btf/dot_general | solution.py:32
  74.8 41.2 %fusion.204 = f32[8,1024,1024]{2,1,0:T(8,128)} fusion(bf16[6,8,1024,1024]{3,2,1,0:T(8,128)(2,1)} %param.11), kind=kOutput, calls=%fused_computation.294 | convolution fusion | flops 17263755264 | bytes 50331648 | tf_op jit(solution)/shard_map/btf,bsf->bts/dot_general | solution.py:38
  116.0 32.1 %fusion.109 = f32[8,1024,1024]{2,1,0:T(8,128)} fusion(bf16[6,8,1024,1024]{3,2,1,0:T(8,128)(2,1)} %param.10), kind=kOutput, calls=%fused_computation.175 | convolution fusion | flops 17179869184 | bytes 50331648 | tf_op jit(solution)/shard_map/btd,bsd->bts/dot_general | solution.py:36
  148.1 32.3 %fusion.106 = f32[8,1024,1024]{2,1,0:T(8,128)} fusion(bf16[6,8,1024,1024]{3,2,1,0:T(8,128)(2,1)} %param.10), kind=kOutput, calls=%fused_computation.172 | convolution fusion | flops 17179869184 | bytes 50331648 | tf_op jit(solution)/shard_map/btd,bsd->bts/dot_general | solution.py:36
  180.4 32.1 %fusion.103 = f32[8,1024,1024]{2,1,0:T(8,128)} fusion(bf16[6,8,1024,1024]{3,2,1,0:T(8,128)(2,1)} %param.10), kind=kOutput, calls=%fused_computation.169 | convolution fusion | flops 17179869184 | bytes 50331648 | tf_op jit(solution)/shard_map/btd,bsd->bts/dot_general | solution.py:36
  212.6 32.5 %fusion.94 = f32[8,1024,1024]{2,1,0:T(8,128)} fusion(bf16[6,8,1024,1024]{3,2,1,0:T(8,128)(2,1)} %param.10), kind=kOutput, calls=%fused_computation.160 | convolution fusion | flops 17179869184 | bytes 50331648 | tf_op jit(solution)/shard_map/btd,bsd->bts/dot_general | solution.py:36
  245.1 40.9 %fusion.207 = f32[8,1024,1024]{2,1,0:T(8,128)} fusion(bf16[6,8,1024,1024]{3,2,1,0:T(8,128)(2,1)} %param.11), kind=kOutput, calls=%fused_computation.295 | convolution fusion | flops 17263755264 | bytes 50331648 | tf_op jit(solution)/shard_map/btf,bsf->bts/dot_general | solution.py:38
  344.4 32.3 %fusion.100 = f32[8,1024,1024]{2,1,0:T(8,128)} fusion(bf16[6,8,1024,1024]{3,2,1,0:T(8,128)(2,1)} %param.10), kind=kOutput, calls=%fused_computation.166 | convolution fusion | flops 17179869184 | bytes 50331648 | tf_op jit(solution)/shard_map/btd,bsd->bts/dot_general | solution.py:36
  376.7 41.0 %fusion.219 = f32[8,1024,1024]{2,1,0:T(8,128)} fusion(bf16[6,8,1024,1024]{3,2,1,0:T(8,128)(2,1)} %param.11), kind=kOutput, calls=%fused_computation.299 | convolution fusion | flops 17263755264 | bytes 50331648 | tf_op jit(solution)/shard_map/btf,bsf->bts/dot_general | solution.py:38
  417.7 41.4 %fusion.216 = f32[8,1024,1024]{2,1,0:T(8,128)} fusion(bf16[6,8,1024,1024]{3,2,1,0:T(8,128)(2,1)} %param.11), kind=kOutput, calls=%fused_computation.298 | convolution fusion | flops 17263755264 | bytes 50331648 | tf_op jit(solution)/shard_map/btf,bsf->bts/dot_general | solution.py:38
  479.2 43.0 %fusion.34 = bf16[8,1024,1024]{2,1,0:T(8,128)(2,1)} fusion(bf16[8,1024,1024]{2,1,0:T(8,128)(2,1)} %fusion.48, bf16[6,8,1024,1024]{3,2,1,0:T(8,128)(2,1)} %param.11, bf16[6,1024,1024]{2,1,0:T(8,128)(2,1)} %param.13), kind=kOutput, calls=%fused_computation.86 | convolution fusion | flops 17347641344 | bytes 52428800 | tf_op jit(solution)/shard_map/btd,fd->btf/dot_general | solution.py:32
  548.5 41.2 %fusion.213 = f32[8,1024,1024]{2,1,0:T(8,128)} fusion(bf16[6,8,1024,1024]{3,2,1,0:T(8,128)(2,1)} %param.11), kind=kOutput, calls=%fused_computation.297 | convolution fusion | flops 17263755264 | bytes 50331648 | tf_op jit(solution)/shard_map/btf,bsf->bts/dot_general | solution.py:38
  589.7 41.4 %fusion.210 = f32[8,1024,1024]{2,1,0:T(8,128)} fusion(bf16[6,8,1024,1024]{3,2,1,0:T(8,128)(2,1)} %param.11), kind=kOutput, calls=%fused_computation.296 | convolution fusion | flops 17263755264 | bytes 50331648 | tf_op jit(solution)/shard_map/btf,bsf->bts/dot_general | solution.py:38
  631.1 201.0 %all-reduce.9.cloned.1.call-done = bf16[8,1024,1024]{2,1,0:T(8,128)(2,1)} async-done(((bf16[8,1024,1024]{2,1,0:T(8,128)(2,1)}), bf16[8,1024,1024]{2,1,0:T(8,128)(2,1)}) %all-reduce.9.cloned.1.call-update) | async-done | bytes 16777232 | tf_op jit(solution)/shard_map/psum | solution.py:35
  852.2 43.0 %fusion.28 = bf16[8,1024,1024]{2,1,0:T(8,128)(2,1)} fusion(bf16[8,1024,1024]{2,1,0:T(8,128)(2,1)} %fusion.50, bf16[6,8,1024,1024]{3,2,1,0:T(8,128)(2,1)} %param.11, bf16[6,1024,1024]{2,1,0:T(8,128)(2,1)} %param.13), kind=kOutput, calls=%fused_computation.80 | convolution fusion | flops 17347641344 | bytes 52428800 | tf_op jit(solution)/shard_map/btd,fd->btf/dot_general | solution.py:32
  919.5 32.4 %fusion.97 = f32[8,1024,1024]{2,1,0:T(8,128)} fusion(bf16[6,8,1024,1024]{3,2,1,0:T(8,128)(2,1)} %param.10), kind=kOutput, calls=%fused_computation.163 | convolution fusion | flops 17179869184 | bytes 50331648 | tf_op jit(solution)/shard_map/btd,bsd->bts/dot_general | solution.py:36
  1010.2 192.0 %all-reduce.11.cloned.1.call-done = bf16[8,1024,1024]{2,1,0:T(8,128)(2,1)} async-done(((bf16[8,1024,1024]{2,1,0:T(8,128)(2,1)}), bf16[8,1024,1024]{2,1,0:T(8,128)(2,1)}) %all-reduce.11.cloned.1.call-update) | async-done | bytes 16777232 | tf_op jit(solution)/shard_map/psum | solution.py:35
  1222.4 43.0 %fusion.22 = bf16[8,1024,1024]{2,1,0:T(8,128)(2,1)} fusion(bf16[8,1024,1024]{2,1,0:T(8,128)(2,1)} %fusion.52, bf16[6,8,1024,1024]{3,2,1,0:T(8,128)(2,1)} %param.11, bf16[6,1024,1024]{2,1,0:T(8,128)(2,1)} %param.13), kind=kOutput, calls=%fused_computation.74 | convolution fusion | flops 17347641344 | bytes 52428800 | tf_op jit(solution)/shard_map/btd,fd->btf/dot_general | solution.py:32
  1376.8 195.6 %all-reduce.13.cloned.1.call-done = bf16[8,1024,1024]{2,1,0:T(8,128)(2,1)} async-done(((bf16[8,1024,1024]{2,1,0:T(8,128)(2,1)}), bf16[8,1024,1024]{2,1,0:T(8,128)(2,1)}) %all-reduce.13.cloned.1.call-update) | async-done | bytes 16777232 | tf_op jit(solution)/shard_map/psum | solution.py:35
  1592.5 43.0 %fusion.16 = bf16[8,1024,1024]{2,1,0:T(8,128)(2,1)} fusion(bf16[8,1024,1024]{2,1,0:T(8,128)(2,1)} %fusion.54, bf16[6,8,1024,1024]{3,2,1,0:T(8,128)(2,1)} %param.11, bf16[6,1024,1024]{2,1,0:T(8,128)(2,1)} %param.13), kind=kOutput, calls=%fused_computation.68 | convolution fusion | flops 17347641344 | bytes 52428800 | tf_op jit(solution)/shard_map/btd,fd->btf/dot_general | solution.py:32
  1746.8 195.7 %all-reduce.15.cloned.1.call-done = bf16[8,1024,1024]{2,1,0:T(8,128)(2,1)} async-done(((bf16[8,1024,1024]{2,1,0:T(8,128)(2,1)}), bf16[8,1024,1024]{2,1,0:T(8,128)(2,1)}) %all-reduce.15.cloned.1.call-update) | async-done | bytes 16777232 | tf_op jit(solution)/shard_map/psum | solution.py:35
  1942.5 45.0 %fusion.46 = bf16[8,1024,1024]{2,1,0:T(8,128)(2,1)} fusion(bf16[6,8,1024,1024]{3,2,1,0:T(8,128)(2,1)} %param.11, bf16[6,1024,1024]{2,1,0:T(8,128)(2,1)} %param.13, bf16[8,1024,1024]{2,1,0:T(8,128)(2,1)} %fusion.54, bf16[8,1024,1024]{2,1,0:T(8,128)(2,1)} %all-reduce.15.cloned.1.call-done), kind=kOutput, calls=%fused_computation.98 | convolution fusion | flops 17381195776 | bytes 69206016 | tf_op jit(solution)/shard_map/btd,fd->btf/dot_general | solution.py:32
  2016.3 37.2 %multiply_reduce_fusion.10 = f32[8]{0:T(128)S(1)} fusion(f32[8,1024,1024]{2,1,0:T(8,128)} %fusion.204, bf16[8,1024,1024]{2,1,0:T(8,128)(2,1)} %fusion.54, bf16[8,1024,1024]{2,1,0:T(8,128)(2,1)} %all-reduce.15.cloned.1.call-done), kind=kOutput, calls=%fused_computation.145 | convolution fusion | flops 17230200832 | bytes 67108896 | tf_op jit(solution)/shard_map/btd,bsd->bts/dot_general | solution.py:39
  2214.5 34.0 %fusion.150 = f32[1024,1024]{1,0:T(8,128)} fusion(f32[8]{0:T(128)S(1)} %get-tuple-element.45, bf16[6,8,1024,1024]{3,2,1,0:T(8,128)(2,1)} %param.11, bf16[8,1024,1024]{2,1,0:T(8,128)(2,1)} %fusion.54, bf16[8,1024,1024]{2,1,0:T(8,128)(2,1)} %all-reduce.15.cloned.1.call-done), kind=kOutput, calls=%fused_computation.211 | convolution fusion | flops 17322475520 | bytes 54525984 | tf_op jit(solution)/shard_map/btf,btd->fd/dot_general | solution.py:47
  2248.6 32.0 %fusion.147 = f32[1024,1024]{1,0:T(8,128)} fusion(bf16[8,1024,1024]{2,1,0:T(8,128)(2,1)} %fusion.54, f32[8]{0:T(128)S(1)} %copy-done.6, bf16[6,8,1024,1024]{3,2,1,0:T(8,128)(2,1)} %param.11), kind=kOutput, calls=%fused_computation.210 | convolution fusion | flops 17288921088 | bytes 37748768 | tf_op jit(solution)/shard_map/btf,btd->fd/dot_general | solution.py:47
  2344.3 31.9 %fusion.138 = f32[1024,1024]{1,0:T(8,128)} fusion(bf16[8,1024,1024]{2,1,0:T(8,128)(2,1)} %fusion.48, f32[8]{0:T(128)S(1)} %copy-done.10, bf16[6,8,1024,1024]{3,2,1,0:T(8,128)(2,1)} %param.11), kind=kOutput, calls=%fused_computation.207 | convolution fusion | flops 17288921088 | bytes 37748768 | tf_op jit(solution)/shard_map/btf,btd->fd/dot_general | solution.py:47
  2376.3 31.7 %fusion.135 = f32[1024,1024]{1,0:T(8,128)} fusion(bf16[8,1024,1024]{2,1,0:T(8,128)(2,1)} %param.14, f32[8]{0:T(128)S(1)} %copy-done.8, bf16[6,8,1024,1024]{3,2,1,0:T(8,128)(2,1)} %param.11), kind=kOutput, calls=%fused_computation.206 | convolution fusion | flops 17288921088 | bytes 37748768 | tf_op jit(solution)/shard_map/btf,btd->fd/dot_general | solution.py:47
  2481.1 34.5 %reduce-scatter.27.cloned.1.call-done = f32[1024,512]{1,0:T(8,128)} async-done(((f32[1024,1024]{1,0:T(8,128)}), f32[1024,512]{1,0:T(8,128)}) %reduce-scatter.27.cloned.1.call-update) | async-done | bytes 2097168 | tf_op jit(solution)/shard_map/reduce_scatter | solution.py:49
  2519.6 49.6 %reduce-scatter.29.cloned.1.call-done = f32[1024,512]{1,0:T(8,128)} async-done(((f32[1024,1024]{1,0:T(8,128)}), f32[1024,512]{1,0:T(8,128)}) %reduce-scatter.29.cloned.1.call-update) | async-done | bytes 2097168 | tf_op jit(solution)/shard_map/reduce_scatter | solution.py:49
  2573.3 49.6 %reduce-scatter.31.cloned.1.call-done = f32[1024,512]{1,0:T(8,128)} async-done(((f32[1024,1024]{1,0:T(8,128)}), f32[1024,512]{1,0:T(8,128)}) %reduce-scatter.31.cloned.1.call-update) | async-done | bytes 2097168 | tf_op jit(solution)/shard_map/reduce_scatter | solution.py:49
  2626.9 49.6 %reduce-scatter.33.cloned.1.call-done = f32[1024,512]{1,0:T(8,128)} async-done(((f32[1024,1024]{1,0:T(8,128)}), f32[1024,512]{1,0:T(8,128)}) %reduce-scatter.33.cloned.1.call-update) | async-done | bytes 2097168 | tf_op jit(solution)/shard_map/reduce_scatter | solution.py:49
  2680.6 49.6 %reduce-scatter.35.cloned.1.call-done = f32[1024,512]{1,0:T(8,128)} async-done(((f32[1024,1024]{1,0:T(8,128)}), f32[1024,512]{1,0:T(8,128)}) %reduce-scatter.35.cloned.1.call-update) | async-done | bytes 2097168 | tf_op jit(solution)/shard_map/reduce_scatter | solution.py:49
  (128 shorter events, 834.0 us)
Async XLA Ops:
  7.2 451.9 %all-reduce.7.cloned.1.call-start = ((), (), s32[]{:S(2)}) async-start(), calls=%async_computation.12 | async-start | bytes 33554432 | tf_op jit(solution)/shard_map/psum | solution.py:35
  74.7 757.3 %all-reduce.9.cloned.1.call-start = ((), (), s32[]{:S(2)}) async-start(), calls=%async_computation.13 | async-start | bytes 33554432 | tf_op jit(solution)/shard_map/psum | solution.py:35
  522.2 24.4 copy-start.11
  522.2 24.4 copy-start.12
  522.2 25.0 copy-start
  522.2 25.6 copy-start.1
  546.5 655.6 %all-reduce.11.cloned.1.call-start = ((), (), s32[]{:S(2)}) async-start(), calls=%async_computation.14 | async-start | bytes 33554432 | tf_op jit(solution)/shard_map/psum | solution.py:35
  919.5 652.9 %all-reduce.13.cloned.1.call-start = ((), (), s32[]{:S(2)}) async-start(), calls=%async_computation.15 | async-start | bytes 33554432 | tf_op jit(solution)/shard_map/psum | solution.py:35
  1289.6 652.9 %all-reduce.15.cloned.1.call-start = ((), (), s32[]{:S(2)}) async-start(), calls=%async_computation.16 | async-start | bytes 33554432 | tf_op jit(solution)/shard_map/psum | solution.py:35
  1659.8 781.0 %reduce-scatter.13.cloned.1.call-start = ((), (), s32[]{:S(2)}) async-start(), calls=%async_computation.17 | async-start | bytes 6291456 | tf_op jit(solution)/shard_map/reduce_scatter | solution.py:48
  2016.3 37.3 %copy-start.2 = (f32[8,2]{0,1:T(2,128)S(1)}, f32[8,2]{0,1:T(2,128)}, u32[]{:S(2)}) copy-start(f32[8,2]{0,1:T(2,128)} %pad_maximum_fusion.5) | copy-start | bytes 196
  2016.3 37.3 %copy-start.3 = (f32[8,2]{0,1:T(2,128)S(1)}, f32[8,2]{0,1:T(2,128)}, u32[]{:S(2)}) copy-start(f32[8,2]{0,1:T(2,128)} %pad_maximum_fusion.4) | copy-start | bytes 196
  2016.3 37.3 %copy-start.4 = (f32[8,2]{0,1:T(2,128)S(1)}, f32[8,2]{0,1:T(2,128)}, u32[]{:S(2)}) copy-start(f32[8,2]{0,1:T(2,128)} %pad_maximum_fusion.3) | copy-start | bytes 196
  2016.3 37.3 %copy-start.5 = (f32[8,2]{0,1:T(2,128)S(1)}, f32[8,2]{0,1:T(2,128)}, u32[]{:S(2)}) copy-start(f32[8,2]{0,1:T(2,128)} %pad_maximum_fusion.2) | copy-start | bytes 196
  2086.6 358.2 %reduce-scatter.15.cloned.1.call-start = ((), (), s32[]{:S(2)}) async-start(), calls=%async_computation.18 | async-start | bytes 6291456 | tf_op jit(solution)/shard_map/reduce_scatter | solution.py:48
  2111.2 337.6 %reduce-scatter.17.cloned.1.call-start = ((), (), s32[]{:S(2)}) async-start(), calls=%async_computation.19 | async-start | bytes 6291456 | tf_op jit(solution)/shard_map/reduce_scatter | solution.py:48
  2138.4 314.5 %reduce-scatter.19.cloned.1.call-start = ((), (), s32[]{:S(2)}) async-start(), calls=%async_computation.20 | async-start | bytes 6291456 | tf_op jit(solution)/shard_map/reduce_scatter | solution.py:48
  2162.9 294.0 %reduce-scatter.21.cloned.1.call-start = ((), (), s32[]{:S(2)}) async-start(), calls=%async_computation.21 | async-start | bytes 6291456 | tf_op jit(solution)/shard_map/reduce_scatter | solution.py:48
  2190.1 270.9 %reduce-scatter.23.cloned.1.call-start = ((), (), s32[]{:S(2)}) async-start(), calls=%async_computation.22 | async-start | bytes 6291456 | tf_op jit(solution)/shard_map/reduce_scatter | solution.py:48
  2214.5 262.6 %reduce-scatter.25.cloned.1.call-start = ((), (), s32[]{:S(2)}) async-start(), calls=%async_computation.23 | async-start | bytes 6291456 | tf_op jit(solution)/shard_map/reduce_scatter | solution.py:49
  2214.5 34.1 %copy-start.6 = (f32[8]{0:T(128)S(1)}, f32[8]{0:T(128)}, u32[]{:S(2)}) copy-start(f32[8]{0:T(128)} %get-tuple-element.24) | copy-start | bytes 100
  2248.6 267.0 %reduce-scatter.27.cloned.1.call-start = ((), (), s32[]{:S(2)}) async-start(), calls=%async_computation.24 | async-start | bytes 6291456 | tf_op jit(solution)/shard_map/reduce_scatter | solution.py:49
  2248.6 32.1 %copy-start.9 = (f32[8]{0:T(128)S(1)}, f32[8]{0:T(128)}, u32[]{:S(2)}) copy-start(f32[8]{0:T(128)} %get-tuple-element.43) | copy-start | bytes 100
  2280.6 288.6 %reduce-scatter.29.cloned.1.call-start = ((), (), s32[]{:S(2)}) async-start(), calls=%async_computation.25 | async-start | bytes 6291456 | tf_op jit(solution)/shard_map/reduce_scatter | solution.py:49
  2280.7 31.8 %copy-start.7 = (f32[8]{0:T(128)S(1)}, f32[8]{0:T(128)}, u32[]{:S(2)}) copy-start(f32[8]{0:T(128)} %get-tuple-element.20) | copy-start | bytes 100
  2312.4 310.5 %reduce-scatter.31.cloned.1.call-start = ((), (), s32[]{:S(2)}) async-start(), calls=%async_computation.26 | async-start | bytes 6291456 | tf_op jit(solution)/shard_map/reduce_scatter | solution.py:49
  2312.5 31.8 %copy-start.10 = (f32[8]{0:T(128)S(1)}, f32[8]{0:T(128)}, u32[]{:S(2)}) copy-start(f32[8]{0:T(128)} %get-tuple-element.41) | copy-start | bytes 100
  2344.2 332.3 %reduce-scatter.33.cloned.1.call-start = ((), (), s32[]{:S(2)}) async-start(), calls=%async_computation.27 | async-start | bytes 6291456 | tf_op jit(solution)/shard_map/reduce_scatter | solution.py:49
  2344.3 32.0 %copy-start.8 = (f32[8]{0:T(128)S(1)}, f32[8]{0:T(128)}, u32[]{:S(2)}) copy-start(f32[8]{0:T(128)} %get-tuple-element.16) | copy-start | bytes 100
  2376.2 353.9 %reduce-scatter.35.cloned.1.call-start = ((), (), s32[]{:S(2)}) async-start(), calls=%async_computation.28 | async-start | bytes 6291456 | tf_op jit(solution)/shard_map/reduce_scatter | solution.py:49
Sparse Core Ops, SparseCore 0:
  74.8 285.3 all-reduce.6
  546.6 285.3 all-reduce.8
  919.6 282.5 all-reduce.10
  1289.7 282.5 all-reduce.12
  1659.9 282.5 all-reduce.14
  2086.7 52.0 reduce-scatter.12
  2141.6 51.4 reduce-scatter.14
  2195.4 51.5 reduce-scatter.16
  2249.2 51.4 reduce-scatter.18
  2302.8 51.4 reduce-scatter.20
  2356.6 51.5 reduce-scatter.22
  2410.3 51.4 reduce-scatter.24
  2464.0 51.4 reduce-scatter.26
  2517.7 51.4 reduce-scatter.28
  2571.3 51.5 reduce-scatter.30
  2625.0 51.4 reduce-scatter.32
  2678.6 51.4 reduce-scatter.34
where the time goes:
time: 2750 us; the launch traced here: 2740 us
  matrix products  1520 us (55%)
  waiting for transfers between devices  1020 us (37%)
  other arithmetic  140 us (5%)
  local copies, waits for them, and re-layouts  38.8 us (1%)
    psum x5, waiting for transfers between devices, local_step(): full_x = lax.psum(part_x, 'tp')  784 us
    dot_general x6, matrix products, local_step(): jnp.einsum('btd,fd->btf', grad_z, w_down[layer], preferred_element_type=j...  260 us
    dot_general x6, matrix products, local_step(): jnp.einsum('btf,bsf->bts', hidden, hidden, preferred_element_type=jnp.flo...  247 us
    reduce_scatter x6, waiting for transfers between devices, local_step(): sum_down = lax.psum_scatter(sum_down, 'dp', scatter_dimension=1, tiled=True)  233 us
    dot_general x6, matrix products, local_step(): jnp.einsum('btd,bsd->bts', x_layer, x_layer, preferred_element_type=jnp.f...  194 us
    dot_general x6, matrix products, local_step(): jnp.einsum('btf,btd->fd', hidden, dz_clip, preferred_element_type=jnp.flo...  193 us
    dot_general x6, matrix products, local_step(): jnp.einsum('btd,bsd->bts', grad_z, grad_z, preferred_element_type=jnp.flo...  182 us
    dot_general x6, matrix products, local_step(): jnp.einsum('btf,bsf->bts', grad_h, grad_h, preferred_element_type=jnp.flo...  173 us
  transfers between devices with their start and end apart: 17, of which 9 were waited for; matrix products, arithmetic and copies ran while one was open for 41% of the time, Pallas kernels for 0%

commit v1 on v0

v1 whole, which is shorter than its diff:
```python
import math
import jax
import jax.numpy as jnp
from jax import lax
from jax.experimental import pallas as pl
from jax.experimental.pallas import tpu as pltpu
from jax.sharding import PartitionSpec as P


GELU_SCALE = math.sqrt(2.0 / math.pi)

T = 1024
D = 1024
Q = 1024
E = 4
TB = 512
NB = T // TB
KB = 512
GB = 256
F32 = jnp.float32
BF16 = jnp.bfloat16
ANY = pl.BlockSpec(memory_space=pl.ANY)
SMEM = pl.BlockSpec(memory_space=pltpu.SMEM)
TOKEN = jax.ShapeDtypeStruct((8, 128), F32)
TOKEN_SPEC = pl.BlockSpec((8, 128), lambda *_: (0, 0))
NT = (((1,), (1,)), ((), ()))
TN = (((0,), (0,)), ((), ()))
PARAMS = pltpu.CompilerParams(vmem_limit_bytes=63 * 1024 * 1024)


def gelu_pair(u):
    u2 = u * u
    t = jnp.tanh(u * (GELU_SCALE + (GELU_SCALE * 0.044715) * u2))
    half = 0.5 + 0.5 * t
    slope = half + (u * (1.0 - t * t)) * (0.5 * GELU_SCALE + (0.5 * GELU_SCALE * 0.134145) * u2)
    return u * half, slope


def block(i, size):
    return pl.ds(pl.multiple_of(i * size, size), size)


def gram_norms(x_ref, dz_ref, dh_ref, h_ref):
    def gram(ref, rows, cols):
        return lax.dot_general(ref[rows, :], ref[cols, :], NT, preferred_element_type=F32)

    def fold(p):
        return jnp.sum(p.reshape(p.shape[0] // 8, 8, GB), axis=0)

    def ring(k, sums):
        at = jnp.where(k == 3, 0, k)
        w = jnp.where(k == 3, 2.0, 1.0)
        rows, cols = pl.ds(pl.multiple_of(at * GB, GB), 2 * GB), block(k, GB)
        p1 = gram(x_ref, rows, cols) * gram(dh_ref, rows, cols)
        p2 = gram(h_ref, rows, cols) * gram(dz_ref, rows, cols)
        return tuple(t + (w * fold(p[:GB]) + 2.0 * fold(p[GB:])) for t, p in zip(sums, (p1, p2)))

    n1, n2 = lax.fori_loop(0, 4, ring, (jnp.zeros((8, GB), F32), jnp.zeros((8, GB), F32)))
    for r, c, w in ((3, 3, 1.0), (2, 0, 2.0)):
        rows, cols = slice(r * GB, (r + 1) * GB), slice(c * GB, (c + 1) * GB)
        n1 = n1 + w * fold(gram(x_ref, rows, cols) * gram(dh_ref, rows, cols))
        n2 = n2 + w * fold(gram(h_ref, rows, cols) * gram(dz_ref, rows, cols))
    return jnp.sum(n1), jnp.sum(n2)


def store_norms(n_ref, tok_ref, n1, n2):
    n_ref[0] = jnp.full((8, 128), n1, F32)
    n_ref[1] = jnp.full((8, 128), n2, F32)
    tok_ref[...] = jnp.zeros((8, 128), F32)


NORM_SHAPE = jax.ShapeDtypeStruct((E, 2, 8, 128), F32)


def norm_spec(ex):
    return pl.BlockSpec((None, 2, 8, 128), lambda *_: (ex, 0, 0, 0))


def chain_call(layer, ex, first, last, norms, scal, dz_prev, part_own, part_recv, u_all, u_recv, x_all, w_down, w_down_r, w_up, w_up_r, bufs, norm_buf, dep):
    at_u = ex if u_recv.shape[0] == E else (ex - 1 if u_recv.shape[0] > 1 else 0)
    at_w = layer if w_down_r.shape[0] > 1 else 0
    names = ["scal", "dz"]
    args = [scal, dz_prev]
    if not first:
        names += ["po", "pr"]
        args += [part_own, part_recv]
    names += ["uo", "ur", "w2o", "w2r"]
    args += [u_all, u_recv, w_down, w_down_r]
    if norms:
        names.append("x")
        args.append(x_all)
    if not last:
        names += ["w1o", "w1r"]
        args += [w_up, w_up_r]
    names.append("dep")
    args.append(dep)
    out_names = ["dz_out", "dh_out", "h_out", "tok"]
    out_shape = [jax.ShapeDtypeStruct((E, T, D), BF16), jax.ShapeDtypeStruct((E, T, 2 * Q), BF16), jax.ShapeDtypeStruct((E, T, 2 * Q), BF16), TOKEN]
    out_specs = [ANY, ANY, ANY, TOKEN_SPEC]
    aliases = {}
    if bufs is not None:
        for k, b in enumerate(bufs):
            aliases[len(args)] = k
            names.append(f"b{k}")
            args.append(b)
    if norms:
        if norm_buf is not None:
            aliases[len(args)] = len(out_names)
            names.append("bn")
            args.append(norm_buf)
        out_names.append("n_out")
        out_shape.append(NORM_SHAPE)
        out_specs.append(norm_spec(ex))
    if not last:
        out_names.append("part_out")
        out_shape.append(jax.ShapeDtypeStruct((T, D), BF16))
        out_specs.append(ANY)
    scratch = {
        "dzp": pltpu.VMEM((T, D), BF16), "po_s": pltpu.VMEM((T, D), BF16), "pr_s": pltpu.VMEM((T, D), BF16),
        "u_s": pltpu.VMEM((2, T, Q), BF16), "x_s": pltpu.VMEM((T, D), BF16), "w2_s": pltpu.VMEM((2 * Q, D), BF16), "w1_s": pltpu.VMEM((2, D, Q), BF16),
        "dz_s": pltpu.VMEM((T, D), BF16), "dh_s": pltpu.VMEM((T, 2 * Q), BF16), "h_s": pltpu.VMEM((T, 2 * Q), BF16), "part_s": pltpu.VMEM((T, D), BF16),
        "in_sem": pltpu.SemaphoreType.DMA((NB, 5)), "w_sem": pltpu.SemaphoreType.DMA((5,)), "out_sem": pltpu.SemaphoreType.DMA((NB, 4)),
    }

    def body(*refs):
        r = dict(zip(names + out_names + list(scratch), refs))
        here = r["scal"][0] * E + ex
        in_sem, w_sem, out_sem = r["in_sem"], r["w_sem"], r["out_sem"]
        dz_src = r["dz"].at[here] if first else r["dz"].at[ex]

        def inputs(i):
            rows = block(i, TB)
            copies = [pltpu.make_async_copy(dz_src.at[rows], r["dzp"].at[rows], in_sem.at[i, 0])]
            if not first:
                copies += [
                    pltpu.make_async_copy(r["po"].at[rows], r["po_s"].at[rows], in_sem.at[i, 1]),
                    pltpu.make_async_copy(r["pr"].at[rows], r["pr_s"].at[rows], in_sem.at[i, 2]),
                ]
            copies += [
                pltpu.make_async_copy(r["uo"].at[layer, here, rows], r["u_s"].at[0, rows], in_sem.at[i, 3]),
                pltpu.make_async_copy(r["ur"].at[at_u, rows], r["u_s"].at[1, rows], in_sem.at[i, 4]),
            ]
            return copies

        def outputs(i):
            rows = block(i, TB)
            return [
                pltpu.make_async_copy(r["dz_s"].at[rows], r["dz_out"].at[ex, rows], out_sem.at[i, 0]),
                pltpu.make_async_copy(r["dh_s"].at[rows], r["dh_out"].at[ex, rows], out_sem.at[i, 1]),
                pltpu.make_async_copy(r["h_s"].at[rows], r["h_out"].at[ex, rows], out_sem.at[i, 2]),
            ]

        def part_output(i):
            rows = block(i, TB)
            return pltpu.make_async_copy(r["part_s"].at[rows], r["part_out"].at[rows], out_sem.at[i, 3])

        w2 = [
            pltpu.make_async_copy(r["w2o"].at[layer], r["w2_s"].at[pl.ds(0, Q)], w_sem.at[0]),
            pltpu.make_async_copy(r["w2r"].at[at_w], r["w2_s"].at[pl.ds(Q, Q)], w_sem.at[1]),
        ]
        ins = inputs(0)
        for c in ins[:-2] + [w2[0], ins[-2], w2[1], ins[-1]]:
            c.start()
        if not last:
            w1 = [
                pltpu.make_async_copy(r["w1o"].at[layer], r["w1_s"].at[0], w_sem.at[2]),
                pltpu.make_async_copy(r["w1r"].at[at_w], r["w1_s"].at[1], w_sem.at[3]),
            ]
            for c in w1:
                c.start()
        for i in range(1, NB):
            for c in inputs(i):
                c.start()
        if norms:
            x_copy = pltpu.make_async_copy(r["x"].at[layer, here], r["x_s"], w_sem.at[4])
            x_copy.start()
        for c in w2:
            c.wait()

        def rows_step(i, carry):
            rows = block(i, TB)
            for c in inputs(i):
                c.wait()
            if first:
                dz = r["dzp"][rows, :]
            else:
                dz = (r["dzp"][rows, :].astype(F32) + (r["po_s"][rows, :].astype(F32) + r["pr_s"][rows, :].astype(F32))).astype(BF16)
            r["dz_s"][rows, :] = dz
            for c in range(4):
                cols = slice(c * 512, (c + 1) * 512)
                back = lax.dot_general(dz, r["w2_s"][cols, :], NT, preferred_element_type=F32)
                val, slope = gelu_pair(r["u_s"][c // 2, rows, (c % 2) * 512:(c % 2 + 1) * 512].astype(F32))
                r["dh_s"][rows, cols] = (slope * back).astype(BF16)
                r["h_s"][rows, cols] = val.astype(BF16)
            if not last:

                @pl.when(i == 0)
                def _():
                    for c in w1:
                        c.wait()

                for c in range(2):
                    cols = slice(c * 512, (c + 1) * 512)
                    acc = lax.dot_general(r["dh_s"][rows, :Q], r["w1_s"][0, cols, :], NT, preferred_element_type=F32)
                    acc = acc + lax.dot_general(r["dh_s"][rows, Q:], r["w1_s"][1, cols, :], NT, preferred_element_type=F32)
                    r["part_s"][rows, cols] = acc.astype(BF16)
            for c in outputs(i):
                c.start()
            if not last:
                part_output(i).start()
            return carry

        lax.fori_loop(0, NB, rows_step, 0)
        if norms:
            x_copy.wait()
            store_norms(r["n_out"], r["tok"], *gram_norms(r["x_s"], r["dz_s"], r["dh_s"], r["h_s"]))
        else:
            r["tok"][...] = jnp.zeros((8, 128), F32)
        for i in range(NB):
            for c in outputs(i):
                c.wait()
            if not last:
                part_output(i).wait()

    outs = pl.pallas_call(
        body,
        out_shape=out_shape,
        in_specs=[SMEM] + [ANY] * (len(args) - 1),
        out_specs=out_specs,
        scratch_shapes=list(scratch.values()),
        input_output_aliases=aliases,
        compiler_params=PARAMS,
        grid=(1,),
    )(*args)
    named = dict(zip(out_names, outs))
    return outs[:3], named.get("n_out", norm_buf), named.get("part_out"), named["tok"]


def norm_call(layer, ex, scal, x_all, bufs, dep):
    def body(s_ref, x_ref, dz_ref, dh_ref, h_ref, dep_ref, n_ref, tok_ref):
        store_norms(n_ref, tok_ref, *gram_norms(x_ref, dz_ref, dh_ref, h_ref))

    def at(width):
        return pl.BlockSpec((None, T, width), lambda i, s: (ex, 0, 0))

    return pl.pallas_call(
        body,
        out_shape=[NORM_SHAPE, TOKEN],
        grid_spec=pltpu.PrefetchScalarGridSpec(
            num_scalar_prefetch=1, grid=(1,),
            in_specs=[pl.BlockSpec((None, None, T, D), lambda i, s: (layer, s[0] * E + ex, 0, 0)), at(D), at(2 * Q), at(2 * Q), ANY],
            out_specs=[norm_spec(ex), TOKEN_SPEC],
        ),
        compiler_params=PARAMS,
    )(scal, x_all, *bufs, dep)


def weight_call(layer, half, x_all, bufs, norms, norms_recv, clip_up, clip_down, scal, recv, dep):
    dz, dh, hid = bufs
    own = half == 0
    steps = E * T // KB
    per = T // KB

    def body(*refs):
        refs = list(refs)
        s_ref, x_ref, dh_ref, h_ref, dz_ref, no_ref, nr_ref, cu_ref, cd_ref = refs[:9]
        del refs[:9]
        if own:
            recv_ref = refs.pop(0)
        refs.pop(0)
        if own:
            send_ref, keep_ref, tok_ref, acc, recv_s, sem, recv_sem = refs
        else:
            g_ref, tok_ref, acc, sem = refs
        k = pl.program_id(0)
        n = no_ref[...] + nr_ref[...]
        c1 = jnp.minimum(1.0, cu_ref[layer] / jnp.sqrt(n[0, 0:1, 0:1]))
        c2 = jnp.minimum(1.0, cd_ref[layer] / jnp.sqrt(n[1, 0:1, 0:1]))
        y = s_ref[1]
        halves = (1 - y, y) if own else (0, 1)
        if own:
            recv_copy = pltpu.make_async_copy(recv_ref, recv_s, recv_sem)

        def copies(g, at):
            ds = block(halves[at], 512)
            if not own:
                part = (0, ds) if g == 0 else (1, slice(None), ds)
                return [pltpu.make_async_copy(acc.at[part], g_ref.at[part], sem.at[g, at, 0])]
            out = (send_ref, keep_ref)[at]
            if g == 0:
                return [pltpu.make_async_copy(acc.at[0, ds], out.at[0], sem.at[g, at, 0])]
            return [
                pltpu.make_async_copy(acc.at[1, pl.ds(b * 512, 512), ds], out.at[1, :, pl.ds(b * 512, 512)], sem.at[g, at, b])
                for b in range(2)
            ]

        @pl.when(k == 0)
        def _():
            tok_ref[...] = jnp.zeros((8, 128), F32)
            if own:
                recv_copy.start()

        def add(init, final):
            dhc = (dh_ref[...].astype(F32) * c1).astype(BF16)
            if final and own:
                recv_copy.wait()
            started = []
            for at in range(2):
                ds = block(halves[at], 512)
                for g in range(2):
                    if g == 0:
                        part = (0, ds)
                        new = lax.dot_general(x_ref[:, ds], dhc, TN, preferred_element_type=F32)
                    else:
                        part = (1, slice(None), ds)
                        new = lax.dot_general(h_ref[...], (dz_ref[:, ds].astype(F32) * c2).astype(BF16), TN, preferred_element_type=F32)
                    if not init:
                        new = acc[part] + new
                    if final and own:
                        new = new + recv_s[part]
                    acc[part] = new
                    if final:
                        if started:
                            for c in copies(*started[-1]):
                                c.start()
                        started.append((g, at))
            if final:
                for c in copies(*started[-1]):
                    c.start()
                for s in started:
                    for c in copies(*s):
                        c.wait()

        @pl.when(k == 0)
        def _():
            add(True, False)

        @pl.when((k > 0) & (k < steps - 1))
        def _():
            add(False, False)

        @pl.when(k == steps - 1)
        def _():
            add(False, True)

    norm_in = pl.BlockSpec((None, 2, 8, 128), lambda k, s: (k // per, 0, 0, 0))
    in_specs = [
        pl.BlockSpec((None, None, KB, D), lambda k, s: (layer, s[0] * E + k // per, k % per, 0)),
        pl.BlockSpec((None, KB, Q), lambda k, s: (k // per, k % per, half)),
        pl.BlockSpec((None, KB, Q), lambda k, s: (k // per, k % per, half)),
        pl.BlockSpec((None, KB, D), lambda k, s: (k // per, k % per, 0)),
        norm_in, norm_in, SMEM, SMEM,
    ]
    args = [x_all, dh, hid, dz, norms, norms_recv, clip_up, clip_down]
    piece = jax.ShapeDtypeStruct((2, 512, 1024), F32)
    scratch = [pltpu.VMEM((2, 1024, 1024), F32)]
    if own:
        in_specs.append(ANY)
        args.append(recv)
        out_shape, out_specs = [piece, piece, TOKEN], [ANY, ANY, TOKEN_SPEC]
        scratch += [pltpu.VMEM((2, 1024, 1024), F32), pltpu.SemaphoreType.DMA((2, 2, 2)), pltpu.SemaphoreType.DMA]
    else:
        out_shape, out_specs = [jax.ShapeDtypeStruct((2, 1024, 1024), F32), TOKEN], [ANY, TOKEN_SPEC]
        scratch += [pltpu.SemaphoreType.DMA((2, 2, 2))]
    return pl.pallas_call(
        body,
        out_shape=out_shape,
        grid_spec=pltpu.PrefetchScalarGridSpec(
            num_scalar_prefetch=1, grid=(steps,), in_specs=in_specs + [ANY], out_specs=out_specs, scratch_shapes=scratch,
        ),
        compiler_params=PARAMS,
    )(scal, *args, dep)


def pack_call(layer, start, count, scal, u_all, dep, weights=()):
    nw = len(weights)

    def body(*refs):
        ins, outs = refs[1:2 + nw], refs[3 + nw:4 + 2 * nw]
        for a, b in zip(ins, outs):
            b[...] = a[...]
        refs[-1][...] = jnp.zeros((8, 128), F32)

    w_in = pl.BlockSpec((None, 512, 1024), lambda e, i, s: (layer, i, 0))
    w_out = pl.BlockSpec((None, 512, 1024), lambda e, i, s: (0, i, 0))
    return pl.pallas_call(
        body,
        out_shape=[jax.ShapeDtypeStruct((count, T, Q), BF16)] + [jax.ShapeDtypeStruct((1, 1024, 1024), BF16)] * nw + [TOKEN],
        grid_spec=pltpu.PrefetchScalarGridSpec(
            num_scalar_prefetch=1, grid=(count, 2),
            in_specs=[pl.BlockSpec((None, None, 512, Q), lambda e, i, s: (layer, (1 - s[0]) * E + start + e, i, 0))] + [w_in] * nw + [ANY],
            out_specs=[pl.BlockSpec((None, 512, Q), lambda e, i, s: (e, i, 0))] + [w_out] * nw + [TOKEN_SPEC],
        ),
        compiler_params=PARAMS,
    )(scal, u_all, *weights, dep)


def final_call(layer, num_layers, total, keep, y_recv, noise_up, noise_down, clip_up, clip_down, noise_mult, outs, dep):
    def body(*refs):
        k1, k2, y1, y2, n1, n2, cu, cd, sg = refs[:9]
        up, down, tok_ref = refs[-3:]
        up[...] = (k1[...] + y1[...] + (sg[0] * cu[layer]) * n1[...]) / total
        down[...] = (k2[...] + y2[...] + (sg[0] * cd[layer]) * n2[...]) / total
        tok_ref[...] = jnp.zeros((8, 128), F32)

    s1 = pl.BlockSpec((None, 512, 512), lambda j: (0, 0, j))
    s2 = pl.BlockSpec((None, 512, 512), lambda j: (1, 0, j))
    up_spec = pl.BlockSpec((None, 512, 512), lambda j: (layer, 0, j))
    down_spec = pl.BlockSpec((None, 512, 512), lambda j: (layer, j, 0))
    in_specs = [s1, s2, s1, s2, up_spec, down_spec, SMEM, SMEM, SMEM, ANY]
    args = [keep, keep, y_recv, y_recv, noise_up, noise_down, clip_up, clip_down, noise_mult, dep]
    aliases = {}
    if outs is not None:
        in_specs += [ANY, ANY]
        args += list(outs)
        aliases = {10: 0, 11: 1}
    up, down, tok = pl.pallas_call(
        body,
        out_shape=[jax.ShapeDtypeStruct((num_layers, 512, 1024), F32), jax.ShapeDtypeStruct((num_layers, 1024, 512), F32), TOKEN],
        grid=(2,),
        in_specs=in_specs,
        out_specs=[up_spec, down_spec, TOKEN_SPEC],
        input_output_aliases=aliases,
        compiler_params=PARAMS,
    )(*args)
    return (up, down), tok


def program_order(num_layers):
    top = num_layers - 1
    order = [("k", "pack", top, 0), ("p", "u", top, 0), ("p", "w", top, 0), ("p", "w", top, 1)]
    order += [("k", "pack", top, 1), ("p", "u", top, 1), ("p", "w", 0, 0), ("p", "w", 0, 1)]

    def chain(layer, e):
        steps = [("k", "chain", layer, e)]
        if e == E - 1:
            steps.append(("p", "n", layer, 0))
        if layer > 0:
            steps.append(("p", "x", layer, e))
        if layer == top and e == 0:
            steps.append(("k", "norm", layer, e))
        return steps

    def give(layer):
        return [("k", "wgrad", layer, 1), ("p", "c", layer, 0)]

    def own(layer):
        return [("k", "wgrad", layer, 0), ("p", "y", layer, 0)]

    for layer in reversed(range(num_layers)):
        order += chain(layer, 0)
        if layer > 0:
            order += [("k", "pack", layer - 1, E), ("p", "u", layer - 1, E)]
        order += chain(layer, 1)
        if layer + 2 <= top:
            order.append(("k", "final", layer + 2, 0))
        order += chain(layer, 2)
        if layer + 1 <= top:
            order += give(layer + 1)
        if layer > 0:
            order += chain(layer, 3)
            if layer + 1 <= top:
                order += own(layer + 1)
        else:
            order += own(1) + chain(0, 3)
    order += give(0) + own(0)
    order += [("k", "final", 1, 0), ("k", "final", 0, 0)]
    return order


def solution(mesh):
    in_specs = (P(None, "dp", None, None), P(None, "dp", None, "tp"), P(None, None, "tp"), P(None, "tp", None), P("dp", None, None), P(None, "dp", "tp"), P(None, "tp", "dp"), P(), P(), P())
    out_specs = (P(None, "dp", "tp"), P(None, "tp", "dp"))
    swap_core = [(0, 1), (1, 0), (2, 3), (3, 2)]
    swap_x = [(0, 2), (2, 0), (1, 3), (3, 1)]
    swap_dp = [(0, 1), (1, 0)]
    num_layers = 6

    def local_step(x_stored, u_stored, w_up, w_down, d_out, noise_up, noise_down, clip_up, clip_down, noise_mult):
        total = float(d_out.shape[0] * mesh.shape["dp"])
        top = num_layers - 1
        scal = jnp.stack([lax.axis_index("tp") % 2, lax.axis_index("dp")]).astype(jnp.int32)
        tok = jnp.zeros((8, 128), F32)
        bufs, norms, part, part_recv, packed, u_recv, w_pack, w_recv = {}, {}, {}, {}, {}, {}, {}, {}
        norms_recv, give, recv, y_send, keep, y_recv = {}, {}, {}, {}, {}, {}
        outs = None
        for step in program_order(num_layers):
            kind, what, layer, k = step
            first, last = layer == top, layer == 0
            if kind == "p":
                if what == "u":
                    u_recv[layer, k] = lax.ppermute(packed[layer, k], "tp", swap_core)
                elif what == "w":
                    w_recv[layer, k] = lax.ppermute(w_pack[k] if first else (w_down, w_up)[k], "tp", swap_core)
                elif what == "n":
                    norms_recv[layer] = lax.ppermute(norms[layer], "tp", swap_x)
                elif what == "x":
                    part_recv[layer, k] = lax.ppermute(part[layer, k], "tp", swap_x)
                elif what == "c":
                    recv[layer] = lax.ppermute(give[layer], "tp", swap_core)
                else:
                    y_recv[layer] = lax.ppermute(y_send[layer], "dp", swap_dp)
            elif what == "pack":
                if first and k == 0:
                    packed[layer, k], w_pack[0], w_pack[1], tok = pack_call(layer, 0, 1, scal, u_stored, tok, (w_down, w_up))
                elif first:
                    packed[layer, k], tok = pack_call(layer, 1, E - 1, scal, u_stored, tok)
                else:
                    packed[layer, k], tok = pack_call(layer, 0, E, scal, u_stored, tok)
            elif what == "chain":
                w_at = top if first else 0
                bufs[layer], norms[layer], part[layer, k], tok = chain_call(
                    layer, k, first, last, not (first and k == 0), scal,
                    d_out if first else bufs[layer + 1][0], None if first else part[layer + 1, k], None if first else part_recv[layer + 1, k],
                    u_stored, u_recv[layer, min(k, 1) if first else E], x_stored,
                    w_down, w_recv[w_at, 0], w_up, w_recv[w_at, 1], bufs.get(layer), norms.get(layer), tok,
                )
            elif what == "norm":
                norms[layer], tok = norm_call(layer, k, scal, x_stored, bufs[layer], tok)
            elif what == "wgrad":
                got = weight_call(
                    layer, k, x_stored, bufs[layer], norms[layer], norms_recv[layer], clip_up, clip_down, scal, recv.get(layer), tok
                )
                tok = got[-1]
                if k == 1:
                    give[layer] = got[0]
                else:
                    y_send[layer], keep[layer] = got[:2]
            else:
                outs, tok = final_call(
                    layer, num_layers, total, keep[layer], y_recv[layer], noise_up, noise_down, clip_up, clip_down, noise_mult, outs, tok
                )
        return outs

    return jax.shard_map(local_step, mesh=mesh, in_specs=in_specs, out_specs=out_specs, check_vma=False)
```

time: 2750 us -> 1800 us (0.65)
  matrix products: 1520 us -> 0 us
  Pallas kernels: 0 us -> 1080 us
  waiting for transfers between devices: 1020 us -> 673 us
  other arithmetic: 140 us -> 0.55 us
  local copies, waits for them, and re-layouts: 38.8 us -> 1.2 us
  starting transfers between devices: 0.71 us -> 34.9 us
    dot_general x47 -> x0, matrix products: 1520 us -> none  [the longest x6 260 us: local_step(): jnp.einsum('btd,fd->btf', grad_z, w_down[layer], preferred_element_type=j...]
    pallas_call x0 -> x50, Pallas kernels: none -> 1080 us  [the longest x24 643 us: chain_call(): pl.pallas_call(body, out_shape=out_shape, in_specs=[SMEM] + [ANY] * (len(...]
    psum x5 -> x0, waiting for transfers between devices: 784 us -> none  [local_step(): full_x = lax.psum(part_x, 'tp')]
    ppermute x0 -> x49, waiting for transfers between devices: none -> 673 us  [the longest x20 460 us: local_step(): part_recv[layer, k] = lax.ppermute(part[layer, k], 'tp', swap_x)]
    reduce_scatter x12 -> x0, waiting for transfers between devices: 233 us -> none  [the longest x6 233 us: local_step(): sum_down = lax.psum_scatter(sum_down, 'dp', scatter_dimension=1, tiled=True)]
    convert_element_type x4 -> x0, other arithmetic: 80.7 us -> none  [local_step(): (grad_z.astype(jnp.float32) + full_x.astype(jnp.float32)).astype(jnp.bflo...]
    unnamed x10 -> x0, other arithmetic: 40.5 us -> none
    ppermute x0 -> x49, starting transfers between devices: none -> 34.9 us  [the longest x20 18.2 us: local_step(): part_recv[layer, k] = lax.ppermute(part[layer, k], 'tp', swap_x)]
  transfers between devices with their start and end apart: 17 -> 49, of which waited for: 9 -> 26; matrix products, arithmetic and copies ran while one was open for 41% -> 0% of each run, Pallas kernels for 0% -> 50%
where the time goes in v1:
time: 1800 us; the launch traced here: 1790 us
  Pallas kernels  1080 us (60%)
  waiting for transfers between devices  673 us (37%)
  starting transfers between devices  34.9 us (2%)
    pallas_call x24, Pallas kernels, chain_call(): pl.pallas_call(body, out_shape=out_shape, in_specs=[SMEM] + [ANY] * (len(...  643 us
    ppermute x20, waiting for transfers between devices, local_step(): part_recv[layer, k] = lax.ppermute(part[layer, k], 'tp', swap_x)  460 us
    pallas_call x12, Pallas kernels, weight_call(): pl.pallas_call(body, out_shape=out_shape, grid_spec=pltpu.PrefetchScalarG...  318 us
    ppermute x6, waiting for transfers between devices, local_step(): y_recv[layer] = lax.ppermute(y_send[layer], 'dp', swap_dp)  134 us
    pallas_call x7, Pallas kernels, pack_call(): pl.pallas_call(body, out_shape=[jax.ShapeDtypeStruct((count, T, Q), BF16)...  61.4 us
    pallas_call x6, Pallas kernels, final_call(): pl.pallas_call(body, out_shape=[jax.ShapeDtypeStruct((num_layers, 512, 10...  41.9 us
  transfers between devices with their start and end apart: 49, of which 26 were waited for; matrix products, arithmetic and copies ran while one was open for 0% of the time, Pallas kernels for 50%

profile of v1, /device:TPU:0, one launch (start us, length us, event | category | flops | bytes accessed | tf_op | source)
XLA Modules:
  0.0 1791.5 jit_solution(3467146448955139617)
XLA Ops:
  113.4 27.3 %shard_map.118 = (bf16[4,1024,1024]{2,1,0:T(8,128)(2,1)}, bf16[4,1024,2048]{2,1,0:T(8,128)(2,1)}, bf16[4,1024,2048]{2,1,0:T(8,128)(2,1)}, f32[8,128]{1,0:T(8,128...) custom-call(s32[2]{0:T(128)} %pad_add_fusion.refs_0_.s_ref, ...), custom_call_target="tpu_custom_call", output_to_operand_aliasing={{0}: (10, {}), {1}: (11, {}), {2}: (12, {}), {4}: (13, {})} | custom-call | tf_op jit(solution)/shard_map/pallas_call | solution.py:225
  143.5 26.7 %shard_map.119 = (bf16[4,1024,1024]{2,1,0:T(8,128)(2,1)}, bf16[4,1024,2048]{2,1,0:T(8,128)(2,1)}, bf16[4,1024,2048]{2,1,0:T(8,128)(2,1)}, f32[8,128]{1,0:T(8,128...) custom-call(s32[2]{0:T(128)} %pad_add_fusion.refs_0_.s_ref, ...), custom_call_target="tpu_custom_call", output_to_operand_aliasing={{0}: (10, {}), {1}: (11, {}), {2}: (12, {}), {4}: (13, {})} | custom-call | tf_op jit(solution)/shard_map/pallas_call | solution.py:225
  170.2 26.7 %shard_map.120 = (bf16[4,1024,1024]{2,1,0:T(8,128)(2,1)}, bf16[4,1024,2048]{2,1,0:T(8,128)(2,1)}, bf16[4,1024,2048]{2,1,0:T(8,128)(2,1)}, f32[8,128]{1,0:T(8,128...) custom-call(s32[2]{0:T(128)} %pad_add_fusion.refs_0_.s_ref, ...), custom_call_target="tpu_custom_call", output_to_operand_aliasing={{0}: (10, {}), {1}: (11, {}), {2}: (12, {}), {4}: (13, {})} | custom-call | tf_op jit(solution)/shard_map/pallas_call | solution.py:225
  198.9 28.0 %shard_map.121 = (bf16[4,1024,1024]{2,1,0:T(8,128)(2,1)}, bf16[4,1024,2048]{2,1,0:T(8,128)(2,1)}, bf16[4,1024,2048]{2,1,0:T(8,128)(2,1)}, f32[8,128]{1,0:T(8,128...) custom-call(s32[2]{0:T(128)} %pad_add_fusion.refs_0_.s_ref, ...), custom_call_target="tpu_custom_call" | custom-call | tf_op jit(solution)/shard_map/pallas_call | solution.py:225
  236.6 28.2 %shard_map.123 = (bf16[4,1024,1024]{2,1,0:T(8,128)(2,1)}, bf16[4,1024,2048]{2,1,0:T(8,128)(2,1)}, bf16[4,1024,2048]{2,1,0:T(8,128)(2,1)}, f32[8,128]{1,0:T(8,128...) custom-call(s32[2]{0:T(128)} %pad_add_fusion.refs_0_.s_ref, ...), custom_call_target="tpu_custom_call", output_to_operand_aliasing={{0}: (12, {}), {1}: (13, {}), {2}: (14, {}), {4}: (15, {})} | custom-call | tf_op jit(solution)/shard_map/pallas_call | solution.py:225
  264.9 28.0 %shard_map.124 = (bf16[4,1024,1024]{2,1,0:T(8,128)(2,1)}, bf16[4,1024,2048]{2,1,0:T(8,128)(2,1)}, bf16[4,1024,2048]{2,1,0:T(8,128)(2,1)}, f32[8,128]{1,0:T(8,128...) custom-call(s32[2]{0:T(128)} %pad_add_fusion.refs_0_.s_ref, ...), custom_call_target="tpu_custom_call", output_to_operand_aliasing={{0}: (12, {}), {1}: (13, {}), {2}: (14, {}), {4}: (15, {})} | custom-call | tf_op jit(solution)/shard_map/pallas_call | solution.py:225
  319.7 47.8 %collective-permute-done.4.refs_3_ = bf16[1024,1024]{1,0:T(8,128)(2,1)} collective-permute-done((bf16[1024,1024]{1,0:T(8,128)(2,1)}, bf16[1024,1024]{1,0:T(8,128)(2,1)}, u32[]{:S(2)}, u32[]{:S(2)}) %collective-permute-start.4) | collective-permute-done | bytes 2097184 | tf_op jit(solution)/shard_map/ppermute | solution.py:498
  367.6 28.0 %shard_map.126 = (bf16[4,1024,1024]{2,1,0:T(8,128)(2,1)}, bf16[4,1024,2048]{2,1,0:T(8,128)(2,1)}, bf16[4,1024,2048]{2,1,0:T(8,128)(2,1)}, f32[8,128]{1,0:T(8,128...) custom-call(s32[2]{0:T(128)} %pad_add_fusion.refs_0_.s_ref, ...), custom_call_target="tpu_custom_call", output_to_operand_aliasing={{0}: (12, {}), {1}: (13, {}), {2}: (14, {}), {4}: (15, {})} | custom-call | tf_op jit(solution)/shard_map/pallas_call | solution.py:225
  395.6 26.8 %shard_map.127 = (f32[2,512,1024]{2,1,0:T(8,128)}, f32[2,512,1024]{2,1,0:T(8,128)}, f32[8,128]{1,0:T(8,128)}) custom-call(s32[2]{0:T(128)} %pad_add_fusion.refs_0_.s_ref, bf16[6,8,1024,1024]{3,2,1,0:T(8,128)(2,1)} %refs_1_.45, bf16[4,1024,2048]{2,1,0:T(8,128)(2,1)} %get-tuple-element.232.refs_2_, bf16[4,1024,2048]{2,1,0:T(8,128)(2,1)} %get-tuple-element.233.refs_3_, ...), custom_call_target="tpu_custom_call" | custom-call | tf_op jit(solution)/shard_map/pallas_call | solution.py:365
  426.6 46.2 %collective-permute-done.19.refs_3_ = bf16[1024,1024]{1,0:T(8,128)(2,1)} collective-permute-done((bf16[1024,1024]{1,0:T(8,128)(2,1)}, bf16[1024,1024]{1,0:T(8,128)(2,1)}, u32[]{:S(2)}, u32[]{:S(2)}) %collective-permute-start.19) | collective-permute-done | bytes 2097184 | tf_op jit(solution)/shard_map/ppermute | solution.py:498
  474.1 28.0 %shard_map.128 = (bf16[4,1024,1024]{2,1,0:T(8,128)(2,1)}, bf16[4,1024,2048]{2,1,0:T(8,128)(2,1)}, bf16[4,1024,2048]{2,1,0:T(8,128)(2,1)}, f32[8,128]{1,0:T(8,128...) custom-call(s32[2]{0:T(128)} %pad_add_fusion.refs_0_.s_ref, ...), custom_call_target="tpu_custom_call" | custom-call | tf_op jit(solution)/shard_map/pallas_call | solution.py:225
  517.8 28.0 %shard_map.130 = (bf16[4,1024,1024]{2,1,0:T(8,128)(2,1)}, bf16[4,1024,2048]{2,1,0:T(8,128)(2,1)}, bf16[4,1024,2048]{2,1,0:T(8,128)(2,1)}, f32[8,128]{1,0:T(8,128...) custom-call(s32[2]{0:T(128)} %pad_add_fusion.refs_0_.s_ref, ...), custom_call_target="tpu_custom_call", output_to_operand_aliasing={{0}: (12, {}), {1}: (13, {}), {2}: (14, {}), {4}: (15, {})} | custom-call | tf_op jit(solution)/shard_map/pallas_call | solution.py:225
  561.1 28.0 %shard_map.132 = (bf16[4,1024,1024]{2,1,0:T(8,128)(2,1)}, bf16[4,1024,2048]{2,1,0:T(8,128)(2,1)}, bf16[4,1024,2048]{2,1,0:T(8,128)(2,1)}, f32[8,128]{1,0:T(8,128...) custom-call(s32[2]{0:T(128)} %pad_add_fusion.refs_0_.s_ref, ...), custom_call_target="tpu_custom_call", output_to_operand_aliasing={{0}: (12, {}), {1}: (13, {}), {2}: (14, {}), {4}: (15, {})} | custom-call | tf_op jit(solution)/shard_map/pallas_call | solution.py:225
  616.8 47.3 %collective-permute-done.12.refs_3_ = bf16[1024,1024]{1,0:T(8,128)(2,1)} collective-permute-done((bf16[1024,1024]{1,0:T(8,128)(2,1)}, bf16[1024,1024]{1,0:T(8,128)(2,1)}, u32[]{:S(2)}, u32[]{:S(2)}) %collective-permute-start.12) | collective-permute-done | bytes 2097184 | tf_op jit(solution)/shard_map/ppermute | solution.py:498
  664.1 27.9 %shard_map.134 = (bf16[4,1024,1024]{2,1,0:T(8,128)(2,1)}, bf16[4,1024,2048]{2,1,0:T(8,128)(2,1)}, bf16[4,1024,2048]{2,1,0:T(8,128)(2,1)}, f32[8,128]{1,0:T(8,128...) custom-call(s32[2]{0:T(128)} %pad_add_fusion.refs_0_.s_ref, ...), custom_call_target="tpu_custom_call", output_to_operand_aliasing={{0}: (12, {}), {1}: (13, {}), {2}: (14, {}), {4}: (15, {})} | custom-call | tf_op jit(solution)/shard_map/pallas_call | solution.py:225
  692.1 26.7 %shard_map.135 = (f32[2,512,1024]{2,1,0:T(8,128)}, f32[2,512,1024]{2,1,0:T(8,128)}, f32[8,128]{1,0:T(8,128)}) custom-call(s32[2]{0:T(128)} %pad_add_fusion.refs_0_.s_ref, bf16[6,8,1024,1024]{3,2,1,0:T(8,128)(2,1)} %refs_1_.45, bf16[4,1024,2048]{2,1,0:T(8,128)(2,1)} %get-tuple-element.259.refs_2_, bf16[4,1024,2048]{2,1,0:T(8,128)(2,1)} %get-tuple-element.260.refs_3_, ...), custom_call_target="tpu_custom_call" | custom-call | tf_op jit(solution)/shard_map/pallas_call | solution.py:365
  721.9 46.3 %collective-permute-done.27.refs_3_ = bf16[1024,1024]{1,0:T(8,128)(2,1)} collective-permute-done((bf16[1024,1024]{1,0:T(8,128)(2,1)}, bf16[1024,1024]{1,0:T(8,128)(2,1)}, u32[]{:S(2)}, u32[]{:S(2)}) %collective-permute-start.27) | collective-permute-done | bytes 2097184 | tf_op jit(solution)/shard_map/ppermute | solution.py:498
  768.7 28.0 %shard_map.136 = (bf16[4,1024,1024]{2,1,0:T(8,128)(2,1)}, bf16[4,1024,2048]{2,1,0:T(8,128)(2,1)}, bf16[4,1024,2048]{2,1,0:T(8,128)(2,1)}, f32[8,128]{1,0:T(8,128...) custom-call(s32[2]{0:T(128)} %pad_add_fusion.refs_0_.s_ref, ...), custom_call_target="tpu_custom_call" | custom-call | tf_op jit(solution)/shard_map/pallas_call | solution.py:225
  813.1 28.2 %shard_map.138 = (bf16[4,1024,1024]{2,1,0:T(8,128)(2,1)}, bf16[4,1024,2048]{2,1,0:T(8,128)(2,1)}, bf16[4,1024,2048]{2,1,0:T(8,128)(2,1)}, f32[8,128]{1,0:T(8,128...) custom-call(s32[2]{0:T(128)} %pad_add_fusion.refs_0_.s_ref, ...), custom_call_target="tpu_custom_call", output_to_operand_aliasing={{0}: (12, {}), {1}: (13, {}), {2}: (14, {}), {4}: (15, {})} | custom-call | tf_op jit(solution)/shard_map/pallas_call | solution.py:225
  856.3 27.9 %shard_map.140 = (bf16[4,1024,1024]{2,1,0:T(8,128)(2,1)}, bf16[4,1024,2048]{2,1,0:T(8,128)(2,1)}, bf16[4,1024,2048]{2,1,0:T(8,128)(2,1)}, f32[8,128]{1,0:T(8,128...) custom-call(s32[2]{0:T(128)} %pad_add_fusion.refs_0_.s_ref, ...), custom_call_target="tpu_custom_call", output_to_operand_aliasing={{0}: (12, {}), {1}: (13, {}), {2}: (14, {}), {4}: (15, {})} | custom-call | tf_op jit(solution)/shard_map/pallas_call | solution.py:225
  911.6 47.4 %collective-permute-done.20.refs_3_ = bf16[1024,1024]{1,0:T(8,128)(2,1)} collective-permute-done((bf16[1024,1024]{1,0:T(8,128)(2,1)}, bf16[1024,1024]{1,0:T(8,128)(2,1)}, u32[]{:S(2)}, u32[]{:S(2)}) %collective-permute-start.20) | collective-permute-done | bytes 2097184 | tf_op jit(solution)/shard_map/ppermute | solution.py:498
  959.0 28.0 %shard_map.142 = (bf16[4,1024,1024]{2,1,0:T(8,128)(2,1)}, bf16[4,1024,2048]{2,1,0:T(8,128)(2,1)}, bf16[4,1024,2048]{2,1,0:T(8,128)(2,1)}, f32[8,128]{1,0:T(8,128...) custom-call(s32[2]{0:T(128)} %pad_add_fusion.refs_0_.s_ref, ...), custom_call_target="tpu_custom_call", output_to_operand_aliasing={{0}: (12, {}), {1}: (13, {}), {2}: (14, {}), {4}: (15, {})} | custom-call | tf_op jit(solution)/shard_map/pallas_call | solution.py:225
  987.1 27.0 %shard_map.143 = (f32[2,512,1024]{2,1,0:T(8,128)}, f32[2,512,1024]{2,1,0:T(8,128)}, f32[8,128]{1,0:T(8,128)}) custom-call(s32[2]{0:T(128)} %pad_add_fusion.refs_0_.s_ref, bf16[6,8,1024,1024]{3,2,1,0:T(8,128)(2,1)} %refs_1_.45, bf16[4,1024,2048]{2,1,0:T(8,128)(2,1)} %get-tuple-element.291.refs_2_, bf16[4,1024,2048]{2,1,0:T(8,128)(2,1)} %get-tuple-element.292.refs_3_, ...), custom_call_target="tpu_custom_call" | custom-call | tf_op jit(solution)/shard_map/pallas_call | solution.py:365
  1018.2 46.2 %collective-permute-done.35.refs_3_ = bf16[1024,1024]{1,0:T(8,128)(2,1)} collective-permute-done((bf16[1024,1024]{1,0:T(8,128)(2,1)}, bf16[1024,1024]{1,0:T(8,128)(2,1)}, u32[]{:S(2)}, u32[]{:S(2)}) %collective-permute-start.35) | collective-permute-done | bytes 2097184 | tf_op jit(solution)/shard_map/ppermute | solution.py:498
  1065.0 28.0 %shard_map.144 = (bf16[4,1024,1024]{2,1,0:T(8,128)(2,1)}, bf16[4,1024,2048]{2,1,0:T(8,128)(2,1)}, bf16[4,1024,2048]{2,1,0:T(8,128)(2,1)}, f32[8,128]{1,0:T(8,128...) custom-call(s32[2]{0:T(128)} %pad_add_fusion.refs_0_.s_ref, ...), custom_call_target="tpu_custom_call" | custom-call | tf_op jit(solution)/shard_map/pallas_call | solution.py:225
  1109.4 28.0 %shard_map.146 = (bf16[4,1024,1024]{2,1,0:T(8,128)(2,1)}, bf16[4,1024,2048]{2,1,0:T(8,128)(2,1)}, bf16[4,1024,2048]{2,1,0:T(8,128)(2,1)}, f32[8,128]{1,0:T(8,128...) custom-call(s32[2]{0:T(128)} %pad_add_fusion.refs_0_.s_ref, ...), custom_call_target="tpu_custom_call", output_to_operand_aliasing={{0}: (12, {}), {1}: (13, {}), {2}: (14, {}), {4}: (15, {})} | custom-call | tf_op jit(solution)/shard_map/pallas_call | solution.py:225
  1152.6 28.0 %shard_map.148 = (bf16[4,1024,1024]{2,1,0:T(8,128)(2,1)}, bf16[4,1024,2048]{2,1,0:T(8,128)(2,1)}, bf16[4,1024,2048]{2,1,0:T(8,128)(2,1)}, f32[8,128]{1,0:T(8,128...) custom-call(s32[2]{0:T(128)} %pad_add_fusion.refs_0_.s_ref, ...), custom_call_target="tpu_custom_call", output_to_operand_aliasing={{0}: (12, {}), {1}: (13, {}), {2}: (14, {}), {4}: (15, {})} | custom-call | tf_op jit(solution)/shard_map/pallas_call | solution.py:225
  1208.3 47.3 %collective-permute-done.28.refs_3_ = bf16[1024,1024]{1,0:T(8,128)(2,1)} collective-permute-done((bf16[1024,1024]{1,0:T(8,128)(2,1)}, bf16[1024,1024]{1,0:T(8,128)(2,1)}, u32[]{:S(2)}, u32[]{:S(2)}) %collective-permute-start.28) | collective-permute-done | bytes 2097184 | tf_op jit(solution)/shard_map/ppermute | solution.py:498
  1255.7 28.0 %shard_map.150 = (bf16[4,1024,1024]{2,1,0:T(8,128)(2,1)}, bf16[4,1024,2048]{2,1,0:T(8,128)(2,1)}, bf16[4,1024,2048]{2,1,0:T(8,128)(2,1)}, f32[8,128]{1,0:T(8,128...) custom-call(s32[2]{0:T(128)} %pad_add_fusion.refs_0_.s_ref, ...), custom_call_target="tpu_custom_call", output_to_operand_aliasing={{0}: (12, {}), {1}: (13, {}), {2}: (14, {}), {4}: (15, {})} | custom-call | tf_op jit(solution)/shard_map/pallas_call | solution.py:225
  1313.3 46.3 %collective-permute-done.43.refs_3_ = bf16[1024,1024]{1,0:T(8,128)(2,1)} collective-permute-done((bf16[1024,1024]{1,0:T(8,128)(2,1)}, bf16[1024,1024]{1,0:T(8,128)(2,1)}, u32[]{:S(2)}, u32[]{:S(2)}) %collective-permute-start.43) | collective-permute-done | bytes 2097184 | tf_op jit(solution)/shard_map/ppermute | solution.py:498
  1642.9 52.1 %collective-permute-done.48.refs_2_.refs_3_ = f32[2,512,1024]{2,1,0:T(8,128)} collective-permute-done((f32[2,512,1024]{2,1,0:T(8,128)}, f32[2,512,1024]{2,1,0:T(8,128)}, u32[]{:S(2)}, u32[]{:S(2)}) %collective-permute-start.48) | collective-permute-done | bytes 4194336 | tf_op jit(solution)/shard_map/ppermute | solution.py:502
  1701.9 82.4 %collective-permute-done.47.refs_2_.refs_3_ = f32[2,512,1024]{2,1,0:T(8,128)} collective-permute-done((f32[2,512,1024]{2,1,0:T(8,128)}, f32[2,512,1024]{2,1,0:T(8,128)}, u32[]{:S(2)}, u32[]{:S(2)}) %collective-permute-start.47) | collective-permute-done | bytes 4194336 | tf_op jit(solution)/shard_map/ppermute | solution.py:502
  (120 shorter events, 670.8 us)
Async XLA Ops:
  0.6 198.3 %collective-permute-start.6 = (bf16[6,1024,1024]{2,1,0:T(8,128)(2,1)}, bf16[6,1024,1024]{2,1,0:T(8,128)(2,1)}, u32[]{:S(2)}, u32[]{:S(2)}) collective-permute-start(bf16[6,1024,1024]{2,1,0:T(8,128)(2,1)} %refs_6_.57), channel_id=1, source_target_pairs={{0,1},{1,0},{2,3},{3,2},{4,5},{5,4},{6,7},{7,6}} | collective-permute-start | bytes 37748744 | tf_op jit(solution)/shard_map/ppermute | solution.py:494
  1.5 197.5 %collective-permute-start.7 = (bf16[6,1024,1024]{2,1,0:T(8,128)(2,1)}, bf16[6,1024,1024]{2,1,0:T(8,128)(2,1)}, u32[]{:S(2)}, u32[]{:S(2)}) collective-permute-start(bf16[6,1024,1024]{2,1,0:T(8,128)(2,1)} %refs_9_.31), channel_id=1, source_target_pairs={{0,1},{1,0},{2,3},{3,2},{4,5},{5,4},{6,7},{7,6}} | collective-permute-start | bytes 37748744 | tf_op jit(solution)/shard_map/ppermute | solution.py:494
  90.9 106.0 %collective-permute-start.5 = (bf16[4,1024,1024]{2,1,0:T(8,128)(2,1)}, bf16[4,1024,1024]{2,1,0:T(8,128)(2,1)}, u32[]{:S(2)}, u32[]{:S(2)}) collective-permute-start(bf16[4,1024,1024]{2,1,0:T(8,128)(2,1)} %get-tuple-element.231), channel_id=1, source_target_pairs={{0,1},{1,0},{2,3},{3,2},{4,5},{5,4},{6,7},{7,6}} | collective-permute-start | bytes 25165832 | tf_op jit(solution)/shard_map/ppermute | solution.py:492
  91.4 78.8 %collective-permute-start.11 = (bf16[1024,1024]{1,0:T(8,128)(2,1)}, bf16[1024,1024]{1,0:T(8,128)(2,1)}, u32[]{:S(2)}, u32[]{:S(2)}) collective-permute-start(bf16[1024,1024]{1,0:T(8,128)(2,1)} %get-tuple-element.237.refs_2_), channel_id=1, source_target_pairs={{0,2},{2,0},{1,3},{3,1},{4,6},{6,4},{5,7},{7,5}} | collective-permute-start | bytes 6291464 | tf_op jit(solution)/shard_map/ppermute | solution.py:498
  140.6 96.0 %collective-permute-start.10 = (bf16[1024,1024]{1,0:T(8,128)(2,1)}, bf16[1024,1024]{1,0:T(8,128)(2,1)}, u32[]{:S(2)}, u32[]{:S(2)}) collective-permute-start(bf16[1024,1024]{1,0:T(8,128)(2,1)} %get-tuple-element.236.refs_2_), channel_id=1, source_target_pairs={{0,2},{2,0},{1,3},{3,1},{4,6},{6,4},{5,7},{7,5}} | collective-permute-start | bytes 6291464 | tf_op jit(solution)/shard_map/ppermute | solution.py:498
  170.2 94.7 %collective-permute-start.9 = (bf16[1024,1024]{1,0:T(8,128)(2,1)}, bf16[1024,1024]{1,0:T(8,128)(2,1)}, u32[]{:S(2)}, u32[]{:S(2)}) collective-permute-start(bf16[1024,1024]{1,0:T(8,128)(2,1)} %get-tuple-element.235.refs_2_), channel_id=1, source_target_pairs={{0,2},{2,0},{1,3},{3,1},{4,6},{6,4},{5,7},{7,5}} | collective-permute-start | bytes 6291464 | tf_op jit(solution)/shard_map/ppermute | solution.py:498
  196.9 95.9 %collective-permute-start.8 = (f32[4,2,8,128]{3,2,1,0:T(8,128)}, f32[4,2,8,128]{3,2,1,0:T(8,128)}, u32[]{:S(2)}, u32[]{:S(2)}) collective-permute-start(f32[4,2,8,128]{3,2,1,0:T(8,128)} %get-tuple-element.234.refs_5_), channel_id=1, source_target_pairs={{0,2},{2,0},{1,3},{3,1},{4,6},{6,4},{5,7},{7,5}} | collective-permute-start | bytes 98312 | tf_op jit(solution)/shard_map/ppermute | solution.py:496
  319.1 76.4 %collective-permute-start.16 = (f32[2,1024,1024]{2,1,0:T(8,128)}, f32[2,1024,1024]{2,1,0:T(8,128)}, u32[]{:S(2)}, u32[]{:S(2)}) collective-permute-start(f32[2,1024,1024]{2,1,0:T(8,128)} %get-tuple-element.263), channel_id=1, source_target_pairs={{0,1},{1,0},{2,3},{3,2},{4,5},{5,4},{6,7},{7,6}} | collective-permute-start | bytes 25165832 | tf_op jit(solution)/shard_map/ppermute | solution.py:500
  319.2 154.9 %collective-permute-start.13 = (bf16[4,1024,1024]{2,1,0:T(8,128)(2,1)}, bf16[4,1024,1024]{2,1,0:T(8,128)(2,1)}, u32[]{:S(2)}, u32[]{:S(2)}) collective-permute-start(bf16[4,1024,1024]{2,1,0:T(8,128)(2,1)} %get-tuple-element.258), channel_id=1, source_target_pairs={{0,1},{1,0},{2,3},{3,2},{4,5},{5,4},{6,7},{7,6}} | collective-permute-start | bytes 25165832 | tf_op jit(solution)/shard_map/ppermute | solution.py:492
  422.4 123.4 %collective-permute-start.17 = (f32[2,512,1024]{2,1,0:T(8,128)}, f32[2,512,1024]{2,1,0:T(8,128)}, u32[]{:S(2)}, u32[]{:S(2)}) collective-permute-start(f32[2,512,1024]{2,1,0:T(8,128)} %get-tuple-element.266), channel_id=1, source_target_pairs={{0,4},{4,0},{1,5},{5,1},{2,6},{6,2},{3,7},{7,3}} | collective-permute-start | bytes 12582920 | tf_op jit(solution)/shard_map/ppermute | solution.py:502
  424.6 93.2 %collective-permute-start.18 = (bf16[1024,1024]{1,0:T(8,128)(2,1)}, bf16[1024,1024]{1,0:T(8,128)(2,1)}, u32[]{:S(2)}, u32[]{:S(2)}) collective-permute-start(bf16[1024,1024]{1,0:T(8,128)(2,1)} %get-tuple-element.267.refs_2_), channel_id=1, source_target_pairs={{0,2},{2,0},{1,3},{3,1},{4,6},{6,4},{5,7},{7,5}} | collective-permute-start | bytes 6291464 | tf_op jit(solution)/shard_map/ppermute | solution.py:498
  426.1 135.0 %collective-permute-start.15 = (bf16[1024,1024]{1,0:T(8,128)(2,1)}, bf16[1024,1024]{1,0:T(8,128)(2,1)}, u32[]{:S(2)}, u32[]{:S(2)}) collective-permute-start(bf16[1024,1024]{1,0:T(8,128)(2,1)} %get-tuple-element.262.refs_2_), channel_id=1, source_target_pairs={{0,2},{2,0},{1,3},{3,1},{4,6},{6,4},{5,7},{7,5}} | collective-permute-start | bytes 6291464 | tf_op jit(solution)/shard_map/ppermute | solution.py:498
  472.9 116.2 %collective-permute-start.14 = (f32[4,2,8,128]{3,2,1,0:T(8,128)}, f32[4,2,8,128]{3,2,1,0:T(8,128)}, u32[]{:S(2)}, u32[]{:S(2)}) collective-permute-start(f32[4,2,8,128]{3,2,1,0:T(8,128)} %get-tuple-element.261.refs_5_), channel_id=1, source_target_pairs={{0,2},{2,0},{1,3},{3,1},{4,6},{6,4},{5,7},{7,5}} | collective-permute-start | bytes 98312 | tf_op jit(solution)/shard_map/ppermute | solution.py:496
  615.8 152.9 %collective-permute-start.21 = (bf16[4,1024,1024]{2,1,0:T(8,128)(2,1)}, bf16[4,1024,1024]{2,1,0:T(8,128)(2,1)}, u32[]{:S(2)}, u32[]{:S(2)}) collective-permute-start(bf16[4,1024,1024]{2,1,0:T(8,128)(2,1)} %get-tuple-element.290), channel_id=1, source_target_pairs={{0,1},{1,0},{2,3},{3,2},{4,5},{5,4},{6,7},{7,6}} | collective-permute-start | bytes 25165832 | tf_op jit(solution)/shard_map/ppermute | solution.py:492
  718.8 122.5 %collective-permute-start.25 = (f32[2,512,1024]{2,1,0:T(8,128)}, f32[2,512,1024]{2,1,0:T(8,128)}, u32[]{:S(2)}, u32[]{:S(2)}) collective-permute-start(f32[2,512,1024]{2,1,0:T(8,128)} %get-tuple-element.298), channel_id=1, source_target_pairs={{0,4},{4,0},{1,5},{5,1},{2,6},{6,2},{3,7},{7,3}} | collective-permute-start | bytes 12582920 | tf_op jit(solution)/shard_map/ppermute | solution.py:502
  719.8 93.3 %collective-permute-start.26 = (bf16[1024,1024]{1,0:T(8,128)(2,1)}, bf16[1024,1024]{1,0:T(8,128)(2,1)}, u32[]{:S(2)}, u32[]{:S(2)}) collective-permute-start(bf16[1024,1024]{1,0:T(8,128)(2,1)} %get-tuple-element.299.refs_2_), channel_id=1, source_target_pairs={{0,2},{2,0},{1,3},{3,1},{4,6},{6,4},{5,7},{7,5}} | collective-permute-start | bytes 6291464 | tf_op jit(solution)/shard_map/ppermute | solution.py:498
  721.4 135.0 %collective-permute-start.23 = (bf16[1024,1024]{1,0:T(8,128)(2,1)}, bf16[1024,1024]{1,0:T(8,128)(2,1)}, u32[]{:S(2)}, u32[]{:S(2)}) collective-permute-start(bf16[1024,1024]{1,0:T(8,128)(2,1)} %get-tuple-element.294.refs_2_), channel_id=1, source_target_pairs={{0,2},{2,0},{1,3},{3,1},{4,6},{6,4},{5,7},{7,5}} | collective-permute-start | bytes 6291464 | tf_op jit(solution)/shard_map/ppermute | solution.py:498
  768.2 116.1 %collective-permute-start.22 = (f32[4,2,8,128]{3,2,1,0:T(8,128)}, f32[4,2,8,128]{3,2,1,0:T(8,128)}, u32[]{:S(2)}, u32[]{:S(2)}) collective-permute-start(f32[4,2,8,128]{3,2,1,0:T(8,128)} %get-tuple-element.293.refs_5_), channel_id=1, source_target_pairs={{0,2},{2,0},{1,3},{3,1},{4,6},{6,4},{5,7},{7,5}} | collective-permute-start | bytes 98312 | tf_op jit(solution)/shard_map/ppermute | solution.py:496
  910.6 76.4 %collective-permute-start.32 = (f32[2,1024,1024]{2,1,0:T(8,128)}, f32[2,1024,1024]{2,1,0:T(8,128)}, u32[]{:S(2)}, u32[]{:S(2)}) collective-permute-start(f32[2,1024,1024]{2,1,0:T(8,128)} %get-tuple-element.329), channel_id=1, source_target_pairs={{0,1},{1,0},{2,3},{3,2},{4,5},{5,4},{6,7},{7,6}} | collective-permute-start | bytes 25165832 | tf_op jit(solution)/shard_map/ppermute | solution.py:500
  910.6 154.3 %collective-permute-start.29 = (bf16[4,1024,1024]{2,1,0:T(8,128)(2,1)}, bf16[4,1024,1024]{2,1,0:T(8,128)(2,1)}, u32[]{:S(2)}, u32[]{:S(2)}) collective-permute-start(bf16[4,1024,1024]{2,1,0:T(8,128)(2,1)} %get-tuple-element.324), channel_id=1, source_target_pairs={{0,1},{1,0},{2,3},{3,2},{4,5},{5,4},{6,7},{7,6}} | collective-permute-start | bytes 25165832 | tf_op jit(solution)/shard_map/ppermute | solution.py:492
  1014.0 123.4 %collective-permute-start.33 = (f32[2,512,1024]{2,1,0:T(8,128)}, f32[2,512,1024]{2,1,0:T(8,128)}, u32[]{:S(2)}, u32[]{:S(2)}) collective-permute-start(f32[2,512,1024]{2,1,0:T(8,128)} %get-tuple-element.332), channel_id=1, source_target_pairs={{0,4},{4,0},{1,5},{5,1},{2,6},{6,2},{3,7},{7,3}} | collective-permute-start | bytes 12582920 | tf_op jit(solution)/shard_map/ppermute | solution.py:502
  1016.2 93.2 %collective-permute-start.34 = (bf16[1024,1024]{1,0:T(8,128)(2,1)}, bf16[1024,1024]{1,0:T(8,128)(2,1)}, u32[]{:S(2)}, u32[]{:S(2)}) collective-permute-start(bf16[1024,1024]{1,0:T(8,128)(2,1)} %get-tuple-element.333.refs_2_), channel_id=1, source_target_pairs={{0,2},{2,0},{1,3},{3,1},{4,6},{6,4},{5,7},{7,5}} | collective-permute-start | bytes 6291464 | tf_op jit(solution)/shard_map/ppermute | solution.py:498
  1017.6 134.9 %collective-permute-start.31 = (bf16[1024,1024]{1,0:T(8,128)(2,1)}, bf16[1024,1024]{1,0:T(8,128)(2,1)}, u32[]{:S(2)}, u32[]{:S(2)}) collective-permute-start(bf16[1024,1024]{1,0:T(8,128)(2,1)} %get-tuple-element.328.refs_2_), channel_id=1, source_target_pairs={{0,2},{2,0},{1,3},{3,1},{4,6},{6,4},{5,7},{7,5}} | collective-permute-start | bytes 6291464 | tf_op jit(solution)/shard_map/ppermute | solution.py:498
  1064.4 116.2 %collective-permute-start.30 = (f32[4,2,8,128]{3,2,1,0:T(8,128)}, f32[4,2,8,128]{3,2,1,0:T(8,128)}, u32[]{:S(2)}, u32[]{:S(2)}) collective-permute-start(f32[4,2,8,128]{3,2,1,0:T(8,128)} %get-tuple-element.327.refs_5_), channel_id=1, source_target_pairs={{0,2},{2,0},{1,3},{3,1},{4,6},{6,4},{5,7},{7,5}} | collective-permute-start | bytes 98312 | tf_op jit(solution)/shard_map/ppermute | solution.py:496
  1207.3 76.4 %collective-permute-start.40 = (f32[2,1024,1024]{2,1,0:T(8,128)}, f32[2,1024,1024]{2,1,0:T(8,128)}, u32[]{:S(2)}, u32[]{:S(2)}) collective-permute-start(f32[2,1024,1024]{2,1,0:T(8,128)} %get-tuple-element.363), channel_id=1, source_target_pairs={{0,1},{1,0},{2,3},{3,2},{4,5},{5,4},{6,7},{7,6}} | collective-permute-start | bytes 25165832 | tf_op jit(solution)/shard_map/ppermute | solution.py:500
  1207.3 152.8 %collective-permute-start.37 = (bf16[4,1024,1024]{2,1,0:T(8,128)(2,1)}, bf16[4,1024,1024]{2,1,0:T(8,128)(2,1)}, u32[]{:S(2)}, u32[]{:S(2)}) collective-permute-start(bf16[4,1024,1024]{2,1,0:T(8,128)(2,1)} %get-tuple-element.358), channel_id=1, source_target_pairs={{0,1},{1,0},{2,3},{3,2},{4,5},{5,4},{6,7},{7,6}} | collective-permute-start | bytes 25165832 | tf_op jit(solution)/shard_map/ppermute | solution.py:492
  1310.3 118.0 %collective-permute-start.41 = (f32[2,512,1024]{2,1,0:T(8,128)}, f32[2,512,1024]{2,1,0:T(8,128)}, u32[]{:S(2)}, u32[]{:S(2)}) collective-permute-start(f32[2,512,1024]{2,1,0:T(8,128)} %get-tuple-element.366), channel_id=1, source_target_pairs={{0,4},{4,0},{1,5},{5,1},{2,6},{6,2},{3,7},{7,3}} | collective-permute-start | bytes 12582920 | tf_op jit(solution)/shard_map/ppermute | solution.py:502
  1311.3 93.3 %collective-permute-start.42 = (bf16[1024,1024]{1,0:T(8,128)(2,1)}, bf16[1024,1024]{1,0:T(8,128)(2,1)}, u32[]{:S(2)}, u32[]{:S(2)}) collective-permute-start(bf16[1024,1024]{1,0:T(8,128)(2,1)} %get-tuple-element.367.refs_2_), channel_id=1, source_target_pairs={{0,2},{2,0},{1,3},{3,1},{4,6},{6,4},{5,7},{7,5}} | collective-permute-start | bytes 6291464 | tf_op jit(solution)/shard_map/ppermute | solution.py:498
  1312.8 134.9 %collective-permute-start.39 = (bf16[1024,1024]{1,0:T(8,128)(2,1)}, bf16[1024,1024]{1,0:T(8,128)(2,1)}, u32[]{:S(2)}, u32[]{:S(2)}) collective-permute-start(bf16[1024,1024]{1,0:T(8,128)(2,1)} %get-tuple-element.362.refs_2_), channel_id=1, source_target_pairs={{0,2},{2,0},{1,3},{3,1},{4,6},{6,4},{5,7},{7,5}} | collective-permute-start | bytes 6291464 | tf_op jit(solution)/shard_map/ppermute | solution.py:498
  1359.6 111.9 %collective-permute-start.38 = (f32[4,2,8,128]{3,2,1,0:T(8,128)}, f32[4,2,8,128]{3,2,1,0:T(8,128)}, u32[]{:S(2)}, u32[]{:S(2)}) collective-permute-start(f32[4,2,8,128]{3,2,1,0:T(8,128)} %get-tuple-element.361.refs_5_), channel_id=1, source_target_pairs={{0,2},{2,0},{1,3},{3,1},{4,6},{6,4},{5,7},{7,5}} | collective-permute-start | bytes 98312 | tf_op jit(solution)/shard_map/ppermute | solution.py:496
  1601.1 93.8 %collective-permute-start.48 = (f32[2,512,1024]{2,1,0:T(8,128)}, f32[2,512,1024]{2,1,0:T(8,128)}, u32[]{:S(2)}, u32[]{:S(2)}) collective-permute-start(f32[2,512,1024]{2,1,0:T(8,128)} %get-tuple-element.401), channel_id=1, source_target_pairs={{0,4},{4,0},{1,5},{5,1},{2,6},{6,2},{3,7},{7,3}} | collective-permute-start | bytes 12582920 | tf_op jit(solution)/shard_map/ppermute | solution.py:502
  1641.2 143.1 %collective-permute-start.47 = (f32[2,512,1024]{2,1,0:T(8,128)}, f32[2,512,1024]{2,1,0:T(8,128)}, u32[]{:S(2)}, u32[]{:S(2)}) collective-permute-start(f32[2,512,1024]{2,1,0:T(8,128)} %get-tuple-element.399), channel_id=1, source_target_pairs={{0,4},{4,0},{1,5},{5,1},{2,6},{6,2},{3,7},{7,3}} | collective-permute-start | bytes 12582920 | tf_op jit(solution)/shard_map/ppermute | solution.py:502
  (18 other events, 674.0 us)

commit v2 on v1

--- a/solution.py
+++ b/solution.py
@@ -76,7 +76,8 @@
     return pl.BlockSpec((None, 2, 8, 128), lambda *_: (ex, 0, 0, 0))
 
 
-def chain_call(layer, ex, first, last, norms, scal, dz_prev, part_own, part_recv, u_all, u_recv, x_all, w_down, w_down_r, w_up, w_up_r, bufs, norm_buf, dep):
+def chain_call(layer, ex, first, last, norms, scal, dz_prev, part_own, part_recv, u_all, u_recv, x_all, w_down, w_down_r, w_up, w_up_r, bufs, norm_buf, pack_buf, dep):
+    packs = not last and ex < 2
     at_u = ex if u_recv.shape[0] == E else (ex - 1 if u_recv.shape[0] > 1 else 0)
     at_w = layer if w_down_r.shape[0] > 1 else 0
     names = ["scal", "dz"]
@@ -115,11 +116,20 @@
         out_names.append("part_out")
         out_shape.append(jax.ShapeDtypeStruct((T, D), BF16))
         out_specs.append(ANY)
+    if packs:
+        if pack_buf is not None:
+            aliases[len(args)] = len(out_names)
+            names.append("bp")
+            args.append(pack_buf)
+        out_names.append("pack_out")
+        out_shape.append(jax.ShapeDtypeStruct((E, T, Q), BF16))
+        out_specs.append(ANY)
     scratch = {
         "dzp": pltpu.VMEM((T, D), BF16), "po_s": pltpu.VMEM((T, D), BF16), "pr_s": pltpu.VMEM((T, D), BF16),
         "u_s": pltpu.VMEM((2, T, Q), BF16), "x_s": pltpu.VMEM((T, D), BF16), "w2_s": pltpu.VMEM((2 * Q, D), BF16), "w1_s": pltpu.VMEM((2, D, Q), BF16),
         "dz_s": pltpu.VMEM((T, D), BF16), "dh_s": pltpu.VMEM((T, 2 * Q), BF16), "h_s": pltpu.VMEM((T, 2 * Q), BF16), "part_s": pltpu.VMEM((T, D), BF16),
         "in_sem": pltpu.SemaphoreType.DMA((NB, 5)), "w_sem": pltpu.SemaphoreType.DMA((5,)), "out_sem": pltpu.SemaphoreType.DMA((NB, 4)),
+        "pk_s": pltpu.VMEM((2, T, Q), BF16), "pk_sem": pltpu.SemaphoreType.DMA((2, 2)),
     }
 
     def body(*refs):
@@ -174,6 +184,12 @@
         if norms:
             x_copy = pltpu.make_async_copy(r["x"].at[layer, here], r["x_s"], w_sem.at[4])
             x_copy.start()
+        if packs:
+            there = (1 - r["scal"][0]) * E
+            pack_in = [pltpu.make_async_copy(r["uo"].at[layer - 1, there + 2 * ex + j], r["pk_s"].at[j], r["pk_sem"].at[0, j]) for j in range(2)]
+            pack_out = [pltpu.make_async_copy(r["pk_s"].at[j], r["pack_out"].at[2 * ex + j], r["pk_sem"].at[1, j]) for j in range(2)]
+            for c in pack_in:
+                c.start()
         for c in w2:
             c.wait()
 
@@ -211,6 +227,10 @@
             return carry
 
         lax.fori_loop(0, NB, rows_step, 0)
+        if packs:
+            for a, b in zip(pack_in, pack_out):
+                a.wait()
+                b.start()
         if norms:
             x_copy.wait()
             store_norms(r["n_out"], r["tok"], *gram_norms(r["x_s"], r["dz_s"], r["dh_s"], r["h_s"]))
@@ -221,6 +241,9 @@
                 c.wait()
             if not last:
                 part_output(i).wait()
+        if packs:
+            for b in pack_out:
+                b.wait()
 
     outs = pl.pallas_call(
         body,
@@ -233,7 +256,7 @@
         grid=(1,),
     )(*args)
     named = dict(zip(out_names, outs))
-    return outs[:3], named.get("n_out", norm_buf), named.get("part_out"), named["tok"]
+    return outs[:3], named.get("n_out", norm_buf), named.get("part_out"), named.get("pack_out", pack_buf), named["tok"]
 
 
 def norm_call(layer, ex, scal, x_all, bufs, dep):
@@ -372,6 +395,80 @@
     )(scal, *args, dep)
 
 
+def weight_piece_call(layer, half, at, x_all, bufs, norms, norms_recv, clip_up, clip_down, scal, recv, dep):
+    dz, dh, hid = bufs
+    own = half == 0
+    steps = E * T // KB
+    per = T // KB
+
+    def body(*refs):
+        refs = list(refs)
+        _, x_ref, dh_ref, h_ref, dz_ref, no_ref, nr_ref, cu_ref, cd_ref = refs[:9]
+        del refs[:9]
+        if own:
+            recv_ref = refs.pop(0)
+        refs.pop(0)
+        out_ref, tok_ref, acc1, acc2 = refs
+        k = pl.program_id(0)
+        n = no_ref[...] + nr_ref[...]
+        c1 = jnp.minimum(1.0, cu_ref[layer] / jnp.sqrt(n[0, 0:1, 0:1]))
+        c2 = jnp.minimum(1.0, cd_ref[layer] / jnp.sqrt(n[1, 0:1, 0:1]))
+
+        def products():
+            g1 = lax.dot_general(x_ref[...], (dh_ref[...].astype(F32) * c1).astype(BF16), TN, preferred_element_type=F32)
+            g2 = lax.dot_general(h_ref[...], (dz_ref[...].astype(F32) * c2).astype(BF16), TN, preferred_element_type=F32)
+            return g1, g2
+
+        @pl.when(k == 0)
+        def _():
+            tok_ref[...] = jnp.zeros((8, 128), F32)
+            acc1[...], acc2[...] = products()
+
+        @pl.when((k > 0) & (k < steps - 1))
+        def _():
+            g1, g2 = products()
+            acc1[...] += g1
+            acc2[...] += g2
+
+        @pl.when(k == steps - 1)
+        def _():
+            g1, g2 = products()
+            g1 = acc1[...] + g1
+            g2 = acc2[...] + g2
+            if own:
+                g1 = g1 + recv_ref[0]
+            out_ref[0] = g1
+            for b in range(2):
+                cols = slice(b * 512, (b + 1) * 512)
+                out_ref[1, :, cols] = g2[cols] + recv_ref[1, :, cols] if own else g2[cols]
+
+    def d_half(s):
+        return 1 - s[1] if at == 0 else s[1]
+
+    norm_in = pl.BlockSpec((None, 2, 8, 128), lambda k, s: (k // per, 0, 0, 0))
+    piece = pl.BlockSpec((2, 512, 1024), lambda k, s: (0, 0, 0))
+    in_specs = [
+        pl.BlockSpec((None, None, KB, 512), lambda k, s: (layer, s[0] * E + k // per, k % per, d_half(s))),
+        pl.BlockSpec((None, KB, Q), lambda k, s: (k // per, k % per, half)),
+        pl.BlockSpec((None, KB, Q), lambda k, s: (k // per, k % per, half)),
+        pl.BlockSpec((None, KB, 512), lambda k, s: (k // per, k % per, d_half(s))),
+        norm_in, norm_in, SMEM, SMEM,
+    ]
+    args = [x_all, dh, hid, dz, norms, norms_recv, clip_up, clip_down]
+    if own:
+        in_specs.append(piece)
+        args.append(recv)
+    return pl.pallas_call(
+        body,
+        out_shape=[jax.ShapeDtypeStruct((2, 512, 1024), F32), TOKEN],
+        grid_spec=pltpu.PrefetchScalarGridSpec(
+            num_scalar_prefetch=1, grid=(steps,), in_specs=in_specs + [ANY], out_specs=[piece, TOKEN_SPEC],
+            scratch_shapes=[pltpu.VMEM((512, 1024), F32), pltpu.VMEM((1024, 512), F32)],
+        ),
+        compiler_params=PARAMS,
+    )(scal, *args, dep)
+
+
 def pack_call(layer, start, count, scal, u_all, dep, weights=()):
     nw = len(weights)
 
@@ -435,10 +532,12 @@
         steps = [("k", "chain", layer, e)]
         if e == E - 1:
             steps.append(("p", "n", layer, 0))
-        if layer > 0:
-            steps.append(("p", "x", layer, e))
+        if layer > 0 and e != E - 2:
+            steps += [("p", "x", layer, k) for k in ((E - 2, E - 1) if e == E - 1 else (e,))]
         if layer == top and e == 0:
             steps.append(("k", "norm", layer, e))
+        if layer > 0 and e == 1:
+            steps.append(("p", "u", layer - 1, E))
         return steps
 
     def give(layer):
@@ -447,24 +546,18 @@
     def own(layer):
         return [("k", "wgrad", layer, 0), ("p", "y", layer, 0)]
 
-    for layer in reversed(range(num_layers)):
-        order += chain(layer, 0)
-        if layer > 0:
-            order += [("k", "pack", layer - 1, E), ("p", "u", layer - 1, E)]
-        order += chain(layer, 1)
+    for layer in range(top, 0, -1):
+        order += chain(layer, 0) + chain(layer, 1) + chain(layer, 2)
+        if layer < top:
+            order += give(layer + 1)
+        order += chain(layer, 3)
         if layer + 2 <= top:
             order.append(("k", "final", layer + 2, 0))
-        order += chain(layer, 2)
-        if layer + 1 <= top:
-            order += give(layer + 1)
-        if layer > 0:
-            order += chain(layer, 3)
-            if layer + 1 <= top:
-                order += own(layer + 1)
-        else:
-            order += own(1) + chain(0, 3)
-    order += give(0) + own(0)
-    order += [("k", "final", 1, 0), ("k", "final", 0, 0)]
+        if layer < top:
+            order += own(layer + 1)
+    order += chain(0, 0) + give(1) + chain(0, 1) + own(1) + chain(0, 2) + chain(0, 3) + [("k", "final", 2, 0)]
+    order += [("k", "piece1", 0, 0), ("p", "c", 0, 0), ("k", "piece1", 0, 1), ("p", "c", 0, 1)]
+    order += [("k", "piece0", 0, 0), ("p", "y", 0, 0), ("k", "piece0", 0, 1), ("k", "final", 1, 0), ("k", "final", 0, 0)]
     return order
 
 
@@ -482,6 +575,7 @@
         scal = jnp.stack([lax.axis_index("tp") % 2, lax.axis_index("dp")]).astype(jnp.int32)
         tok = jnp.zeros((8, 128), F32)
         bufs, norms, part, part_recv, packed, u_recv, w_pack, w_recv = {}, {}, {}, {}, {}, {}, {}, {}
+        pieces = {}
         norms_recv, give, recv, y_send, keep, y_recv = {}, {}, {}, {}, {}, {}
         outs = None
         for step in program_order(num_layers):
@@ -497,23 +591,24 @@
                 elif what == "x":
                     part_recv[layer, k] = lax.ppermute(part[layer, k], "tp", swap_x)
                 elif what == "c":
-                    recv[layer] = lax.ppermute(give[layer], "tp", swap_core)
+                    if last:
+                        pieces[2, k] = lax.ppermute(pieces[1, k], "tp", swap_core)
+                    else:
+                        recv[layer] = lax.ppermute(give[layer], "tp", swap_core)
                 else:
                     y_recv[layer] = lax.ppermute(y_send[layer], "dp", swap_dp)
             elif what == "pack":
                 if first and k == 0:
                     packed[layer, k], w_pack[0], w_pack[1], tok = pack_call(layer, 0, 1, scal, u_stored, tok, (w_down, w_up))
-                elif first:
+                else:
                     packed[layer, k], tok = pack_call(layer, 1, E - 1, scal, u_stored, tok)
-                else:
-                    packed[layer, k], tok = pack_call(layer, 0, E, scal, u_stored, tok)
             elif what == "chain":
                 w_at = top if first else 0
-                bufs[layer], norms[layer], part[layer, k], tok = chain_call(
+                bufs[layer], norms[layer], part[layer, k], packed[layer - 1, E], tok = chain_call(
                     layer, k, first, last, not (first and k == 0), scal,
                     d_out if first else bufs[layer + 1][0], None if first else part[layer + 1, k], None if first else part_recv[layer + 1, k],
                     u_stored, u_recv[layer, min(k, 1) if first else E], x_stored,
-                    w_down, w_recv[w_at, 0], w_up, w_recv[w_at, 1], bufs.get(layer), norms.get(layer), tok,
+                    w_down, w_recv[w_at, 0], w_up, w_recv[w_at, 1], bufs.get(layer), norms.get(layer), packed.get((layer - 1, E)), tok,
                 )
             elif what == "norm":
                 norms[layer], tok = norm_call(layer, k, scal, x_stored, bufs[layer], tok)
@@ -526,6 +621,13 @@
                     give[layer] = got[0]
                 else:
                     y_send[layer], keep[layer] = got[:2]
+            elif what in ("piece1", "piece0"):
+                half = int(what[-1])
+                pieces[half, k], tok = weight_piece_call(
+                    layer, half, k, x_stored, bufs[layer], norms[layer], norms_recv[layer], clip_up, clip_down, scal, pieces.get((2, k)), tok
+                )
+                if half == 0:
+                    (y_send, keep)[k][layer] = pieces[0, k]
             else:
                 outs, tok = final_call(
                     layer, num_layers, total, keep[layer], y_recv[layer], noise_up, noise_down, clip_up, clip_down, noise_mult, outs, tok

time: 1800 us -> 1690 us (0.939)
  waiting for transfers between devices: 673 us -> 574 us
  Pallas kernels: 1080 us -> 1060 us
    ppermute x20, waiting for transfers between devices: 460 us -> 291 us  [local_step(): part_recv[layer, k] = lax.ppermute(part[layer, k], 'tp', swap_x)]
    ppermute x6, waiting for transfers between devices: 134 us -> 229 us  [local_step(): y_recv[layer] = lax.ppermute(y_send[layer], 'dp', swap_dp)]
    pallas_call x0 -> x4, Pallas kernels: none -> 73.3 us  [weight_piece_call(): pl.pallas_call(body, out_shape=[jax.ShapeDtypeStruct((2, 512, 1024), F32)...]
    pallas_call x12 -> x10, Pallas kernels: 318 us -> 266 us  [weight_call(): pl.pallas_call(body, out_shape=out_shape, grid_spec=pltpu.PrefetchScalarG...]
    pallas_call x7 -> x2, Pallas kernels: 61.4 us -> 13.1 us  [pack_call(): pl.pallas_call(body, out_shape=[jax.ShapeDtypeStruct((count, T, Q), BF16)...]
    ppermute x6 -> x5, waiting for transfers between devices: 24.9 us -> 0.01 us  [local_step(): recv[layer] = lax.ppermute(give[layer], 'tp', swap_core)]
    ppermute x4, waiting for transfers between devices: 28 us -> 50.7 us  [local_step(): lax.ppermute(w_pack[k] if first else (w_down, w_up)[k], 'tp', swap_core)]
    ppermute x7, waiting for transfers between devices: 22.1 us -> 3.01 us  [local_step(): u_recv[layer, k] = lax.ppermute(packed[layer, k], 'tp', swap_core)]
  transfers between devices with their start and end apart: 49 -> 50, of which waited for: 26 -> 18; matrix products, arithmetic and copies ran while one was open for 0% -> 0% of each run, Pallas kernels for 50% -> 53%
where the time goes in v2:
time: 1690 us; the launch traced here: 1680 us
  Pallas kernels  1060 us (63%)
  waiting for transfers between devices  574 us (34%)
  starting transfers between devices  45 us (3%)
    pallas_call x24, Pallas kernels, chain_call(): pl.pallas_call(body, out_shape=out_shape, in_specs=[SMEM] + [ANY] * (len(...  646 us
    ppermute x20, waiting for transfers between devices, local_step(): part_recv[layer, k] = lax.ppermute(part[layer, k], 'tp', swap_x)  291 us
    pallas_call x10, Pallas kernels, weight_call(): pl.pallas_call(body, out_shape=out_shape, grid_spec=pltpu.PrefetchScalarG...  266 us
    ppermute x6, waiting for transfers between devices, local_step(): y_recv[layer] = lax.ppermute(y_send[layer], 'dp', swap_dp)  229 us
    pallas_call x4, Pallas kernels, weight_piece_call(): pl.pallas_call(body, out_shape=[jax.ShapeDtypeStruct((2, 512, 1024), F32)...  73.3 us
    ppermute x4, waiting for transfers between devices, local_step(): lax.ppermute(w_pack[k] if first else (w_down, w_up)[k], 'tp', swap_core)  50.7 us
    pallas_call x6, Pallas kernels, final_call(): pl.pallas_call(body, out_shape=[jax.ShapeDtypeStruct((num_layers, 512, 10...  41.9 us
  transfers between devices with their start and end apart: 50, of which 18 were waited for; matrix products, arithmetic and copies ran while one was open for 0% of the time, Pallas kernels for 53%

profile of v2, /device:TPU:0, one launch (start us, length us, event | category | flops | bytes accessed | tf_op | source)
XLA Modules:
  0.0 1678.9 jit_solution(16534930734531717419)
XLA Ops:
  16.7 30.1 %collective-permute-done.1.refs_5_ = bf16[1,1024,1024]{2,1,0:T(8,128)(2,1)} collective-permute-done((bf16[1,1024,1024]{2,1,0:T(8,128)(2,1)}, bf16[1,1024,1024]{2,1,0:T(8,128)(2,1)}, u32[]{:S(2)}, u32[]{:S(2)}) %collective-permute-start.1) | collective-permute-done | bytes 2097184 | tf_op jit(solution)/shard_map/ppermute | solution.py:588
  105.9 27.3 %shard_map.117 = (bf16[4,1024,1024]{2,1,0:T(8,128)(2,1)}, bf16[4,1024,2048]{2,1,0:T(8,128)(2,1)}, bf16[4,1024,2048]{2,1,0:T(8,128)(2,1)}, f32[8,128]{1,0:T(8,128...) custom-call(s32[2]{0:T(128)} %pad_add_fusion.refs_0_.s_ref, ...), custom_call_target="tpu_custom_call", output_to_operand_aliasing={{0}: (10, {}), {1}: (11, {}), {2}: (12, {}), {4}: (13, {}),... | custom-call | tf_op jit(solution)/shard_map/pallas_call | solution.py:248
  211.7 28.3 %shard_map.120 = (bf16[4,1024,1024]{2,1,0:T(8,128)(2,1)}, bf16[4,1024,2048]{2,1,0:T(8,128)(2,1)}, bf16[4,1024,2048]{2,1,0:T(8,128)(2,1)}, f32[8,128]{1,0:T(8,128...) custom-call(s32[2]{0:T(128)} %pad_add_fusion.refs_0_.s_ref, ...), custom_call_target="tpu_custom_call" | custom-call | tf_op jit(solution)/shard_map/pallas_call | solution.py:248
  240.1 28.1 %shard_map.121 = (bf16[4,1024,1024]{2,1,0:T(8,128)(2,1)}, bf16[4,1024,2048]{2,1,0:T(8,128)(2,1)}, bf16[4,1024,2048]{2,1,0:T(8,128)(2,1)}, f32[8,128]{1,0:T(8,128...) custom-call(s32[2]{0:T(128)} %pad_add_fusion.refs_0_.s_ref, ...), custom_call_target="tpu_custom_call", output_to_operand_aliasing={{0}: (12, {}), {1}: (13, {}), {2}: (14, {}), {4}: (15, {}),... | custom-call | tf_op jit(solution)/shard_map/pallas_call | solution.py:248
  272.8 28.0 %shard_map.122 = (bf16[4,1024,1024]{2,1,0:T(8,128)(2,1)}, bf16[4,1024,2048]{2,1,0:T(8,128)(2,1)}, bf16[4,1024,2048]{2,1,0:T(8,128)(2,1)}, f32[8,128]{1,0:T(8,128...) custom-call(s32[2]{0:T(128)} %pad_add_fusion.refs_0_.s_ref, ...), custom_call_target="tpu_custom_call", output_to_operand_aliasing={{0}: (12, {}), {1}: (13, {}), {2}: (14, {}), {4}: (15, {})} | custom-call | tf_op jit(solution)/shard_map/pallas_call | solution.py:248
  331.7 45.0 %collective-permute-done.4.refs_3_ = bf16[1024,1024]{1,0:T(8,128)(2,1)} collective-permute-done((bf16[1024,1024]{1,0:T(8,128)(2,1)}, bf16[1024,1024]{1,0:T(8,128)(2,1)}, u32[]{:S(2)}, u32[]{:S(2)}) %collective-permute-start.4) | collective-permute-done | bytes 2097184 | tf_op jit(solution)/shard_map/ppermute | solution.py:592
  378.5 28.3 %shard_map.124 = (bf16[4,1024,1024]{2,1,0:T(8,128)(2,1)}, bf16[4,1024,2048]{2,1,0:T(8,128)(2,1)}, bf16[4,1024,2048]{2,1,0:T(8,128)(2,1)}, f32[8,128]{1,0:T(8,128...) custom-call(s32[2]{0:T(128)} %pad_add_fusion.refs_0_.s_ref, ...), custom_call_target="tpu_custom_call", output_to_operand_aliasing={{0}: (12, {}), {1}: (13, {}), {2}: (14, {}), {4}: (15, {})} | custom-call | tf_op jit(solution)/shard_map/pallas_call | solution.py:248
  407.1 26.7 %shard_map.125 = (f32[2,512,1024]{2,1,0:T(8,128)}, f32[2,512,1024]{2,1,0:T(8,128)}, f32[8,128]{1,0:T(8,128)}) custom-call(s32[2]{0:T(128)} %pad_add_fusion.refs_0_.s_ref, bf16[6,8,1024,1024]{3,2,1,0:T(8,128)(2,1)} %refs_1_.39, bf16[4,1024,2048]{2,1,0:T(8,128)(2,1)} %get-tuple-element.235.refs_2_, bf16[4,1024,2048]{2,1,0:T(8,128)(2,1)} %get-tuple-element.236.refs_3_, ...), custom_call_target="tpu_custom_call" | custom-call | tf_op jit(solution)/shard_map/pallas_call | solution.py:388
  433.8 28.0 %shard_map.126 = (bf16[4,1024,1024]{2,1,0:T(8,128)(2,1)}, bf16[4,1024,2048]{2,1,0:T(8,128)(2,1)}, bf16[4,1024,2048]{2,1,0:T(8,128)(2,1)}, f32[8,128]{1,0:T(8,128...) custom-call(s32[2]{0:T(128)} %pad_add_fusion.refs_0_.s_ref, ...), custom_call_target="tpu_custom_call" | custom-call | tf_op jit(solution)/shard_map/pallas_call | solution.py:248
  466.6 28.1 %shard_map.127 = (bf16[4,1024,1024]{2,1,0:T(8,128)(2,1)}, bf16[4,1024,2048]{2,1,0:T(8,128)(2,1)}, bf16[4,1024,2048]{2,1,0:T(8,128)(2,1)}, f32[8,128]{1,0:T(8,128...) custom-call(s32[2]{0:T(128)} %pad_add_fusion.refs_0_.s_ref, ...), custom_call_target="tpu_custom_call", output_to_operand_aliasing={{0}: (12, {}), {1}: (13, {}), {2}: (14, {}), {4}: (15, {}),... | custom-call | tf_op jit(solution)/shard_map/pallas_call | solution.py:248
  511.0 28.3 %shard_map.128 = (bf16[4,1024,1024]{2,1,0:T(8,128)(2,1)}, bf16[4,1024,2048]{2,1,0:T(8,128)(2,1)}, bf16[4,1024,2048]{2,1,0:T(8,128)(2,1)}, f32[8,128]{1,0:T(8,128...) custom-call(s32[2]{0:T(128)} %pad_add_fusion.refs_0_.s_ref, ...), custom_call_target="tpu_custom_call", output_to_operand_aliasing={{0}: (12, {}), {1}: (13, {}), {2}: (14, {}), {4}: (15, {})} | custom-call | tf_op jit(solution)/shard_map/pallas_call | solution.py:248
  570.0 46.8 %collective-permute-done.12.refs_3_ = bf16[1024,1024]{1,0:T(8,128)(2,1)} collective-permute-done((bf16[1024,1024]{1,0:T(8,128)(2,1)}, bf16[1024,1024]{1,0:T(8,128)(2,1)}, u32[]{:S(2)}, u32[]{:S(2)}) %collective-permute-start.12) | collective-permute-done | bytes 2097184 | tf_op jit(solution)/shard_map/ppermute | solution.py:592
  618.3 40.8 %collective-permute-done.26.refs_2_.refs_3_ = f32[2,512,1024]{2,1,0:T(8,128)} collective-permute-done((f32[2,512,1024]{2,1,0:T(8,128)}, f32[2,512,1024]{2,1,0:T(8,128)}, u32[]{:S(2)}, u32[]{:S(2)}) %collective-permute-start.26) | collective-permute-done | bytes 4194336 | tf_op jit(solution)/shard_map/ppermute | solution.py:599
  660.8 28.0 %shard_map.130 = (bf16[4,1024,1024]{2,1,0:T(8,128)(2,1)}, bf16[4,1024,2048]{2,1,0:T(8,128)(2,1)}, bf16[4,1024,2048]{2,1,0:T(8,128)(2,1)}, f32[8,128]{1,0:T(8,128...) custom-call(s32[2]{0:T(128)} %pad_add_fusion.refs_0_.s_ref, ...), custom_call_target="tpu_custom_call", output_to_operand_aliasing={{0}: (12, {}), {1}: (13, {}), {2}: (14, {}), {4}: (15, {})} | custom-call | tf_op jit(solution)/shard_map/pallas_call | solution.py:248
  696.8 26.8 %shard_map.132 = (f32[2,512,1024]{2,1,0:T(8,128)}, f32[2,512,1024]{2,1,0:T(8,128)}, f32[8,128]{1,0:T(8,128)}) custom-call(s32[2]{0:T(128)} %pad_add_fusion.refs_0_.s_ref, bf16[6,8,1024,1024]{3,2,1,0:T(8,128)(2,1)} %refs_1_.39, bf16[4,1024,2048]{2,1,0:T(8,128)(2,1)} %get-tuple-element.262.refs_2_, bf16[4,1024,2048]{2,1,0:T(8,128)(2,1)} %get-tuple-element.263.refs_3_, ...), custom_call_target="tpu_custom_call" | custom-call | tf_op jit(solution)/shard_map/pallas_call | solution.py:388
  723.6 28.3 %shard_map.133 = (bf16[4,1024,1024]{2,1,0:T(8,128)(2,1)}, bf16[4,1024,2048]{2,1,0:T(8,128)(2,1)}, bf16[4,1024,2048]{2,1,0:T(8,128)(2,1)}, f32[8,128]{1,0:T(8,128...) custom-call(s32[2]{0:T(128)} %pad_add_fusion.refs_0_.s_ref, ...), custom_call_target="tpu_custom_call" | custom-call | tf_op jit(solution)/shard_map/pallas_call | solution.py:248
  751.9 28.0 %shard_map.134 = (bf16[4,1024,1024]{2,1,0:T(8,128)(2,1)}, bf16[4,1024,2048]{2,1,0:T(8,128)(2,1)}, bf16[4,1024,2048]{2,1,0:T(8,128)(2,1)}, f32[8,128]{1,0:T(8,128...) custom-call(s32[2]{0:T(128)} %pad_add_fusion.refs_0_.s_ref, ...), custom_call_target="tpu_custom_call", output_to_operand_aliasing={{0}: (12, {}), {1}: (13, {}), {2}: (14, {}), {4}: (15, {}),... | custom-call | tf_op jit(solution)/shard_map/pallas_call | solution.py:248
  779.9 28.0 %shard_map.135 = (bf16[4,1024,1024]{2,1,0:T(8,128)(2,1)}, bf16[4,1024,2048]{2,1,0:T(8,128)(2,1)}, bf16[4,1024,2048]{2,1,0:T(8,128)(2,1)}, f32[8,128]{1,0:T(8,128...) custom-call(s32[2]{0:T(128)} %pad_add_fusion.refs_0_.s_ref, ...), custom_call_target="tpu_custom_call", output_to_operand_aliasing={{0}: (12, {}), {1}: (13, {}), {2}: (14, {}), {4}: (15, {})} | custom-call | tf_op jit(solution)/shard_map/pallas_call | solution.py:248
  838.9 46.8 %collective-permute-done.19.refs_3_ = bf16[1024,1024]{1,0:T(8,128)(2,1)} collective-permute-done((bf16[1024,1024]{1,0:T(8,128)(2,1)}, bf16[1024,1024]{1,0:T(8,128)(2,1)}, u32[]{:S(2)}, u32[]{:S(2)}) %collective-permute-start.19) | collective-permute-done | bytes 2097184 | tf_op jit(solution)/shard_map/ppermute | solution.py:592
  887.2 40.8 %collective-permute-done.34.refs_2_.refs_3_ = f32[2,512,1024]{2,1,0:T(8,128)} collective-permute-done((f32[2,512,1024]{2,1,0:T(8,128)}, f32[2,512,1024]{2,1,0:T(8,128)}, u32[]{:S(2)}, u32[]{:S(2)}) %collective-permute-start.34) | collective-permute-done | bytes 4194336 | tf_op jit(solution)/shard_map/ppermute | solution.py:599
  929.6 28.3 %shard_map.137 = (bf16[4,1024,1024]{2,1,0:T(8,128)(2,1)}, bf16[4,1024,2048]{2,1,0:T(8,128)(2,1)}, bf16[4,1024,2048]{2,1,0:T(8,128)(2,1)}, f32[8,128]{1,0:T(8,128...) custom-call(s32[2]{0:T(128)} %pad_add_fusion.refs_0_.s_ref, ...), custom_call_target="tpu_custom_call", output_to_operand_aliasing={{0}: (12, {}), {1}: (13, {}), {2}: (14, {}), {4}: (15, {})} | custom-call | tf_op jit(solution)/shard_map/pallas_call | solution.py:248
  965.2 26.8 %shard_map.139 = (f32[2,512,1024]{2,1,0:T(8,128)}, f32[2,512,1024]{2,1,0:T(8,128)}, f32[8,128]{1,0:T(8,128)}) custom-call(s32[2]{0:T(128)} %pad_add_fusion.refs_0_.s_ref, bf16[6,8,1024,1024]{3,2,1,0:T(8,128)(2,1)} %refs_1_.39, bf16[4,1024,2048]{2,1,0:T(8,128)(2,1)} %get-tuple-element.291.refs_2_, bf16[4,1024,2048]{2,1,0:T(8,128)(2,1)} %get-tuple-element.292.refs_3_, ...), custom_call_target="tpu_custom_call" | custom-call | tf_op jit(solution)/shard_map/pallas_call | solution.py:388
  992.1 28.0 %shard_map.140 = (bf16[4,1024,1024]{2,1,0:T(8,128)(2,1)}, bf16[4,1024,2048]{2,1,0:T(8,128)(2,1)}, bf16[4,1024,2048]{2,1,0:T(8,128)(2,1)}, f32[8,128]{1,0:T(8,128...) custom-call(s32[2]{0:T(128)} %pad_add_fusion.refs_0_.s_ref, ...), custom_call_target="tpu_custom_call" | custom-call | tf_op jit(solution)/shard_map/pallas_call | solution.py:248
  1020.2 28.1 %shard_map.141 = (bf16[4,1024,1024]{2,1,0:T(8,128)(2,1)}, bf16[4,1024,2048]{2,1,0:T(8,128)(2,1)}, bf16[4,1024,2048]{2,1,0:T(8,128)(2,1)}, f32[8,128]{1,0:T(8,128...) custom-call(s32[2]{0:T(128)} %pad_add_fusion.refs_0_.s_ref, ...), custom_call_target="tpu_custom_call", output_to_operand_aliasing={{0}: (12, {}), {1}: (13, {}), {2}: (14, {}), {4}: (15, {}),... | custom-call | tf_op jit(solution)/shard_map/pallas_call | solution.py:248
  1048.3 28.3 %shard_map.142 = (bf16[4,1024,1024]{2,1,0:T(8,128)(2,1)}, bf16[4,1024,2048]{2,1,0:T(8,128)(2,1)}, bf16[4,1024,2048]{2,1,0:T(8,128)(2,1)}, f32[8,128]{1,0:T(8,128...) custom-call(s32[2]{0:T(128)} %pad_add_fusion.refs_0_.s_ref, ...), custom_call_target="tpu_custom_call", output_to_operand_aliasing={{0}: (12, {}), {1}: (13, {}), {2}: (14, {}), {4}: (15, {})} | custom-call | tf_op jit(solution)/shard_map/pallas_call | solution.py:248
  1107.4 46.8 %collective-permute-done.27.refs_3_ = bf16[1024,1024]{1,0:T(8,128)(2,1)} collective-permute-done((bf16[1024,1024]{1,0:T(8,128)(2,1)}, bf16[1024,1024]{1,0:T(8,128)(2,1)}, u32[]{:S(2)}, u32[]{:S(2)}) %collective-permute-start.27) | collective-permute-done | bytes 2097184 | tf_op jit(solution)/shard_map/ppermute | solution.py:592
  1154.2 28.0 %shard_map.144 = (bf16[4,1024,1024]{2,1,0:T(8,128)(2,1)}, bf16[4,1024,2048]{2,1,0:T(8,128)(2,1)}, bf16[4,1024,2048]{2,1,0:T(8,128)(2,1)}, f32[8,128]{1,0:T(8,128...) custom-call(s32[2]{0:T(128)} %pad_add_fusion.refs_0_.s_ref, ...), custom_call_target="tpu_custom_call", output_to_operand_aliasing={{0}: (12, {}), {1}: (13, {}), {2}: (14, {}), {4}: (15, {})} | custom-call | tf_op jit(solution)/shard_map/pallas_call | solution.py:248
  1203.5 26.8 %shard_map.146 = (f32[2,512,1024]{2,1,0:T(8,128)}, f32[2,512,1024]{2,1,0:T(8,128)}, f32[8,128]{1,0:T(8,128)}) custom-call(s32[2]{0:T(128)} %pad_add_fusion.refs_0_.s_ref, bf16[6,8,1024,1024]{3,2,1,0:T(8,128)(2,1)} %refs_1_.39, bf16[4,1024,2048]{2,1,0:T(8,128)(2,1)} %get-tuple-element.323.refs_2_, bf16[4,1024,2048]{2,1,0:T(8,128)(2,1)} %get-tuple-element.324.refs_3_, ...), custom_call_target="tpu_custom_call" | custom-call | tf_op jit(solution)/shard_map/pallas_call | solution.py:388
  1286.4 45.3 %collective-permute-done.43.refs_3_ = bf16[1024,1024]{1,0:T(8,128)(2,1)} collective-permute-done((bf16[1024,1024]{1,0:T(8,128)(2,1)}, bf16[1024,1024]{1,0:T(8,128)(2,1)}, u32[]{:S(2)}, u32[]{:S(2)}) %collective-permute-start.43) | collective-permute-done | bytes 2097184 | tf_op jit(solution)/shard_map/ppermute | solution.py:592
  1355.6 26.9 %shard_map.150 = (f32[2,512,1024]{2,1,0:T(8,128)}, f32[2,512,1024]{2,1,0:T(8,128)}, f32[8,128]{1,0:T(8,128)}) custom-call(s32[2]{0:T(128)} %pad_add_fusion.refs_0_.s_ref, bf16[6,8,1024,1024]{3,2,1,0:T(8,128)(2,1)} %refs_1_.39, bf16[4,1024,2048]{2,1,0:T(8,128)(2,1)} %get-tuple-element.358.refs_2_, bf16[4,1024,2048]{2,1,0:T(8,128)(2,1)} %get-tuple-element.359.refs_3_, ...), custom_call_target="tpu_custom_call" | custom-call | tf_op jit(solution)/shard_map/pallas_call | solution.py:388
  1529.6 53.1 %collective-permute-done.49.refs_2_.refs_3_ = f32[2,512,1024]{2,1,0:T(8,128)} collective-permute-done((f32[2,512,1024]{2,1,0:T(8,128)}, f32[2,512,1024]{2,1,0:T(8,128)}, u32[]{:S(2)}, u32[]{:S(2)}) %collective-permute-start.49) | collective-permute-done | bytes 4194336 | tf_op jit(solution)/shard_map/ppermute | solution.py:599
  1589.6 82.0 %collective-permute-done.48.refs_2_.refs_3_ = f32[2,512,1024]{2,1,0:T(8,128)} collective-permute-done((f32[2,512,1024]{2,1,0:T(8,128)}, f32[2,512,1024]{2,1,0:T(8,128)}, u32[]{:S(2)}, u32[]{:S(2)}) %collective-permute-start.48) | collective-permute-done | bytes 4194336 | tf_op jit(solution)/shard_map/ppermute | solution.py:599
  (121 shorter events, 588.0 us)
Async XLA Ops:
  14.9 91.0 %collective-permute-start = (bf16[3,1024,1024]{2,1,0:T(8,128)(2,1)}, bf16[3,1024,1024]{2,1,0:T(8,128)(2,1)}, u32[]{:S(2)}, u32[]{:S(2)}) collective-permute-start(bf16[3,1024,1024]{2,1,0:T(8,128)(2,1)} %get-tuple-element.210), channel_id=1, source_target_pairs={{0,1},{1,0},{2,3},{3,2},{4,5},{5,4},{6,7},{7,6}} | collective-permute-start | bytes 18874376 | tf_op jit(solution)/shard_map/ppermute | solution.py:586
  15.7 196.0 %collective-permute-start.6 = (bf16[6,1024,1024]{2,1,0:T(8,128)(2,1)}, bf16[6,1024,1024]{2,1,0:T(8,128)(2,1)}, u32[]{:S(2)}, u32[]{:S(2)}) collective-permute-start(bf16[6,1024,1024]{2,1,0:T(8,128)(2,1)} %refs_6_.56), channel_id=1, source_target_pairs={{0,1},{1,0},{2,3},{3,2},{4,5},{5,4},{6,7},{7,6}} | collective-permute-start | bytes 37748744 | tf_op jit(solution)/shard_map/ppermute | solution.py:588
  16.2 195.5 %collective-permute-start.7 = (bf16[6,1024,1024]{2,1,0:T(8,128)(2,1)}, bf16[6,1024,1024]{2,1,0:T(8,128)(2,1)}, u32[]{:S(2)}, u32[]{:S(2)}) collective-permute-start(bf16[6,1024,1024]{2,1,0:T(8,128)(2,1)} %refs_9_.31), channel_id=1, source_target_pairs={{0,1},{1,0},{2,3},{3,2},{4,5},{5,4},{6,7},{7,6}} | collective-permute-start | bytes 37748744 | tf_op jit(solution)/shard_map/ppermute | solution.py:588
  136.2 103.9 %collective-permute-start.10 = (bf16[1024,1024]{1,0:T(8,128)(2,1)}, bf16[1024,1024]{1,0:T(8,128)(2,1)}, u32[]{:S(2)}, u32[]{:S(2)}) collective-permute-start(bf16[1024,1024]{1,0:T(8,128)(2,1)} %get-tuple-element.239.refs_2_), channel_id=1, source_target_pairs={{0,2},{2,0},{1,3},{3,1},{4,6},{6,4},{5,7},{7,5}} | collective-permute-start | bytes 6291464 | tf_op jit(solution)/shard_map/ppermute | solution.py:592
  327.4 106.4 %collective-permute-start.13 = (bf16[4,1024,1024]{2,1,0:T(8,128)(2,1)}, bf16[4,1024,1024]{2,1,0:T(8,128)(2,1)}, u32[]{:S(2)}, u32[]{:S(2)}) collective-permute-start(bf16[4,1024,1024]{2,1,0:T(8,128)(2,1)} %get-tuple-element.261), channel_id=1, source_target_pairs={{0,1},{1,0},{2,3},{3,2},{4,5},{5,4},{6,7},{7,6}} | collective-permute-start | bytes 25165832 | tf_op jit(solution)/shard_map/ppermute | solution.py:586
  329.7 104.1 %collective-permute-start.17 = (bf16[1024,1024]{1,0:T(8,128)(2,1)}, bf16[1024,1024]{1,0:T(8,128)(2,1)}, u32[]{:S(2)}, u32[]{:S(2)}) collective-permute-start(bf16[1024,1024]{1,0:T(8,128)(2,1)} %get-tuple-element.267.refs_2_), channel_id=1, source_target_pairs={{0,2},{2,0},{1,3},{3,1},{4,6},{6,4},{5,7},{7,5}} | collective-permute-start | bytes 6291464 | tf_op jit(solution)/shard_map/ppermute | solution.py:592
  330.0 136.7 %collective-permute-start.16 = (bf16[1024,1024]{1,0:T(8,128)(2,1)}, bf16[1024,1024]{1,0:T(8,128)(2,1)}, u32[]{:S(2)}, u32[]{:S(2)}) collective-permute-start(bf16[1024,1024]{1,0:T(8,128)(2,1)} %get-tuple-element.266.refs_2_), channel_id=1, source_target_pairs={{0,2},{2,0},{1,3},{3,1},{4,6},{6,4},{5,7},{7,5}} | collective-permute-start | bytes 6291464 | tf_op jit(solution)/shard_map/ppermute | solution.py:592
  376.7 134.3 %collective-permute-start.15 = (bf16[1024,1024]{1,0:T(8,128)(2,1)}, bf16[1024,1024]{1,0:T(8,128)(2,1)}, u32[]{:S(2)}, u32[]{:S(2)}) collective-permute-start(bf16[1024,1024]{1,0:T(8,128)(2,1)} %get-tuple-element.265.refs_2_), channel_id=1, source_target_pairs={{0,2},{2,0},{1,3},{3,1},{4,6},{6,4},{5,7},{7,5}} | collective-permute-start | bytes 6291464 | tf_op jit(solution)/shard_map/ppermute | solution.py:592
  406.8 132.5 %collective-permute-start.14 = (f32[4,2,8,128]{3,2,1,0:T(8,128)}, f32[4,2,8,128]{3,2,1,0:T(8,128)}, u32[]{:S(2)}, u32[]{:S(2)}) collective-permute-start(f32[4,2,8,128]{3,2,1,0:T(8,128)} %get-tuple-element.264.refs_5_), channel_id=1, source_target_pairs={{0,2},{2,0},{1,3},{3,1},{4,6},{6,4},{5,7},{7,5}} | collective-permute-start | bytes 98312 | tf_op jit(solution)/shard_map/ppermute | solution.py:590
  565.7 123.1 %collective-permute-start.25 = (f32[2,1024,1024]{2,1,0:T(8,128)}, f32[2,1024,1024]{2,1,0:T(8,128)}, u32[]{:S(2)}, u32[]{:S(2)}) collective-permute-start(f32[2,1024,1024]{2,1,0:T(8,128)} %get-tuple-element.297), channel_id=1, source_target_pairs={{0,1},{1,0},{2,3},{3,2},{4,5},{5,4},{6,7},{7,6}} | collective-permute-start | bytes 25165832 | tf_op jit(solution)/shard_map/ppermute | solution.py:597
  565.7 157.9 %collective-permute-start.20 = (bf16[4,1024,1024]{2,1,0:T(8,128)(2,1)}, bf16[4,1024,1024]{2,1,0:T(8,128)(2,1)}, u32[]{:S(2)}, u32[]{:S(2)}) collective-permute-start(bf16[4,1024,1024]{2,1,0:T(8,128)(2,1)} %get-tuple-element.290), channel_id=1, source_target_pairs={{0,1},{1,0},{2,3},{3,2},{4,5},{5,4},{6,7},{7,6}} | collective-permute-start | bytes 25165832 | tf_op jit(solution)/shard_map/ppermute | solution.py:586
  566.2 92.9 %collective-permute-start.26 = (f32[2,512,1024]{2,1,0:T(8,128)}, f32[2,512,1024]{2,1,0:T(8,128)}, u32[]{:S(2)}, u32[]{:S(2)}) collective-permute-start(f32[2,512,1024]{2,1,0:T(8,128)} %get-tuple-element.299), channel_id=1, source_target_pairs={{0,4},{4,0},{1,5},{5,1},{2,6},{6,2},{3,7},{7,3}} | collective-permute-start | bytes 12582920 | tf_op jit(solution)/shard_map/ppermute | solution.py:599
  569.5 154.1 %collective-permute-start.24 = (bf16[1024,1024]{1,0:T(8,128)(2,1)}, bf16[1024,1024]{1,0:T(8,128)(2,1)}, u32[]{:S(2)}, u32[]{:S(2)}) collective-permute-start(bf16[1024,1024]{1,0:T(8,128)(2,1)} %get-tuple-element.296.refs_2_), channel_id=1, source_target_pairs={{0,2},{2,0},{1,3},{3,1},{4,6},{6,4},{5,7},{7,5}} | collective-permute-start | bytes 6291464 | tf_op jit(solution)/shard_map/ppermute | solution.py:592
  616.8 135.1 %collective-permute-start.23 = (bf16[1024,1024]{1,0:T(8,128)(2,1)}, bf16[1024,1024]{1,0:T(8,128)(2,1)}, u32[]{:S(2)}, u32[]{:S(2)}) collective-permute-start(bf16[1024,1024]{1,0:T(8,128)(2,1)} %get-tuple-element.295.refs_2_), channel_id=1, source_target_pairs={{0,2},{2,0},{1,3},{3,1},{4,6},{6,4},{5,7},{7,5}} | collective-permute-start | bytes 6291464 | tf_op jit(solution)/shard_map/ppermute | solution.py:592
  659.1 120.9 %collective-permute-start.22 = (bf16[1024,1024]{1,0:T(8,128)(2,1)}, bf16[1024,1024]{1,0:T(8,128)(2,1)}, u32[]{:S(2)}, u32[]{:S(2)}) collective-permute-start(bf16[1024,1024]{1,0:T(8,128)(2,1)} %get-tuple-element.294.refs_2_), channel_id=1, source_target_pairs={{0,2},{2,0},{1,3},{3,1},{4,6},{6,4},{5,7},{7,5}} | collective-permute-start | bytes 6291464 | tf_op jit(solution)/shard_map/ppermute | solution.py:592
  688.8 119.2 %collective-permute-start.21 = (f32[4,2,8,128]{3,2,1,0:T(8,128)}, f32[4,2,8,128]{3,2,1,0:T(8,128)}, u32[]{:S(2)}, u32[]{:S(2)}) collective-permute-start(f32[4,2,8,128]{3,2,1,0:T(8,128)} %get-tuple-element.293.refs_5_), channel_id=1, source_target_pairs={{0,2},{2,0},{1,3},{3,1},{4,6},{6,4},{5,7},{7,5}} | collective-permute-start | bytes 98312 | tf_op jit(solution)/shard_map/ppermute | solution.py:590
  834.5 123.3 %collective-permute-start.33 = (f32[2,1024,1024]{2,1,0:T(8,128)}, f32[2,1024,1024]{2,1,0:T(8,128)}, u32[]{:S(2)}, u32[]{:S(2)}) collective-permute-start(f32[2,1024,1024]{2,1,0:T(8,128)} %get-tuple-element.329), channel_id=1, source_target_pairs={{0,1},{1,0},{2,3},{3,2},{4,5},{5,4},{6,7},{7,6}} | collective-permute-start | bytes 25165832 | tf_op jit(solution)/shard_map/ppermute | solution.py:597
  834.5 157.6 %collective-permute-start.28 = (bf16[4,1024,1024]{2,1,0:T(8,128)(2,1)}, bf16[4,1024,1024]{2,1,0:T(8,128)(2,1)}, u32[]{:S(2)}, u32[]{:S(2)}) collective-permute-start(bf16[4,1024,1024]{2,1,0:T(8,128)(2,1)} %get-tuple-element.322), channel_id=1, source_target_pairs={{0,1},{1,0},{2,3},{3,2},{4,5},{5,4},{6,7},{7,6}} | collective-permute-start | bytes 25165832 | tf_op jit(solution)/shard_map/ppermute | solution.py:586
  835.0 92.9 %collective-permute-start.34 = (f32[2,512,1024]{2,1,0:T(8,128)}, f32[2,512,1024]{2,1,0:T(8,128)}, u32[]{:S(2)}, u32[]{:S(2)}) collective-permute-start(f32[2,512,1024]{2,1,0:T(8,128)} %get-tuple-element.331), channel_id=1, source_target_pairs={{0,4},{4,0},{1,5},{5,1},{2,6},{6,2},{3,7},{7,3}} | collective-permute-start | bytes 12582920 | tf_op jit(solution)/shard_map/ppermute | solution.py:599
  838.4 153.7 %collective-permute-start.32 = (bf16[1024,1024]{1,0:T(8,128)(2,1)}, bf16[1024,1024]{1,0:T(8,128)(2,1)}, u32[]{:S(2)}, u32[]{:S(2)}) collective-permute-start(bf16[1024,1024]{1,0:T(8,128)(2,1)} %get-tuple-element.328.refs_2_), channel_id=1, source_target_pairs={{0,2},{2,0},{1,3},{3,1},{4,6},{6,4},{5,7},{7,5}} | collective-permute-start | bytes 6291464 | tf_op jit(solution)/shard_map/ppermute | solution.py:592
  885.7 134.5 %collective-permute-start.31 = (bf16[1024,1024]{1,0:T(8,128)(2,1)}, bf16[1024,1024]{1,0:T(8,128)(2,1)}, u32[]{:S(2)}, u32[]{:S(2)}) collective-permute-start(bf16[1024,1024]{1,0:T(8,128)(2,1)} %get-tuple-element.327.refs_2_), channel_id=1, source_target_pairs={{0,2},{2,0},{1,3},{3,1},{4,6},{6,4},{5,7},{7,5}} | collective-permute-start | bytes 6291464 | tf_op jit(solution)/shard_map/ppermute | solution.py:592
  927.9 120.3 %collective-permute-start.30 = (bf16[1024,1024]{1,0:T(8,128)(2,1)}, bf16[1024,1024]{1,0:T(8,128)(2,1)}, u32[]{:S(2)}, u32[]{:S(2)}) collective-permute-start(bf16[1024,1024]{1,0:T(8,128)(2,1)} %get-tuple-element.326.refs_2_), channel_id=1, source_target_pairs={{0,2},{2,0},{1,3},{3,1},{4,6},{6,4},{5,7},{7,5}} | collective-permute-start | bytes 6291464 | tf_op jit(solution)/shard_map/ppermute | solution.py:592
  957.8 118.7 %collective-permute-start.29 = (f32[4,2,8,128]{3,2,1,0:T(8,128)}, f32[4,2,8,128]{3,2,1,0:T(8,128)}, u32[]{:S(2)}, u32[]{:S(2)}) collective-permute-start(f32[4,2,8,128]{3,2,1,0:T(8,128)} %get-tuple-element.325.refs_5_), channel_id=1, source_target_pairs={{0,2},{2,0},{1,3},{3,1},{4,6},{6,4},{5,7},{7,5}} | collective-permute-start | bytes 98312 | tf_op jit(solution)/shard_map/ppermute | solution.py:590
  1103.0 100.5 %collective-permute-start.40 = (f32[2,1024,1024]{2,1,0:T(8,128)}, f32[2,1024,1024]{2,1,0:T(8,128)}, u32[]{:S(2)}, u32[]{:S(2)}) collective-permute-start(f32[2,1024,1024]{2,1,0:T(8,128)} %get-tuple-element.362), channel_id=1, source_target_pairs={{0,1},{1,0},{2,3},{3,2},{4,5},{5,4},{6,7},{7,6}} | collective-permute-start | bytes 25165832 | tf_op jit(solution)/shard_map/ppermute | solution.py:597
  1103.0 127.3 %collective-permute-start.36 = (bf16[4,1024,1024]{2,1,0:T(8,128)(2,1)}, bf16[4,1024,1024]{2,1,0:T(8,128)(2,1)}, u32[]{:S(2)}, u32[]{:S(2)}) collective-permute-start(bf16[4,1024,1024]{2,1,0:T(8,128)(2,1)} %get-tuple-element.356), channel_id=1, source_target_pairs={{0,1},{1,0},{2,3},{3,2},{4,5},{5,4},{6,7},{7,6}} | collective-permute-start | bytes 25165832 | tf_op jit(solution)/shard_map/ppermute | solution.py:586
  1103.5 92.9 %collective-permute-start.41 = (f32[2,512,1024]{2,1,0:T(8,128)}, f32[2,512,1024]{2,1,0:T(8,128)}, u32[]{:S(2)}, u32[]{:S(2)}) collective-permute-start(f32[2,512,1024]{2,1,0:T(8,128)} %get-tuple-element.364), channel_id=1, source_target_pairs={{0,4},{4,0},{1,5},{5,1},{2,6},{6,2},{3,7},{7,3}} | collective-permute-start | bytes 12582920 | tf_op jit(solution)/shard_map/ppermute | solution.py:599
  1106.9 123.4 %collective-permute-start.39 = (bf16[1024,1024]{1,0:T(8,128)(2,1)}, bf16[1024,1024]{1,0:T(8,128)(2,1)}, u32[]{:S(2)}, u32[]{:S(2)}) collective-permute-start(bf16[1024,1024]{1,0:T(8,128)(2,1)} %get-tuple-element.361.refs_2_), channel_id=1, source_target_pairs={{0,2},{2,0},{1,3},{3,1},{4,6},{6,4},{5,7},{7,5}} | collective-permute-start | bytes 6291464 | tf_op jit(solution)/shard_map/ppermute | solution.py:592
  1281.0 165.0 %collective-permute-start.45 = (f32[2,512,1024]{2,1,0:T(8,128)}, f32[2,512,1024]{2,1,0:T(8,128)}, u32[]{:S(2)}, u32[]{:S(2)}) collective-permute-start(f32[2,512,1024]{2,1,0:T(8,128)} %get-tuple-element.394), channel_id=1, source_target_pairs={{0,4},{4,0},{1,5},{5,1},{2,6},{6,2},{3,7},{7,3}} | collective-permute-start | bytes 12582920 | tf_op jit(solution)/shard_map/ppermute | solution.py:599
  1284.4 98.1 %collective-permute-start.37 = (bf16[1024,1024]{1,0:T(8,128)(2,1)}, bf16[1024,1024]{1,0:T(8,128)(2,1)}, u32[]{:S(2)}, u32[]{:S(2)}) collective-permute-start(bf16[1024,1024]{1,0:T(8,128)(2,1)} %get-tuple-element.357.refs_2_), channel_id=1, source_target_pairs={{0,2},{2,0},{1,3},{3,1},{4,6},{6,4},{5,7},{7,5}} | collective-permute-start | bytes 6291464 | tf_op jit(solution)/shard_map/ppermute | solution.py:592
  1284.9 135.9 %collective-permute-start.35 = (bf16[1024,1024]{1,0:T(8,128)(2,1)}, bf16[1024,1024]{1,0:T(8,128)(2,1)}, u32[]{:S(2)}, u32[]{:S(2)}) collective-permute-start(bf16[1024,1024]{1,0:T(8,128)(2,1)} %get-tuple-element.355.refs_2_), channel_id=1, source_target_pairs={{0,2},{2,0},{1,3},{3,1},{4,6},{6,4},{5,7},{7,5}} | collective-permute-start | bytes 6291464 | tf_op jit(solution)/shard_map/ppermute | solution.py:592
  1488.9 93.8 %collective-permute-start.49 = (f32[2,512,1024]{2,1,0:T(8,128)}, f32[2,512,1024]{2,1,0:T(8,128)}, u32[]{:S(2)}, u32[]{:S(2)}) collective-permute-start(f32[2,512,1024]{2,1,0:T(8,128)} %get-tuple-element.407), channel_id=1, source_target_pairs={{0,4},{4,0},{1,5},{5,1},{2,6},{6,2},{3,7},{7,3}} | collective-permute-start | bytes 12582920 | tf_op jit(solution)/shard_map/ppermute | solution.py:599
  1508.3 163.3 %collective-permute-start.48 = (f32[2,512,1024]{2,1,0:T(8,128)}, f32[2,512,1024]{2,1,0:T(8,128)}, u32[]{:S(2)}, u32[]{:S(2)}) collective-permute-start(f32[2,512,1024]{2,1,0:T(8,128)} %get-tuple-element.405), channel_id=1, source_target_pairs={{0,4},{4,0},{1,5},{5,1},{2,6},{6,2},{3,7},{7,3}} | collective-permute-start | bytes 12582920 | tf_op jit(solution)/shard_map/ppermute | solution.py:599
  (20 other events, 933.4 us)

commit v3 on v2

--- a/solution.py
+++ b/solution.py
@@ -15,7 +15,6 @@
 E = 4
 TB = 512
 NB = T // TB
-KB = 512
 GB = 256
 F32 = jnp.float32
 BF16 = jnp.bfloat16
@@ -25,6 +24,8 @@
 TOKEN_SPEC = pl.BlockSpec((8, 128), lambda *_: (0, 0))
 NT = (((1,), (1,)), ((), ()))
 TN = (((0,), (0,)), ((), ()))
+CHAIN_FORM = ((False, True, 512), (True, True, 512), (True, False, 256), (True, False, 512), (False, True, 512), (False, True, 512))
+WGRAD_FORM = ((512, True), (1024, True), (512, False), (1024, False), (512, False), (1024, True))
 PARAMS = pltpu.CompilerParams(vmem_limit_bytes=63 * 1024 * 1024)
 
 
@@ -40,27 +41,51 @@
     return pl.ds(pl.multiple_of(i * size, size), size)
 
 
-def gram_norms(x_ref, dz_ref, dh_ref, h_ref):
-    def gram(ref, rows, cols):
-        return lax.dot_general(ref[rows, :], ref[cols, :], NT, preferred_element_type=F32)
-
-    def fold(p):
-        return jnp.sum(p.reshape(p.shape[0] // 8, 8, GB), axis=0)
-
+def gram(ref, rows, cols):
+    return lax.dot_general(ref[rows, :], ref[cols, :], NT, preferred_element_type=F32)
+
+
+def fold(p):
+    return jnp.sum(p.reshape(p.shape[0] // 8, 8, GB), axis=0)
+
+
+def ring_rows(k):
+    return slice(0, 2 * GB) if k == 3 else slice(k * GB, (k + 2) * GB)
+
+
+SINGLES = ((3, 3, 1.0), (2, 0, 2.0))
+
+
+def single_block(r, c):
+    return slice(r * GB, (r + 1) * GB), slice(c * GB, (c + 1) * GB)
+
+
+def gram_x_ring(k, x_ref, ring_ref):
+    ring_ref[k] = gram(x_ref, ring_rows(k), slice(k * GB, (k + 1) * GB))
+
+
+def gram_x_single(k, x_ref, single_ref):
+    single_ref[k] = gram(x_ref, *single_block(*SINGLES[k][:2]))
+
+
+def gram_norms(ring_ref, single_ref, dz_ref, dh_ref, h_ref):
     def ring(k, sums):
         at = jnp.where(k == 3, 0, k)
         w = jnp.where(k == 3, 2.0, 1.0)
         rows, cols = pl.ds(pl.multiple_of(at * GB, GB), 2 * GB), block(k, GB)
-        p1 = gram(x_ref, rows, cols) * gram(dh_ref, rows, cols)
+        p1 = ring_ref[k] * gram(dh_ref, rows, cols)
         p2 = gram(h_ref, rows, cols) * gram(dz_ref, rows, cols)
         return tuple(t + (w * fold(p[:GB]) + 2.0 * fold(p[GB:])) for t, p in zip(sums, (p1, p2)))
 
     n1, n2 = lax.fori_loop(0, 4, ring, (jnp.zeros((8, GB), F32), jnp.zeros((8, GB), F32)))
-    for r, c, w in ((3, 3, 1.0), (2, 0, 2.0)):
-        rows, cols = slice(r * GB, (r + 1) * GB), slice(c * GB, (c + 1) * GB)
-        n1 = n1 + w * fold(gram(x_ref, rows, cols) * gram(dh_ref, rows, cols))
+    for k, (r, c, w) in enumerate(SINGLES):
+        rows, cols = single_block(r, c)
+        n1 = n1 + w * fold(single_ref[k] * gram(dh_ref, rows, cols))
         n2 = n2 + w * fold(gram(h_ref, rows, cols) * gram(dz_ref, rows, cols))
     return jnp.sum(n1), jnp.sum(n2)
+
+
+GRAM_SCRATCH = (pltpu.VMEM((4, 2 * GB, GB), F32), pltpu.VMEM((2, GB, GB), F32))
 
 
 def store_norms(n_ref, tok_ref, n1, n2):
@@ -128,7 +153,8 @@
         "dzp": pltpu.VMEM((T, D), BF16), "po_s": pltpu.VMEM((T, D), BF16), "pr_s": pltpu.VMEM((T, D), BF16),
         "u_s": pltpu.VMEM((2, T, Q), BF16), "x_s": pltpu.VMEM((T, D), BF16), "w2_s": pltpu.VMEM((2 * Q, D), BF16), "w1_s": pltpu.VMEM((2, D, Q), BF16),
         "dz_s": pltpu.VMEM((T, D), BF16), "dh_s": pltpu.VMEM((T, 2 * Q), BF16), "h_s": pltpu.VMEM((T, 2 * Q), BF16), "part_s": pltpu.VMEM((T, D), BF16),
-        "in_sem": pltpu.SemaphoreType.DMA((NB, 5)), "w_sem": pltpu.SemaphoreType.DMA((5,)), "out_sem": pltpu.SemaphoreType.DMA((NB, 4)),
+        "ring_s": GRAM_SCRATCH[0], "single_s": GRAM_SCRATCH[1],
+        "in_sem": pltpu.SemaphoreType.DMA((NB, 5)), "w_sem": pltpu.SemaphoreType.DMA((7,)), "out_sem": pltpu.SemaphoreType.DMA((NB, 4)),
         "pk_s": pltpu.VMEM((2, T, Q), BF16), "pk_sem": pltpu.SemaphoreType.DMA((2, 2)),
     }
 
@@ -165,75 +191,140 @@
             return pltpu.make_async_copy(r["part_s"].at[rows], r["part_out"].at[rows], out_sem.at[i, 3])
 
         w2 = [
-            pltpu.make_async_copy(r["w2o"].at[layer], r["w2_s"].at[pl.ds(0, Q)], w_sem.at[0]),
-            pltpu.make_async_copy(r["w2r"].at[at_w], r["w2_s"].at[pl.ds(Q, Q)], w_sem.at[1]),
+            pltpu.make_async_copy(
+                (r["w2o"].at[layer] if c < 2 else r["w2r"].at[at_w]).at[pl.ds((c % 2) * 512, 512)], r["w2_s"].at[pl.ds(c * 512, 512)], w_sem.at[c]
+            )
+            for c in range(4)
         ]
-        ins = inputs(0)
-        for c in ins[:-2] + [w2[0], ins[-2], w2[1], ins[-1]]:
-            c.start()
+        ins = [inputs(i) for i in range(NB)]
+        flat, late, wide = CHAIN_FORM[layer]
+        now = ins[0][:-2] + [w2[0], ins[0][-2], w2[1], w2[2], ins[0][-1], w2[3]]
+        later = []
+        if norms:
+            x_copy = pltpu.make_async_copy(r["x"].at[layer, here], r["x_s"], w_sem.at[4])
+            (now if flat else later).append(x_copy)
+        later = ins[1] + later
         if not last:
             w1 = [
-                pltpu.make_async_copy(r["w1o"].at[layer], r["w1_s"].at[0], w_sem.at[2]),
-                pltpu.make_async_copy(r["w1r"].at[at_w], r["w1_s"].at[1], w_sem.at[3]),
+                pltpu.make_async_copy(r["w1o"].at[layer], r["w1_s"].at[0], w_sem.at[5]),
+                pltpu.make_async_copy(r["w1r"].at[at_w], r["w1_s"].at[1], w_sem.at[6]),
             ]
-            for c in w1:
-                c.start()
-        for i in range(1, NB):
-            for c in inputs(i):
-                c.start()
-        if norms:
-            x_copy = pltpu.make_async_copy(r["x"].at[layer, here], r["x_s"], w_sem.at[4])
-            x_copy.start()
+            later = w1 + later
         if packs:
             there = (1 - r["scal"][0]) * E
             pack_in = [pltpu.make_async_copy(r["uo"].at[layer - 1, there + 2 * ex + j], r["pk_s"].at[j], r["pk_sem"].at[0, j]) for j in range(2)]
             pack_out = [pltpu.make_async_copy(r["pk_s"].at[j], r["pack_out"].at[2 * ex + j], r["pk_sem"].at[1, j]) for j in range(2)]
-            for c in pack_in:
-                c.start()
-        for c in w2:
-            c.wait()
-
-        def rows_step(i, carry):
-            rows = block(i, TB)
-            for c in inputs(i):
-                c.wait()
+            later += pack_in
+        for c in now + ([] if late else later):
+            c.start()
+
+        def store_dz(rows):
             if first:
-                dz = r["dzp"][rows, :]
+                r["dz_s"][rows, :] = r["dzp"][rows, :]
             else:
-                dz = (r["dzp"][rows, :].astype(F32) + (r["po_s"][rows, :].astype(F32) + r["pr_s"][rows, :].astype(F32))).astype(BF16)
-            r["dz_s"][rows, :] = dz
-            for c in range(4):
-                cols = slice(c * 512, (c + 1) * 512)
-                back = lax.dot_general(dz, r["w2_s"][cols, :], NT, preferred_element_type=F32)
-                val, slope = gelu_pair(r["u_s"][c // 2, rows, (c % 2) * 512:(c % 2 + 1) * 512].astype(F32))
+                r["dz_s"][rows, :] = (r["dzp"][rows, :].astype(F32) + (r["po_s"][rows, :].astype(F32) + r["pr_s"][rows, :].astype(F32))).astype(BF16)
+
+        def back_chunk(rows, c):
+            for lo in range(c * 512, (c + 1) * 512, wide):
+                cols, part = slice(lo, lo + wide), slice(lo % Q, lo % Q + wide)
+                back = lax.dot_general(r["dz_s"][rows, :], r["w2_s"][cols, :], NT, preferred_element_type=F32)
+                val, slope = gelu_pair(r["u_s"][c // 2, rows, part].astype(F32))
                 r["dh_s"][rows, cols] = (slope * back).astype(BF16)
                 r["h_s"][rows, cols] = val.astype(BF16)
+
+        def part_chunk(rows, c):
+            cols = slice(c * 512, (c + 1) * 512)
+            acc = lax.dot_general(r["dh_s"][rows, :Q], r["w1_s"][0, cols, :], NT, preferred_element_type=F32)
+            acc = acc + lax.dot_general(r["dh_s"][rows, Q:], r["w1_s"][1, cols, :], NT, preferred_element_type=F32)
+            r["part_s"][rows, cols] = acc.astype(BF16)
+
+        rows0, rows1 = slice(0, TB), slice(TB, T)
+        if flat:
+            for o in ins[0][:-2]:
+                o.wait()
+            store_dz(rows0)
+            for o in now[-(len(now) - len(ins[0][:-2])):]:
+                o.wait()
+            if late:
+                for o in later:
+                    o.start()
+            for c in range(4):
+                back_chunk(rows0, c)
+                if norms:
+                    gram_x_ring(c, r["x_s"], r["ring_s"])
+            for o in ins[1][:-2]:
+                o.wait()
+            store_dz(rows1)
+            for o in ins[1][-2:] + ([] if last else w1):
+                o.wait()
+            for c in range(4):
+                back_chunk(rows1, c)
+                if c == 0:
+                    for o in outputs(0):
+                        o.start()
+                if norms and c < 2:
+                    gram_x_single(c, r["x_s"], r["single_s"])
+                if not last and c % 2 == 1:
+                    part_chunk(rows0, c // 2)
+            if packs:
+                for p, q in zip(pack_in, pack_out):
+                    p.wait()
+                    q.start()
             if not last:
-
-                @pl.when(i == 0)
+                part_chunk(rows1, 0)
+                part_output(0).start()
+                part_chunk(rows1, 1)
+                part_output(1).start()
+            for o in outputs(1):
+                o.start()
+        else:
+            for o in now[len(ins[0][:-2]):]:
+                o.wait()
+            for o in ins[0][:-2]:
+                o.wait()
+            if late:
+                for o in later:
+                    o.start()
+
+            def rows_step(i, carry):
+                rows = block(i, TB)
+
+                @pl.when(i > 0)
                 def _():
-                    for c in w1:
-                        c.wait()
-
-                for c in range(2):
-                    cols = slice(c * 512, (c + 1) * 512)
-                    acc = lax.dot_general(r["dh_s"][rows, :Q], r["w1_s"][0, cols, :], NT, preferred_element_type=F32)
-                    acc = acc + lax.dot_general(r["dh_s"][rows, Q:], r["w1_s"][1, cols, :], NT, preferred_element_type=F32)
-                    r["part_s"][rows, cols] = acc.astype(BF16)
-            for c in outputs(i):
-                c.start()
-            if not last:
-                part_output(i).start()
-            return carry
-
-        lax.fori_loop(0, NB, rows_step, 0)
-        if packs:
-            for a, b in zip(pack_in, pack_out):
-                a.wait()
-                b.start()
+                    for o in ins[1]:
+                        o.wait()
+
+                store_dz(rows)
+                for c in range(4):
+                    back_chunk(rows, c)
+                if not last:
+
+                    @pl.when(i == 0)
+                    def _():
+                        for o in w1:
+                            o.wait()
+
+                    part_chunk(rows, 0)
+                    part_chunk(rows, 1)
+                for o in outputs(i):
+                    o.start()
+                if not last:
+                    part_output(i).start()
+                return carry
+
+            lax.fori_loop(0, NB, rows_step, 0)
+            if packs:
+                for p, q in zip(pack_in, pack_out):
+                    p.wait()
+                    q.start()
+            if norms:
+                x_copy.wait()
+                for k in range(4):
+                    gram_x_ring(k, r["x_s"], r["ring_s"])
+                for k in range(2):
+                    gram_x_single(k, r["x_s"], r["single_s"])
         if norms:
-            x_copy.wait()
-            store_norms(r["n_out"], r["tok"], *gram_norms(r["x_s"], r["dz_s"], r["dh_s"], r["h_s"]))
+            store_norms(r["n_out"], r["tok"], *gram_norms(r["ring_s"], r["single_s"], r["dz_s"], r["dh_s"], r["h_s"]))
         else:
             r["tok"][...] = jnp.zeros((8, 128), F32)
         for i in range(NB):
@@ -260,8 +351,12 @@
 
 
 def norm_call(layer, ex, scal, x_all, bufs, dep):
-    def body(s_ref, x_ref, dz_ref, dh_ref, h_ref, dep_ref, n_ref, tok_ref):
-        store_norms(n_ref, tok_ref, *gram_norms(x_ref, dz_ref, dh_ref, h_ref))
+    def body(s_ref, x_ref, dz_ref, dh_ref, h_ref, dep_ref, n_ref, tok_ref, ring_ref, single_ref):
+        for k in range(4):
+            gram_x_ring(k, x_ref, ring_ref)
+        for k in range(2):
+            gram_x_single(k, x_ref, single_ref)
+        store_norms(n_ref, tok_ref, *gram_norms(ring_ref, single_ref, dz_ref, dh_ref, h_ref))
 
     def at(width):
         return pl.BlockSpec((None, T, width), lambda i, s: (ex, 0, 0))
@@ -272,7 +367,7 @@
         grid_spec=pltpu.PrefetchScalarGridSpec(
             num_scalar_prefetch=1, grid=(1,),
             in_specs=[pl.BlockSpec((None, None, T, D), lambda i, s: (layer, s[0] * E + ex, 0, 0)), at(D), at(2 * Q), at(2 * Q), ANY],
-            out_specs=[norm_spec(ex), TOKEN_SPEC],
+            out_specs=[norm_spec(ex), TOKEN_SPEC], scratch_shapes=GRAM_SCRATCH,
         ),
         compiler_params=PARAMS,
     )(scal, x_all, *bufs, dep)
@@ -281,8 +376,9 @@
 def weight_call(layer, half, x_all, bufs, norms, norms_recv, clip_up, clip_down, scal, recv, dep):
     dz, dh, hid = bufs
     own = half == 0
-    steps = E * T // KB
-    per = T // KB
+    kb, split = WGRAD_FORM[layer]
+    steps = E * T // kb
+    per = T // kb
 
     def body(*refs):
         refs = list(refs)
@@ -327,31 +423,49 @@
             dhc = (dh_ref[...].astype(F32) * c1).astype(BF16)
             if final and own:
                 recv_copy.wait()
-            started = []
-            for at in range(2):
-                ds = block(halves[at], 512)
+            if split:
+                started = []
+                for at in range(2):
+                    ds = block(halves[at], 512)
+                    for g in range(2):
+                        if g == 0:
+                            part = (0, ds)
+                            new = lax.dot_general(x_ref[:, ds], dhc, TN, preferred_element_type=F32)
+                        else:
+                            part = (1, slice(None), ds)
+                            new = lax.dot_general(h_ref[...], (dz_ref[:, ds].astype(F32) * c2).astype(BF16), TN, preferred_element_type=F32)
+                        if not init:
+                            new = acc[part] + new
+                        if final and own:
+                            new = new + recv_s[part]
+                        acc[part] = new
+                        if final:
+                            if started:
+                                for c in copies(*started[-1]):
+                                    c.start()
+                            started.append((g, at))
+                if final:
+                    for c in copies(*started[-1]):
+                        c.start()
+                    for s in started:
+                        for c in copies(*s):
+                            c.wait()
+            else:
                 for g in range(2):
                     if g == 0:
-                        part = (0, ds)
-                        new = lax.dot_general(x_ref[:, ds], dhc, TN, preferred_element_type=F32)
+                        new = lax.dot_general(x_ref[...], dhc, TN, preferred_element_type=F32)
                     else:
-                        part = (1, slice(None), ds)
-                        new = lax.dot_general(h_ref[...], (dz_ref[:, ds].astype(F32) * c2).astype(BF16), TN, preferred_element_type=F32)
+                        new = lax.dot_general(h_ref[...], (dz_ref[...].astype(F32) * c2).astype(BF16), TN, preferred_element_type=F32)
                     if not init:
-                        new = acc[part] + new
+                        new = acc[g] + new
                     if final and own:
-                        new = new + recv_s[part]
-                    acc[part] = new
-                    if final:
-                        if started:
-                            for c in copies(*started[-1]):
-                                c.start()
-                        started.append((g, at))
-            if final:
-                for c in copies(*started[-1]):
-                    c.start()
-                for s in started:
-                    for c in copies(*s):
+                        new = new + recv_s[g]
+                    acc[g] = new
+                if final:
+                    sent = [c for at in range(2) for g in range(2) for c in copies(g, at)]
+                    for c in sent:
+                        c.start()
+                    for c in sent:
                         c.wait()
 
         @pl.when(k == 0)
@@ -368,10 +482,10 @@
 
     norm_in = pl.BlockSpec((None, 2, 8, 128), lambda k, s: (k // per, 0, 0, 0))
     in_specs = [
-        pl.BlockSpec((None, None, KB, D), lambda k, s: (layer, s[0] * E + k // per, k % per, 0)),
-        pl.BlockSpec((None, KB, Q), lambda k, s: (k // per, k % per, half)),
-        pl.BlockSpec((None, KB, Q), lambda k, s: (k // per, k % per, half)),
-        pl.BlockSpec((None, KB, D), lambda k, s: (k // per, k % per, 0)),
+        pl.BlockSpec((None, None, kb, D), lambda k, s: (layer, s[0] * E + k // per, k % per, 0)),
+        pl.BlockSpec((None, kb, Q), lambda k, s: (k // per, k % per, half)),
+        pl.BlockSpec((None, kb, Q), lambda k, s: (k // per, k % per, half)),
+        pl.BlockSpec((None, kb, D), lambda k, s: (k // per, k % per, 0)),
         norm_in, norm_in, SMEM, SMEM,
     ]
     args = [x_all, dh, hid, dz, norms, norms_recv, clip_up, clip_down]
@@ -398,8 +512,7 @@
 def weight_piece_call(layer, half, at, x_all, bufs, norms, norms_recv, clip_up, clip_down, scal, recv, dep):
     dz, dh, hid = bufs
     own = half == 0
-    steps = E * T // KB
-    per = T // KB
+    steps = E
 
     def body(*refs):
         refs = list(refs)
@@ -445,13 +558,13 @@
     def d_half(s):
         return 1 - s[1] if at == 0 else s[1]
 
-    norm_in = pl.BlockSpec((None, 2, 8, 128), lambda k, s: (k // per, 0, 0, 0))
+    norm_in = pl.BlockSpec((None, 2, 8, 128), lambda k, s: (k, 0, 0, 0))
     piece = pl.BlockSpec((2, 512, 1024), lambda k, s: (0, 0, 0))
     in_specs = [
-        pl.BlockSpec((None, None, KB, 512), lambda k, s: (layer, s[0] * E + k // per, k % per, d_half(s))),
-        pl.BlockSpec((None, KB, Q), lambda k, s: (k // per, k % per, half)),
-        pl.BlockSpec((None, KB, Q), lambda k, s: (k // per, k % per, half)),
-        pl.BlockSpec((None, KB, 512), lambda k, s: (k // per, k % per, d_half(s))),
+        pl.BlockSpec((None, None, T, 512), lambda k, s: (layer, s[0] * E + k, 0, d_half(s))),
+        pl.BlockSpec((None, T, Q), lambda k, s: (k, 0, half)),
+        pl.BlockSpec((None, T, Q), lambda k, s: (k, 0, half)),
+        pl.BlockSpec((None, T, 512), lambda k, s: (k, 0, d_half(s))),
         norm_in, norm_in, SMEM, SMEM,
     ]
     args = [x_all, dh, hid, dz, norms, norms_recv, clip_up, clip_down]
@@ -529,11 +642,12 @@
     order += [("k", "pack", top, 1), ("p", "u", top, 1), ("p", "w", 0, 0), ("p", "w", 0, 1)]
 
     def chain(layer, e):
+        held = range(E - 3 if layer == 1 else E - 2, E)
         steps = [("k", "chain", layer, e)]
         if e == E - 1:
             steps.append(("p", "n", layer, 0))
-        if layer > 0 and e != E - 2:
-            steps += [("p", "x", layer, k) for k in ((E - 2, E - 1) if e == E - 1 else (e,))]
+        if layer > 0 and (e == E - 1 or e not in held):
+            steps += [("p", "x", layer, k) for k in (held if e == E - 1 else (e,))]
         if layer == top and e == 0:
             steps.append(("k", "norm", layer, e))
         if layer > 0 and e == 1:
@@ -551,13 +665,13 @@
         if layer < top:
             order += give(layer + 1)
         order += chain(layer, 3)
-        if layer + 2 <= top:
+        if 1 < layer < top - 1:
             order.append(("k", "final", layer + 2, 0))
         if layer < top:
             order += own(layer + 1)
-    order += chain(0, 0) + give(1) + chain(0, 1) + own(1) + chain(0, 2) + chain(0, 3) + [("k", "final", 2, 0)]
-    order += [("k", "piece1", 0, 0), ("p", "c", 0, 0), ("k", "piece1", 0, 1), ("p", "c", 0, 1)]
-    order += [("k", "piece0", 0, 0), ("p", "y", 0, 0), ("k", "piece0", 0, 1), ("k", "final", 1, 0), ("k", "final", 0, 0)]
+    order += give(1) + chain(0, 0) + own(1) + chain(0, 1) + chain(0, 2) + [("k", "final", 3, 0)] + chain(0, 3)
+    order += [("k", "piece1", 0, 0), ("p", "c", 0, 0), ("k", "final", 2, 0), ("k", "piece0", 0, 0), ("p", "y", 0, 0)]
+    order += [("k", "piece1", 0, 1), ("p", "c", 0, 1), ("k", "final", 1, 0), ("k", "piece0", 0, 1), ("k", "final", 0, 0)]
     return order
 
 

time: 1690 us -> 1740 us (1.030)
  waiting for transfers between devices: 574 us -> 621 us
    ppermute x6, waiting for transfers between devices: 229 us -> 262 us  [local_step(): y_recv[layer] = lax.ppermute(y_send[layer], 'dp', swap_dp)]
  transfers between devices with their start and end apart: 50 -> 50, of which waited for: 18 -> 20; matrix products, arithmetic and copies ran while one was open for 0% -> 0% of each run, Pallas kernels for 53% -> 53%
where the time goes in v3:
time: 1740 us; the launch traced here: 1730 us
  Pallas kernels  1060 us (61%)
  waiting for transfers between devices  621 us (36%)
  starting transfers between devices  44 us (3%)
    pallas_call x24, Pallas kernels, chain_call(): pl.pallas_call(body, out_shape=out_shape, in_specs=[SMEM] + [ANY] * (len(...  648 us
    ppermute x20, waiting for transfers between devices, local_step(): part_recv[layer, k] = lax.ppermute(part[layer, k], 'tp', swap_x)  303 us
    pallas_call x10, Pallas kernels, weight_call(): pl.pallas_call(body, out_shape=out_shape, grid_spec=pltpu.PrefetchScalarG...  270 us
    ppermute x6, waiting for transfers between devices, local_step(): y_recv[layer] = lax.ppermute(y_send[layer], 'dp', swap_dp)  262 us
    pallas_call x4, Pallas kernels, weight_piece_call(): pl.pallas_call(body, out_shape=[jax.ShapeDtypeStruct((2, 512, 1024), F32)...  69.4 us
    ppermute x4, waiting for transfers between devices, local_step(): lax.ppermute(w_pack[k] if first else (w_down, w_up)[k], 'tp', swap_core)  50.7 us
    pallas_call x6, Pallas kernels, final_call(): pl.pallas_call(body, out_shape=[jax.ShapeDtypeStruct((num_layers, 512, 10...  41.9 us
  transfers between devices with their start and end apart: 50, of which 20 were waited for; matrix products, arithmetic and copies ran while one was open for 0% of the time, Pallas kernels for 53%

profile of v3, /device:TPU:0, one launch (start us, length us, event | category | flops | bytes accessed | tf_op | source)
XLA Modules:
  0.0 1727.7 jit_solution(11496176897794062732)
XLA Ops:
  16.8 30.1 %collective-permute-done.1.refs_5_ = bf16[1,1024,1024]{2,1,0:T(8,128)(2,1)} collective-permute-done((bf16[1,1024,1024]{2,1,0:T(8,128)(2,1)}, bf16[1,1024,1024]{2,1,0:T(8,128)(2,1)}, u32[]{:S(2)}, u32[]{:S(2)}) %collective-permute-start.1) | collective-permute-done | bytes 2097184 | tf_op jit(solution)/shard_map/ppermute | solution.py:702
  136.5 27.6 %shard_map.118 = (bf16[4,1024,1024]{2,1,0:T(8,128)(2,1)}, bf16[4,1024,2048]{2,1,0:T(8,128)(2,1)}, bf16[4,1024,2048]{2,1,0:T(8,128)(2,1)}, f32[8,128]{1,0:T(8,128...) custom-call(s32[2]{0:T(128)} %pad_add_fusion.refs_0_.s_ref, ...), custom_call_target="tpu_custom_call", output_to_operand_aliasing={{0}: (10, {}), {1}: (11, {}), {2}: (12, {}), {4}: (13, {})} | custom-call | tf_op jit(solution)/shard_map/pallas_call | solution.py:339
  212.6 27.9 %shard_map.120 = (bf16[4,1024,1024]{2,1,0:T(8,128)(2,1)}, bf16[4,1024,2048]{2,1,0:T(8,128)(2,1)}, bf16[4,1024,2048]{2,1,0:T(8,128)(2,1)}, f32[8,128]{1,0:T(8,128...) custom-call(s32[2]{0:T(128)} %pad_add_fusion.refs_0_.s_ref, ...), custom_call_target="tpu_custom_call" | custom-call | tf_op jit(solution)/shard_map/pallas_call | solution.py:339
  240.5 28.1 %shard_map.121 = (bf16[4,1024,1024]{2,1,0:T(8,128)(2,1)}, bf16[4,1024,2048]{2,1,0:T(8,128)(2,1)}, bf16[4,1024,2048]{2,1,0:T(8,128)(2,1)}, f32[8,128]{1,0:T(8,128...) custom-call(s32[2]{0:T(128)} %pad_add_fusion.refs_0_.s_ref, ...), custom_call_target="tpu_custom_call", output_to_operand_aliasing={{0}: (12, {}), {1}: (13, {}), {2}: (14, {}), {4}: (15, {}),... | custom-call | tf_op jit(solution)/shard_map/pallas_call | solution.py:339
  273.2 27.9 %shard_map.122 = (bf16[4,1024,1024]{2,1,0:T(8,128)(2,1)}, bf16[4,1024,2048]{2,1,0:T(8,128)(2,1)}, bf16[4,1024,2048]{2,1,0:T(8,128)(2,1)}, f32[8,128]{1,0:T(8,128...) custom-call(s32[2]{0:T(128)} %pad_add_fusion.refs_0_.s_ref, ...), custom_call_target="tpu_custom_call", output_to_operand_aliasing={{0}: (12, {}), {1}: (13, {}), {2}: (14, {}), {4}: (15, {})} | custom-call | tf_op jit(solution)/shard_map/pallas_call | solution.py:339
  331.3 45.0 %collective-permute-done.4.refs_3_ = bf16[1024,1024]{1,0:T(8,128)(2,1)} collective-permute-done((bf16[1024,1024]{1,0:T(8,128)(2,1)}, bf16[1024,1024]{1,0:T(8,128)(2,1)}, u32[]{:S(2)}, u32[]{:S(2)}) %collective-permute-start.4) | collective-permute-done | bytes 2097184 | tf_op jit(solution)/shard_map/ppermute | solution.py:706
  378.1 28.1 %shard_map.124 = (bf16[4,1024,1024]{2,1,0:T(8,128)(2,1)}, bf16[4,1024,2048]{2,1,0:T(8,128)(2,1)}, bf16[4,1024,2048]{2,1,0:T(8,128)(2,1)}, f32[8,128]{1,0:T(8,128...) custom-call(s32[2]{0:T(128)} %pad_add_fusion.refs_0_.s_ref, ...), custom_call_target="tpu_custom_call", output_to_operand_aliasing={{0}: (12, {}), {1}: (13, {}), {2}: (14, {}), {4}: (15, {})} | custom-call | tf_op jit(solution)/shard_map/pallas_call | solution.py:339
  433.4 28.6 %shard_map.126 = (bf16[4,1024,1024]{2,1,0:T(8,128)(2,1)}, bf16[4,1024,2048]{2,1,0:T(8,128)(2,1)}, bf16[4,1024,2048]{2,1,0:T(8,128)(2,1)}, f32[8,128]{1,0:T(8,128...) custom-call(s32[2]{0:T(128)} %pad_add_fusion.refs_0_.s_ref, ...), custom_call_target="tpu_custom_call" | custom-call | tf_op jit(solution)/shard_map/pallas_call | solution.py:339
  466.2 28.8 %shard_map.127 = (bf16[4,1024,1024]{2,1,0:T(8,128)(2,1)}, bf16[4,1024,2048]{2,1,0:T(8,128)(2,1)}, bf16[4,1024,2048]{2,1,0:T(8,128)(2,1)}, f32[8,128]{1,0:T(8,128...) custom-call(s32[2]{0:T(128)} %pad_add_fusion.refs_0_.s_ref, ...), custom_call_target="tpu_custom_call", output_to_operand_aliasing={{0}: (12, {}), {1}: (13, {}), {2}: (14, {}), {4}: (15, {}),... | custom-call | tf_op jit(solution)/shard_map/pallas_call | solution.py:339
  510.6 28.4 %shard_map.128 = (bf16[4,1024,1024]{2,1,0:T(8,128)(2,1)}, bf16[4,1024,2048]{2,1,0:T(8,128)(2,1)}, bf16[4,1024,2048]{2,1,0:T(8,128)(2,1)}, f32[8,128]{1,0:T(8,128...) custom-call(s32[2]{0:T(128)} %pad_add_fusion.refs_0_.s_ref, ...), custom_call_target="tpu_custom_call", output_to_operand_aliasing={{0}: (12, {}), {1}: (13, {}), {2}: (14, {}), {4}: (15, {})} | custom-call | tf_op jit(solution)/shard_map/pallas_call | solution.py:339
  570.7 46.8 %collective-permute-done.12.refs_3_ = bf16[1024,1024]{1,0:T(8,128)(2,1)} collective-permute-done((bf16[1024,1024]{1,0:T(8,128)(2,1)}, bf16[1024,1024]{1,0:T(8,128)(2,1)}, u32[]{:S(2)}, u32[]{:S(2)}) %collective-permute-start.12) | collective-permute-done | bytes 2097184 | tf_op jit(solution)/shard_map/ppermute | solution.py:706
  619.0 40.8 %collective-permute-done.26.refs_2_.refs_3_ = f32[2,512,1024]{2,1,0:T(8,128)} collective-permute-done((f32[2,512,1024]{2,1,0:T(8,128)}, f32[2,512,1024]{2,1,0:T(8,128)}, u32[]{:S(2)}, u32[]{:S(2)}) %collective-permute-start.26) | collective-permute-done | bytes 4194336 | tf_op jit(solution)/shard_map/ppermute | solution.py:713
  661.5 28.7 %shard_map.130 = (bf16[4,1024,1024]{2,1,0:T(8,128)(2,1)}, bf16[4,1024,2048]{2,1,0:T(8,128)(2,1)}, bf16[4,1024,2048]{2,1,0:T(8,128)(2,1)}, f32[8,128]{1,0:T(8,128...) custom-call(s32[2]{0:T(128)} %pad_add_fusion.refs_0_.s_ref, ...), custom_call_target="tpu_custom_call", output_to_operand_aliasing={{0}: (12, {}), {1}: (13, {}), {2}: (14, {}), {4}: (15, {})} | custom-call | tf_op jit(solution)/shard_map/pallas_call | solution.py:339
  698.2 27.8 %shard_map.132 = (f32[2,512,1024]{2,1,0:T(8,128)}, f32[2,512,1024]{2,1,0:T(8,128)}, f32[8,128]{1,0:T(8,128)}) custom-call(s32[2]{0:T(128)} %pad_add_fusion.refs_0_.s_ref, bf16[6,8,1024,1024]{3,2,1,0:T(8,128)(2,1)} %refs_1_.39, bf16[4,1024,2048]{2,1,0:T(8,128)(2,1)} %get-tuple-element.262.refs_2_, bf16[4,1024,2048]{2,1,0:T(8,128)(2,1)} %get-tuple-element.263.refs_3_, ...), custom_call_target="tpu_custom_call" | custom-call | tf_op jit(solution)/shard_map/pallas_call | solution.py:502
  726.0 29.0 %shard_map.133 = (bf16[4,1024,1024]{2,1,0:T(8,128)(2,1)}, bf16[4,1024,2048]{2,1,0:T(8,128)(2,1)}, bf16[4,1024,2048]{2,1,0:T(8,128)(2,1)}, f32[8,128]{1,0:T(8,128...) custom-call(s32[2]{0:T(128)} %pad_add_fusion.refs_0_.s_ref, ...), custom_call_target="tpu_custom_call" | custom-call | tf_op jit(solution)/shard_map/pallas_call | solution.py:339
  754.9 28.7 %shard_map.134 = (bf16[4,1024,1024]{2,1,0:T(8,128)(2,1)}, bf16[4,1024,2048]{2,1,0:T(8,128)(2,1)}, bf16[4,1024,2048]{2,1,0:T(8,128)(2,1)}, f32[8,128]{1,0:T(8,128...) custom-call(s32[2]{0:T(128)} %pad_add_fusion.refs_0_.s_ref, ...), custom_call_target="tpu_custom_call", output_to_operand_aliasing={{0}: (12, {}), {1}: (13, {}), {2}: (14, {}), {4}: (15, {}),... | custom-call | tf_op jit(solution)/shard_map/pallas_call | solution.py:339
  783.7 28.7 %shard_map.135 = (bf16[4,1024,1024]{2,1,0:T(8,128)(2,1)}, bf16[4,1024,2048]{2,1,0:T(8,128)(2,1)}, bf16[4,1024,2048]{2,1,0:T(8,128)(2,1)}, f32[8,128]{1,0:T(8,128...) custom-call(s32[2]{0:T(128)} %pad_add_fusion.refs_0_.s_ref, ...), custom_call_target="tpu_custom_call", output_to_operand_aliasing={{0}: (12, {}), {1}: (13, {}), {2}: (14, {}), {4}: (15, {})} | custom-call | tf_op jit(solution)/shard_map/pallas_call | solution.py:339
  843.8 46.8 %collective-permute-done.19.refs_3_ = bf16[1024,1024]{1,0:T(8,128)(2,1)} collective-permute-done((bf16[1024,1024]{1,0:T(8,128)(2,1)}, bf16[1024,1024]{1,0:T(8,128)(2,1)}, u32[]{:S(2)}, u32[]{:S(2)}) %collective-permute-start.19) | collective-permute-done | bytes 2097184 | tf_op jit(solution)/shard_map/ppermute | solution.py:706
  892.0 40.8 %collective-permute-done.34.refs_2_.refs_3_ = f32[2,512,1024]{2,1,0:T(8,128)} collective-permute-done((f32[2,512,1024]{2,1,0:T(8,128)}, f32[2,512,1024]{2,1,0:T(8,128)}, u32[]{:S(2)}, u32[]{:S(2)}) %collective-permute-start.34) | collective-permute-done | bytes 4194336 | tf_op jit(solution)/shard_map/ppermute | solution.py:713
  934.5 28.7 %shard_map.137 = (bf16[4,1024,1024]{2,1,0:T(8,128)(2,1)}, bf16[4,1024,2048]{2,1,0:T(8,128)(2,1)}, bf16[4,1024,2048]{2,1,0:T(8,128)(2,1)}, f32[8,128]{1,0:T(8,128...) custom-call(s32[2]{0:T(128)} %pad_add_fusion.refs_0_.s_ref, ...), custom_call_target="tpu_custom_call", output_to_operand_aliasing={{0}: (12, {}), {1}: (13, {}), {2}: (14, {}), {4}: (15, {})} | custom-call | tf_op jit(solution)/shard_map/pallas_call | solution.py:339
  970.6 27.7 %shard_map.139 = (f32[2,512,1024]{2,1,0:T(8,128)}, f32[2,512,1024]{2,1,0:T(8,128)}, f32[8,128]{1,0:T(8,128)}) custom-call(s32[2]{0:T(128)} %pad_add_fusion.refs_0_.s_ref, bf16[6,8,1024,1024]{3,2,1,0:T(8,128)(2,1)} %refs_1_.39, bf16[4,1024,2048]{2,1,0:T(8,128)(2,1)} %get-tuple-element.291.refs_2_, bf16[4,1024,2048]{2,1,0:T(8,128)(2,1)} %get-tuple-element.292.refs_3_, ...), custom_call_target="tpu_custom_call" | custom-call | tf_op jit(solution)/shard_map/pallas_call | solution.py:502
  998.3 28.2 %shard_map.140 = (bf16[4,1024,1024]{2,1,0:T(8,128)(2,1)}, bf16[4,1024,2048]{2,1,0:T(8,128)(2,1)}, bf16[4,1024,2048]{2,1,0:T(8,128)(2,1)}, f32[8,128]{1,0:T(8,128...) custom-call(s32[2]{0:T(128)} %pad_add_fusion.refs_0_.s_ref, ...), custom_call_target="tpu_custom_call" | custom-call | tf_op jit(solution)/shard_map/pallas_call | solution.py:339
  1026.6 28.0 %shard_map.141 = (bf16[4,1024,1024]{2,1,0:T(8,128)(2,1)}, bf16[4,1024,2048]{2,1,0:T(8,128)(2,1)}, bf16[4,1024,2048]{2,1,0:T(8,128)(2,1)}, f32[8,128]{1,0:T(8,128...) custom-call(s32[2]{0:T(128)} %pad_add_fusion.refs_0_.s_ref, ...), custom_call_target="tpu_custom_call", output_to_operand_aliasing={{0}: (12, {}), {1}: (13, {}), {2}: (14, {}), {4}: (15, {}),... | custom-call | tf_op jit(solution)/shard_map/pallas_call | solution.py:339
  1054.6 28.1 %shard_map.142 = (bf16[4,1024,1024]{2,1,0:T(8,128)(2,1)}, bf16[4,1024,2048]{2,1,0:T(8,128)(2,1)}, bf16[4,1024,2048]{2,1,0:T(8,128)(2,1)}, f32[8,128]{1,0:T(8,128...) custom-call(s32[2]{0:T(128)} %pad_add_fusion.refs_0_.s_ref, ...), custom_call_target="tpu_custom_call", output_to_operand_aliasing={{0}: (12, {}), {1}: (13, {}), {2}: (14, {}), {4}: (15, {})} | custom-call | tf_op jit(solution)/shard_map/pallas_call | solution.py:339
  1082.7 27.4 %shard_map.143 = (f32[2,1024,1024]{2,1,0:T(8,128)}, f32[8,128]{1,0:T(8,128)}) custom-call(s32[2]{0:T(128)} %pad_add_fusion.refs_0_.s_ref, bf16[6,8,1024,1024]{3,2,1,0:T(8,128)(2,1)} %refs_1_.39, bf16[4,1024,2048]{2,1,0:T(8,128)(2,1)} %get-tuple-element.323.refs_2_, bf16[4,1024,2048]{2,1,0:T(8,128)(2,1)} %get-tuple-element.324.refs_3_, ...), custom_call_target="tpu_custom_call" | custom-call | tf_op jit(solution)/shard_map/pallas_call | solution.py:502
  1112.0 46.5 %collective-permute-done.27.refs_3_ = bf16[1024,1024]{1,0:T(8,128)(2,1)} collective-permute-done((bf16[1024,1024]{1,0:T(8,128)(2,1)}, bf16[1024,1024]{1,0:T(8,128)(2,1)}, u32[]{:S(2)}, u32[]{:S(2)}) %collective-permute-start.27) | collective-permute-done | bytes 2097184 | tf_op jit(solution)/shard_map/ppermute | solution.py:706
  1158.5 27.8 %shard_map.144 = (bf16[4,1024,1024]{2,1,0:T(8,128)(2,1)}, bf16[4,1024,2048]{2,1,0:T(8,128)(2,1)}, bf16[4,1024,2048]{2,1,0:T(8,128)(2,1)}, f32[8,128]{1,0:T(8,128...) custom-call(s32[2]{0:T(128)} %pad_add_fusion.refs_0_.s_ref, ...), custom_call_target="tpu_custom_call", output_to_operand_aliasing={{0}: (12, {}), {1}: (13, {}), {2}: (14, {}), {4}: (15, {})} | custom-call | tf_op jit(solution)/shard_map/pallas_call | solution.py:339
  1188.0 27.5 %shard_map.145 = (f32[2,512,1024]{2,1,0:T(8,128)}, f32[2,512,1024]{2,1,0:T(8,128)}, f32[8,128]{1,0:T(8,128)}) custom-call(s32[2]{0:T(128)} %pad_add_fusion.refs_0_.s_ref, bf16[6,8,1024,1024]{3,2,1,0:T(8,128)(2,1)} %refs_1_.39, bf16[4,1024,2048]{2,1,0:T(8,128)(2,1)} %get-tuple-element.323.refs_2_, bf16[4,1024,2048]{2,1,0:T(8,128)(2,1)} %get-tuple-element.324.refs_3_, ...), custom_call_target="tpu_custom_call" | custom-call | tf_op jit(solution)/shard_map/pallas_call | solution.py:502
  1245.7 45.3 %collective-permute-done.43.refs_3_ = bf16[1024,1024]{1,0:T(8,128)(2,1)} collective-permute-done((bf16[1024,1024]{1,0:T(8,128)(2,1)}, bf16[1024,1024]{1,0:T(8,128)(2,1)}, u32[]{:S(2)}, u32[]{:S(2)}) %collective-permute-start.43) | collective-permute-done | bytes 2097184 | tf_op jit(solution)/shard_map/ppermute | solution.py:706
  1470.7 71.8 %collective-permute-done.46.refs_2_.refs_3_ = f32[2,512,1024]{2,1,0:T(8,128)} collective-permute-done((f32[2,512,1024]{2,1,0:T(8,128)}, f32[2,512,1024]{2,1,0:T(8,128)}, u32[]{:S(2)}, u32[]{:S(2)}) %collective-permute-start.46) | collective-permute-done | bytes 4194336 | tf_op jit(solution)/shard_map/ppermute | solution.py:713
  1586.0 46.3 %collective-permute-done.48.refs_2_.refs_3_ = f32[2,512,1024]{2,1,0:T(8,128)} collective-permute-done((f32[2,512,1024]{2,1,0:T(8,128)}, f32[2,512,1024]{2,1,0:T(8,128)}, u32[]{:S(2)}, u32[]{:S(2)}) %collective-permute-start.48) | collective-permute-done | bytes 4194336 | tf_op jit(solution)/shard_map/ppermute | solution.py:713
  1657.8 62.7 %collective-permute-done.49.refs_2_.refs_3_ = f32[2,512,1024]{2,1,0:T(8,128)} collective-permute-done((f32[2,512,1024]{2,1,0:T(8,128)}, f32[2,512,1024]{2,1,0:T(8,128)}, u32[]{:S(2)}, u32[]{:S(2)}) %collective-permute-start.49) | collective-permute-done | bytes 4194336 | tf_op jit(solution)/shard_map/ppermute | solution.py:713
  (121 shorter events, 611.2 us)
Async XLA Ops:
  14.9 91.3 %collective-permute-start = (bf16[3,1024,1024]{2,1,0:T(8,128)(2,1)}, bf16[3,1024,1024]{2,1,0:T(8,128)(2,1)}, u32[]{:S(2)}, u32[]{:S(2)}) collective-permute-start(bf16[3,1024,1024]{2,1,0:T(8,128)(2,1)} %get-tuple-element.210), channel_id=1, source_target_pairs={{0,1},{1,0},{2,3},{3,2},{4,5},{5,4},{6,7},{7,6}} | collective-permute-start | bytes 18874376 | tf_op jit(solution)/shard_map/ppermute | solution.py:700
  15.7 196.8 %collective-permute-start.6 = (bf16[6,1024,1024]{2,1,0:T(8,128)(2,1)}, bf16[6,1024,1024]{2,1,0:T(8,128)(2,1)}, u32[]{:S(2)}, u32[]{:S(2)}) collective-permute-start(bf16[6,1024,1024]{2,1,0:T(8,128)(2,1)} %refs_6_.56), channel_id=1, source_target_pairs={{0,1},{1,0},{2,3},{3,2},{4,5},{5,4},{6,7},{7,6}} | collective-permute-start | bytes 37748744 | tf_op jit(solution)/shard_map/ppermute | solution.py:702
  16.2 196.3 %collective-permute-start.7 = (bf16[6,1024,1024]{2,1,0:T(8,128)(2,1)}, bf16[6,1024,1024]{2,1,0:T(8,128)(2,1)}, u32[]{:S(2)}, u32[]{:S(2)}) collective-permute-start(bf16[6,1024,1024]{2,1,0:T(8,128)(2,1)} %refs_9_.31), channel_id=1, source_target_pairs={{0,1},{1,0},{2,3},{3,2},{4,5},{5,4},{6,7},{7,6}} | collective-permute-start | bytes 37748744 | tf_op jit(solution)/shard_map/ppermute | solution.py:702
  136.5 104.0 %collective-permute-start.10 = (bf16[1024,1024]{1,0:T(8,128)(2,1)}, bf16[1024,1024]{1,0:T(8,128)(2,1)}, u32[]{:S(2)}, u32[]{:S(2)}) collective-permute-start(bf16[1024,1024]{1,0:T(8,128)(2,1)} %get-tuple-element.239.refs_2_), channel_id=1, source_target_pairs={{0,2},{2,0},{1,3},{3,1},{4,6},{6,4},{5,7},{7,5}} | collective-permute-start | bytes 6291464 | tf_op jit(solution)/shard_map/ppermute | solution.py:706
  183.3 89.9 %collective-permute-start.9 = (bf16[1024,1024]{1,0:T(8,128)(2,1)}, bf16[1024,1024]{1,0:T(8,128)(2,1)}, u32[]{:S(2)}, u32[]{:S(2)}) collective-permute-start(bf16[1024,1024]{1,0:T(8,128)(2,1)} %get-tuple-element.238.refs_2_), channel_id=1, source_target_pairs={{0,2},{2,0},{1,3},{3,1},{4,6},{6,4},{5,7},{7,5}} | collective-permute-start | bytes 6291464 | tf_op jit(solution)/shard_map/ppermute | solution.py:706
  327.0 106.4 %collective-permute-start.13 = (bf16[4,1024,1024]{2,1,0:T(8,128)(2,1)}, bf16[4,1024,1024]{2,1,0:T(8,128)(2,1)}, u32[]{:S(2)}, u32[]{:S(2)}) collective-permute-start(bf16[4,1024,1024]{2,1,0:T(8,128)(2,1)} %get-tuple-element.261), channel_id=1, source_target_pairs={{0,1},{1,0},{2,3},{3,2},{4,5},{5,4},{6,7},{7,6}} | collective-permute-start | bytes 25165832 | tf_op jit(solution)/shard_map/ppermute | solution.py:700
  329.3 104.2 %collective-permute-start.17 = (bf16[1024,1024]{1,0:T(8,128)(2,1)}, bf16[1024,1024]{1,0:T(8,128)(2,1)}, u32[]{:S(2)}, u32[]{:S(2)}) collective-permute-start(bf16[1024,1024]{1,0:T(8,128)(2,1)} %get-tuple-element.267.refs_2_), channel_id=1, source_target_pairs={{0,2},{2,0},{1,3},{3,1},{4,6},{6,4},{5,7},{7,5}} | collective-permute-start | bytes 6291464 | tf_op jit(solution)/shard_map/ppermute | solution.py:706
  329.5 136.7 %collective-permute-start.16 = (bf16[1024,1024]{1,0:T(8,128)(2,1)}, bf16[1024,1024]{1,0:T(8,128)(2,1)}, u32[]{:S(2)}, u32[]{:S(2)}) collective-permute-start(bf16[1024,1024]{1,0:T(8,128)(2,1)} %get-tuple-element.266.refs_2_), channel_id=1, source_target_pairs={{0,2},{2,0},{1,3},{3,1},{4,6},{6,4},{5,7},{7,5}} | collective-permute-start | bytes 6291464 | tf_op jit(solution)/shard_map/ppermute | solution.py:706
  376.3 134.3 %collective-permute-start.15 = (bf16[1024,1024]{1,0:T(8,128)(2,1)}, bf16[1024,1024]{1,0:T(8,128)(2,1)}, u32[]{:S(2)}, u32[]{:S(2)}) collective-permute-start(bf16[1024,1024]{1,0:T(8,128)(2,1)} %get-tuple-element.265.refs_2_), channel_id=1, source_target_pairs={{0,2},{2,0},{1,3},{3,1},{4,6},{6,4},{5,7},{7,5}} | collective-permute-start | bytes 6291464 | tf_op jit(solution)/shard_map/ppermute | solution.py:706
  406.2 132.8 %collective-permute-start.14 = (f32[4,2,8,128]{3,2,1,0:T(8,128)}, f32[4,2,8,128]{3,2,1,0:T(8,128)}, u32[]{:S(2)}, u32[]{:S(2)}) collective-permute-start(f32[4,2,8,128]{3,2,1,0:T(8,128)} %get-tuple-element.264.refs_5_), channel_id=1, source_target_pairs={{0,2},{2,0},{1,3},{3,1},{4,6},{6,4},{5,7},{7,5}} | collective-permute-start | bytes 98312 | tf_op jit(solution)/shard_map/ppermute | solution.py:704
  566.4 123.8 %collective-permute-start.25 = (f32[2,1024,1024]{2,1,0:T(8,128)}, f32[2,1024,1024]{2,1,0:T(8,128)}, u32[]{:S(2)}, u32[]{:S(2)}) collective-permute-start(f32[2,1024,1024]{2,1,0:T(8,128)} %get-tuple-element.297), channel_id=1, source_target_pairs={{0,1},{1,0},{2,3},{3,2},{4,5},{5,4},{6,7},{7,6}} | collective-permute-start | bytes 25165832 | tf_op jit(solution)/shard_map/ppermute | solution.py:711
  566.4 159.5 %collective-permute-start.20 = (bf16[4,1024,1024]{2,1,0:T(8,128)(2,1)}, bf16[4,1024,1024]{2,1,0:T(8,128)(2,1)}, u32[]{:S(2)}, u32[]{:S(2)}) collective-permute-start(bf16[4,1024,1024]{2,1,0:T(8,128)(2,1)} %get-tuple-element.290), channel_id=1, source_target_pairs={{0,1},{1,0},{2,3},{3,2},{4,5},{5,4},{6,7},{7,6}} | collective-permute-start | bytes 25165832 | tf_op jit(solution)/shard_map/ppermute | solution.py:700
  566.9 92.9 %collective-permute-start.26 = (f32[2,512,1024]{2,1,0:T(8,128)}, f32[2,512,1024]{2,1,0:T(8,128)}, u32[]{:S(2)}, u32[]{:S(2)}) collective-permute-start(f32[2,512,1024]{2,1,0:T(8,128)} %get-tuple-element.299), channel_id=1, source_target_pairs={{0,4},{4,0},{1,5},{5,1},{2,6},{6,2},{3,7},{7,3}} | collective-permute-start | bytes 12582920 | tf_op jit(solution)/shard_map/ppermute | solution.py:713
  570.2 155.7 %collective-permute-start.24 = (bf16[1024,1024]{1,0:T(8,128)(2,1)}, bf16[1024,1024]{1,0:T(8,128)(2,1)}, u32[]{:S(2)}, u32[]{:S(2)}) collective-permute-start(bf16[1024,1024]{1,0:T(8,128)(2,1)} %get-tuple-element.296.refs_2_), channel_id=1, source_target_pairs={{0,2},{2,0},{1,3},{3,1},{4,6},{6,4},{5,7},{7,5}} | collective-permute-start | bytes 6291464 | tf_op jit(solution)/shard_map/ppermute | solution.py:706
  617.5 137.4 %collective-permute-start.23 = (bf16[1024,1024]{1,0:T(8,128)(2,1)}, bf16[1024,1024]{1,0:T(8,128)(2,1)}, u32[]{:S(2)}, u32[]{:S(2)}) collective-permute-start(bf16[1024,1024]{1,0:T(8,128)(2,1)} %get-tuple-element.295.refs_2_), channel_id=1, source_target_pairs={{0,2},{2,0},{1,3},{3,1},{4,6},{6,4},{5,7},{7,5}} | collective-permute-start | bytes 6291464 | tf_op jit(solution)/shard_map/ppermute | solution.py:706
  659.8 123.9 %collective-permute-start.22 = (bf16[1024,1024]{1,0:T(8,128)(2,1)}, bf16[1024,1024]{1,0:T(8,128)(2,1)}, u32[]{:S(2)}, u32[]{:S(2)}) collective-permute-start(bf16[1024,1024]{1,0:T(8,128)(2,1)} %get-tuple-element.294.refs_2_), channel_id=1, source_target_pairs={{0,2},{2,0},{1,3},{3,1},{4,6},{6,4},{5,7},{7,5}} | collective-permute-start | bytes 6291464 | tf_op jit(solution)/shard_map/ppermute | solution.py:706
  690.2 122.2 %collective-permute-start.21 = (f32[4,2,8,128]{3,2,1,0:T(8,128)}, f32[4,2,8,128]{3,2,1,0:T(8,128)}, u32[]{:S(2)}, u32[]{:S(2)}) collective-permute-start(f32[4,2,8,128]{3,2,1,0:T(8,128)} %get-tuple-element.293.refs_5_), channel_id=1, source_target_pairs={{0,2},{2,0},{1,3},{3,1},{4,6},{6,4},{5,7},{7,5}} | collective-permute-start | bytes 98312 | tf_op jit(solution)/shard_map/ppermute | solution.py:704
  839.5 123.8 %collective-permute-start.33 = (f32[2,1024,1024]{2,1,0:T(8,128)}, f32[2,1024,1024]{2,1,0:T(8,128)}, u32[]{:S(2)}, u32[]{:S(2)}) collective-permute-start(f32[2,1024,1024]{2,1,0:T(8,128)} %get-tuple-element.329), channel_id=1, source_target_pairs={{0,1},{1,0},{2,3},{3,2},{4,5},{5,4},{6,7},{7,6}} | collective-permute-start | bytes 25165832 | tf_op jit(solution)/shard_map/ppermute | solution.py:711
  839.5 158.8 %collective-permute-start.28 = (bf16[4,1024,1024]{2,1,0:T(8,128)(2,1)}, bf16[4,1024,1024]{2,1,0:T(8,128)(2,1)}, u32[]{:S(2)}, u32[]{:S(2)}) collective-permute-start(bf16[4,1024,1024]{2,1,0:T(8,128)(2,1)} %get-tuple-element.322), channel_id=1, source_target_pairs={{0,1},{1,0},{2,3},{3,2},{4,5},{5,4},{6,7},{7,6}} | collective-permute-start | bytes 25165832 | tf_op jit(solution)/shard_map/ppermute | solution.py:700
  840.0 92.8 %collective-permute-start.34 = (f32[2,512,1024]{2,1,0:T(8,128)}, f32[2,512,1024]{2,1,0:T(8,128)}, u32[]{:S(2)}, u32[]{:S(2)}) collective-permute-start(f32[2,512,1024]{2,1,0:T(8,128)} %get-tuple-element.331), channel_id=1, source_target_pairs={{0,4},{4,0},{1,5},{5,1},{2,6},{6,2},{3,7},{7,3}} | collective-permute-start | bytes 12582920 | tf_op jit(solution)/shard_map/ppermute | solution.py:713
  843.2 155.1 %collective-permute-start.32 = (bf16[1024,1024]{1,0:T(8,128)(2,1)}, bf16[1024,1024]{1,0:T(8,128)(2,1)}, u32[]{:S(2)}, u32[]{:S(2)}) collective-permute-start(bf16[1024,1024]{1,0:T(8,128)(2,1)} %get-tuple-element.328.refs_2_), channel_id=1, source_target_pairs={{0,2},{2,0},{1,3},{3,1},{4,6},{6,4},{5,7},{7,5}} | collective-permute-start | bytes 6291464 | tf_op jit(solution)/shard_map/ppermute | solution.py:706
  890.6 136.0 %collective-permute-start.31 = (bf16[1024,1024]{1,0:T(8,128)(2,1)}, bf16[1024,1024]{1,0:T(8,128)(2,1)}, u32[]{:S(2)}, u32[]{:S(2)}) collective-permute-start(bf16[1024,1024]{1,0:T(8,128)(2,1)} %get-tuple-element.327.refs_2_), channel_id=1, source_target_pairs={{0,2},{2,0},{1,3},{3,1},{4,6},{6,4},{5,7},{7,5}} | collective-permute-start | bytes 6291464 | tf_op jit(solution)/shard_map/ppermute | solution.py:706
  932.8 121.8 %collective-permute-start.30 = (bf16[1024,1024]{1,0:T(8,128)(2,1)}, bf16[1024,1024]{1,0:T(8,128)(2,1)}, u32[]{:S(2)}, u32[]{:S(2)}) collective-permute-start(bf16[1024,1024]{1,0:T(8,128)(2,1)} %get-tuple-element.326.refs_2_), channel_id=1, source_target_pairs={{0,2},{2,0},{1,3},{3,1},{4,6},{6,4},{5,7},{7,5}} | collective-permute-start | bytes 6291464 | tf_op jit(solution)/shard_map/ppermute | solution.py:706
  963.2 119.4 %collective-permute-start.29 = (f32[4,2,8,128]{3,2,1,0:T(8,128)}, f32[4,2,8,128]{3,2,1,0:T(8,128)}, u32[]{:S(2)}, u32[]{:S(2)}) collective-permute-start(f32[4,2,8,128]{3,2,1,0:T(8,128)} %get-tuple-element.325.refs_5_), channel_id=1, source_target_pairs={{0,2},{2,0},{1,3},{3,1},{4,6},{6,4},{5,7},{7,5}} | collective-permute-start | bytes 98312 | tf_op jit(solution)/shard_map/ppermute | solution.py:704
  1111.8 179.5 %collective-permute-start.36 = (bf16[4,1024,1024]{2,1,0:T(8,128)(2,1)}, bf16[4,1024,1024]{2,1,0:T(8,128)(2,1)}, u32[]{:S(2)}, u32[]{:S(2)}) collective-permute-start(bf16[4,1024,1024]{2,1,0:T(8,128)(2,1)} %get-tuple-element.356), channel_id=1, source_target_pairs={{0,1},{1,0},{2,3},{3,2},{4,5},{5,4},{6,7},{7,6}} | collective-permute-start | bytes 25165832 | tf_op jit(solution)/shard_map/ppermute | solution.py:700
  1242.5 161.5 %collective-permute-start.37 = (f32[2,512,1024]{2,1,0:T(8,128)}, f32[2,512,1024]{2,1,0:T(8,128)}, u32[]{:S(2)}, u32[]{:S(2)}) collective-permute-start(f32[2,512,1024]{2,1,0:T(8,128)} %get-tuple-element.358), channel_id=1, source_target_pairs={{0,4},{4,0},{1,5},{5,1},{2,6},{6,2},{3,7},{7,3}} | collective-permute-start | bytes 12582920 | tf_op jit(solution)/shard_map/ppermute | solution.py:713
  1244.2 98.5 %collective-permute-start.39 = (bf16[1024,1024]{1,0:T(8,128)(2,1)}, bf16[1024,1024]{1,0:T(8,128)(2,1)}, u32[]{:S(2)}, u32[]{:S(2)}) collective-permute-start(bf16[1024,1024]{1,0:T(8,128)(2,1)} %get-tuple-element.360.refs_2_), channel_id=1, source_target_pairs={{0,2},{2,0},{1,3},{3,1},{4,6},{6,4},{5,7},{7,5}} | collective-permute-start | bytes 6291464 | tf_op jit(solution)/shard_map/ppermute | solution.py:706
  1290.9 89.9 %collective-permute-start.38 = (bf16[1024,1024]{1,0:T(8,128)(2,1)}, bf16[1024,1024]{1,0:T(8,128)(2,1)}, u32[]{:S(2)}, u32[]{:S(2)}) collective-permute-start(bf16[1024,1024]{1,0:T(8,128)(2,1)} %get-tuple-element.359.refs_2_), channel_id=1, source_target_pairs={{0,2},{2,0},{1,3},{3,1},{4,6},{6,4},{5,7},{7,5}} | collective-permute-start | bytes 6291464 | tf_op jit(solution)/shard_map/ppermute | solution.py:706
  1291.3 134.0 %collective-permute-start.35 = (bf16[1024,1024]{1,0:T(8,128)(2,1)}, bf16[1024,1024]{1,0:T(8,128)(2,1)}, u32[]{:S(2)}, u32[]{:S(2)}) collective-permute-start(bf16[1024,1024]{1,0:T(8,128)(2,1)} %get-tuple-element.355.refs_2_), channel_id=1, source_target_pairs={{0,2},{2,0},{1,3},{3,1},{4,6},{6,4},{5,7},{7,5}} | collective-permute-start | bytes 6291464 | tf_op jit(solution)/shard_map/ppermute | solution.py:706
  1448.7 93.8 %collective-permute-start.46 = (f32[2,512,1024]{2,1,0:T(8,128)}, f32[2,512,1024]{2,1,0:T(8,128)}, u32[]{:S(2)}, u32[]{:S(2)}) collective-permute-start(f32[2,512,1024]{2,1,0:T(8,128)} %get-tuple-element.396), channel_id=1, source_target_pairs={{0,4},{4,0},{1,5},{5,1},{2,6},{6,2},{3,7},{7,3}} | collective-permute-start | bytes 12582920 | tf_op jit(solution)/shard_map/ppermute | solution.py:713
  1469.2 163.1 %collective-permute-start.48 = (f32[2,512,1024]{2,1,0:T(8,128)}, f32[2,512,1024]{2,1,0:T(8,128)}, u32[]{:S(2)}, u32[]{:S(2)}) collective-permute-start(f32[2,512,1024]{2,1,0:T(8,128)} %get-tuple-element.404), channel_id=1, source_target_pairs={{0,4},{4,0},{1,5},{5,1},{2,6},{6,2},{3,7},{7,3}} | collective-permute-start | bytes 12582920 | tf_op jit(solution)/shard_map/ppermute | solution.py:713
  1584.1 136.4 %collective-permute-start.49 = (f32[2,512,1024]{2,1,0:T(8,128)}, f32[2,512,1024]{2,1,0:T(8,128)}, u32[]{:S(2)}, u32[]{:S(2)}) collective-permute-start(f32[2,512,1024]{2,1,0:T(8,128)} %get-tuple-element.410), channel_id=1, source_target_pairs={{0,4},{4,0},{1,5},{5,1},{2,6},{6,2},{3,7},{7,3}} | collective-permute-start | bytes 12582920 | tf_op jit(solution)/shard_map/ppermute | solution.py:713
  (20 other events, 968.5 us)

commit v4 on v2

--- a/solution.py
+++ b/solution.py
@@ -15,7 +15,6 @@
 E = 4
 TB = 512
 NB = T // TB
-KB = 512
 GB = 256
 F32 = jnp.float32
 BF16 = jnp.bfloat16
@@ -40,27 +39,51 @@
     return pl.ds(pl.multiple_of(i * size, size), size)
 
 
-def gram_norms(x_ref, dz_ref, dh_ref, h_ref):
-    def gram(ref, rows, cols):
-        return lax.dot_general(ref[rows, :], ref[cols, :], NT, preferred_element_type=F32)
-
-    def fold(p):
-        return jnp.sum(p.reshape(p.shape[0] // 8, 8, GB), axis=0)
-
+def gram(ref, rows, cols):
+    return lax.dot_general(ref[rows, :], ref[cols, :], NT, preferred_element_type=F32)
+
+
+def fold(p):
+    return jnp.sum(p.reshape(p.shape[0] // 8, 8, GB), axis=0)
+
+
+def ring_rows(k):
+    return slice(0, 2 * GB) if k == 3 else slice(k * GB, (k + 2) * GB)
+
+
+SINGLES = ((3, 3, 1.0), (2, 0, 2.0))
+
+
+def single_block(r, c):
+    return slice(r * GB, (r + 1) * GB), slice(c * GB, (c + 1) * GB)
+
+
+def gram_x_ring(k, x_ref, ring_ref):
+    ring_ref[k] = gram(x_ref, ring_rows(k), slice(k * GB, (k + 1) * GB))
+
+
+def gram_x_single(k, x_ref, single_ref):
+    single_ref[k] = gram(x_ref, *single_block(*SINGLES[k][:2]))
+
+
+def gram_norms(ring_ref, single_ref, dz_ref, dh_ref, h_ref):
     def ring(k, sums):
         at = jnp.where(k == 3, 0, k)
         w = jnp.where(k == 3, 2.0, 1.0)
         rows, cols = pl.ds(pl.multiple_of(at * GB, GB), 2 * GB), block(k, GB)
-        p1 = gram(x_ref, rows, cols) * gram(dh_ref, rows, cols)
+        p1 = ring_ref[k] * gram(dh_ref, rows, cols)
         p2 = gram(h_ref, rows, cols) * gram(dz_ref, rows, cols)
         return tuple(t + (w * fold(p[:GB]) + 2.0 * fold(p[GB:])) for t, p in zip(sums, (p1, p2)))
 
     n1, n2 = lax.fori_loop(0, 4, ring, (jnp.zeros((8, GB), F32), jnp.zeros((8, GB), F32)))
-    for r, c, w in ((3, 3, 1.0), (2, 0, 2.0)):
-        rows, cols = slice(r * GB, (r + 1) * GB), slice(c * GB, (c + 1) * GB)
-        n1 = n1 + w * fold(gram(x_ref, rows, cols) * gram(dh_ref, rows, cols))
+    for k, (r, c, w) in enumerate(SINGLES):
+        rows, cols = single_block(r, c)
+        n1 = n1 + w * fold(single_ref[k] * gram(dh_ref, rows, cols))
         n2 = n2 + w * fold(gram(h_ref, rows, cols) * gram(dz_ref, rows, cols))
     return jnp.sum(n1), jnp.sum(n2)
+
+
+GRAM_SCRATCH = (pltpu.VMEM((4, 2 * GB, GB), F32), pltpu.VMEM((2, GB, GB), F32))
 
 
 def store_norms(n_ref, tok_ref, n1, n2):
@@ -72,19 +95,20 @@
 NORM_SHAPE = jax.ShapeDtypeStruct((E, 2, 8, 128), F32)
 
 
-def norm_spec(ex):
-    return pl.BlockSpec((None, 2, 8, 128), lambda *_: (ex, 0, 0, 0))
-
-
-def chain_call(layer, ex, first, last, norms, scal, dz_prev, part_own, part_recv, u_all, u_recv, x_all, w_down, w_down_r, w_up, w_up_r, bufs, norm_buf, pack_buf, dep):
-    packs = not last and ex < 2
-    at_u = ex if u_recv.shape[0] == E else (ex - 1 if u_recv.shape[0] > 1 else 0)
+def norm_spec(exs):
+    if len(exs) == 1:
+        return pl.BlockSpec((None, 2, 8, 128), lambda *_: (exs[0], 0, 0, 0))
+    return pl.BlockSpec((len(exs), 2, 8, 128), lambda *_: (exs[0] // len(exs), 0, 0, 0))
+
+
+def chain_call(layer, exs, blocks, first, last, norms, packs, apart, scal, dz_prev, sources, u_all, u_recv, x_all, w_down, w_down_r, w_up, w_up_r, bufs, norm_buf, pack_buf, dep):
     at_w = layer if w_down_r.shape[0] > 1 else 0
     names = ["scal", "dz"]
     args = [scal, dz_prev]
     if not first:
-        names += ["po", "pr"]
-        args += [part_own, part_recv]
+        for k, own, received in sorted({v[0]: v[:3] for v in sources.values()}.values(), key=lambda v: v[0]):
+            names += [f"po{k}", f"pr{k}"]
+            args += [own, received]
     names += ["uo", "ur", "w2o", "w2r"]
     args += [u_all, u_recv, w_down, w_down_r]
     if norms:
@@ -111,10 +135,12 @@
             args.append(norm_buf)
         out_names.append("n_out")
         out_shape.append(NORM_SHAPE)
-        out_specs.append(norm_spec(ex))
-    if not last:
-        out_names.append("part_out")
-        out_shape.append(jax.ShapeDtypeStruct((T, D), BF16))
+        out_specs.append(norm_spec(exs))
+    parts = 0 if last else (len(exs) if apart else 1)
+    for k in range(parts):
+        out_names.append(f"part{k}")
+        rows = (len(blocks) * TB, D)
+        out_shape.append(jax.ShapeDtypeStruct(rows if len(exs) == 1 or apart else (len(exs), *rows), BF16))
         out_specs.append(ANY)
     if packs:
         if pack_buf is not None:
@@ -126,124 +152,144 @@
         out_specs.append(ANY)
     scratch = {
         "dzp": pltpu.VMEM((T, D), BF16), "po_s": pltpu.VMEM((T, D), BF16), "pr_s": pltpu.VMEM((T, D), BF16),
-        "u_s": pltpu.VMEM((2, T, Q), BF16), "x_s": pltpu.VMEM((T, D), BF16), "w2_s": pltpu.VMEM((2 * Q, D), BF16), "w1_s": pltpu.VMEM((2, D, Q), BF16),
+        "u_s": pltpu.VMEM((2, T, Q), BF16), "x_s": pltpu.VMEM((len(exs), T, D), BF16), "w2_s": pltpu.VMEM((2 * Q, D), BF16), "w1_s": pltpu.VMEM((2, D, Q), BF16),
         "dz_s": pltpu.VMEM((T, D), BF16), "dh_s": pltpu.VMEM((T, 2 * Q), BF16), "h_s": pltpu.VMEM((T, 2 * Q), BF16), "part_s": pltpu.VMEM((T, D), BF16),
-        "in_sem": pltpu.SemaphoreType.DMA((NB, 5)), "w_sem": pltpu.SemaphoreType.DMA((5,)), "out_sem": pltpu.SemaphoreType.DMA((NB, 4)),
-        "pk_s": pltpu.VMEM((2, T, Q), BF16), "pk_sem": pltpu.SemaphoreType.DMA((2, 2)),
+        "ring_s": GRAM_SCRATCH[0], "single_s": GRAM_SCRATCH[1],
+        "in_sem": pltpu.SemaphoreType.DMA((NB, 5)), "w_sem": pltpu.SemaphoreType.DMA((4,)), "out_sem": pltpu.SemaphoreType.DMA((NB, 4)),
+        "x_sem": pltpu.SemaphoreType.DMA((len(exs),)), "pk_s": pltpu.VMEM((2, T, Q), BF16), "pk_sem": pltpu.SemaphoreType.DMA((2, 2)),
     }
 
     def body(*refs):
         r = dict(zip(names + out_names + list(scratch), refs))
-        here = r["scal"][0] * E + ex
         in_sem, w_sem, out_sem = r["in_sem"], r["w_sem"], r["out_sem"]
-        dz_src = r["dz"].at[here] if first else r["dz"].at[ex]
-
-        def inputs(i):
-            rows = block(i, TB)
+        core0 = r["scal"][0] * E
+
+        def inputs(ex, i):
+            rows = pl.ds(i * TB, TB)
+            at_u = ex if u_recv.shape[0] == E else (ex - 1 if u_recv.shape[0] > 1 else 0)
+            dz_src = r["dz"].at[core0 + ex] if first else r["dz"].at[ex]
             copies = [pltpu.make_async_copy(dz_src.at[rows], r["dzp"].at[rows], in_sem.at[i, 0])]
             if not first:
+                k, _, _, index = sources[ex, i]
                 copies += [
-                    pltpu.make_async_copy(r["po"].at[rows], r["po_s"].at[rows], in_sem.at[i, 1]),
-                    pltpu.make_async_copy(r["pr"].at[rows], r["pr_s"].at[rows], in_sem.at[i, 2]),
+                    pltpu.make_async_copy(r[f"po{k}"].at[index], r["po_s"].at[rows], in_sem.at[i, 1]),
+                    pltpu.make_async_copy(r[f"pr{k}"].at[index], r["pr_s"].at[rows], in_sem.at[i, 2]),
                 ]
-            copies += [
-                pltpu.make_async_copy(r["uo"].at[layer, here, rows], r["u_s"].at[0, rows], in_sem.at[i, 3]),
+            return copies + [
+                pltpu.make_async_copy(r["uo"].at[layer, core0 + ex, rows], r["u_s"].at[0, rows], in_sem.at[i, 3]),
                 pltpu.make_async_copy(r["ur"].at[at_u, rows], r["u_s"].at[1, rows], in_sem.at[i, 4]),
             ]
-            return copies
-
-        def outputs(i):
+
+        def outputs(ex, i):
             rows = block(i, TB)
-            return [
+            copies = [
                 pltpu.make_async_copy(r["dz_s"].at[rows], r["dz_out"].at[ex, rows], out_sem.at[i, 0]),
                 pltpu.make_async_copy(r["dh_s"].at[rows], r["dh_out"].at[ex, rows], out_sem.at[i, 1]),
                 pltpu.make_async_copy(r["h_s"].at[rows], r["h_out"].at[ex, rows], out_sem.at[i, 2]),
             ]
-
-        def part_output(i):
-            rows = block(i, TB)
-            return pltpu.make_async_copy(r["part_s"].at[rows], r["part_out"].at[rows], out_sem.at[i, 3])
+            if not last:
+                j = exs.index(ex)
+                out = r[f"part{j}"] if apart or len(exs) == 1 else r["part0"].at[j]
+                copies.append(pltpu.make_async_copy(r["part_s"].at[rows], out.at[block(i - blocks[0], TB)], out_sem.at[i, 3]))
+            return copies
 
         w2 = [
             pltpu.make_async_copy(r["w2o"].at[layer], r["w2_s"].at[pl.ds(0, Q)], w_sem.at[0]),
             pltpu.make_async_copy(r["w2r"].at[at_w], r["w2_s"].at[pl.ds(Q, Q)], w_sem.at[1]),
         ]
-        ins = inputs(0)
-        for c in ins[:-2] + [w2[0], ins[-2], w2[1], ins[-1]]:
-            c.start()
+        w1 = []
         if not last:
             w1 = [
                 pltpu.make_async_copy(r["w1o"].at[layer], r["w1_s"].at[0], w_sem.at[2]),
                 pltpu.make_async_copy(r["w1r"].at[at_w], r["w1_s"].at[1], w_sem.at[3]),
             ]
-            for c in w1:
-                c.start()
-        for i in range(1, NB):
-            for c in inputs(i):
-                c.start()
-        if norms:
-            x_copy = pltpu.make_async_copy(r["x"].at[layer, here], r["x_s"], w_sem.at[4])
-            x_copy.start()
+        x_copies = [pltpu.make_async_copy(r["x"].at[layer, core0 + ex], r["x_s"].at[j], r["x_sem"].at[j]) for j, ex in enumerate(exs)] if norms else []
+        pack_in, pack_out = [], []
         if packs:
             there = (1 - r["scal"][0]) * E
-            pack_in = [pltpu.make_async_copy(r["uo"].at[layer - 1, there + 2 * ex + j], r["pk_s"].at[j], r["pk_sem"].at[0, j]) for j in range(2)]
-            pack_out = [pltpu.make_async_copy(r["pk_s"].at[j], r["pack_out"].at[2 * ex + j], r["pk_sem"].at[1, j]) for j in range(2)]
-            for c in pack_in:
+            at = 2 * exs[0]
+            pack_in = [pltpu.make_async_copy(r["uo"].at[layer - 1, there + at + j], r["pk_s"].at[j], r["pk_sem"].at[0, j]) for j in range(2)]
+            pack_out = [pltpu.make_async_copy(r["pk_s"].at[j], r["pack_out"].at[at + j], r["pk_sem"].at[1, j]) for j in range(2)]
+
+        def wait_all(copies):
+            for c in copies:
+                c.wait()
+
+        def start_all(copies):
+            for c in copies:
                 c.start()
-        for c in w2:
-            c.wait()
-
-        def rows_step(i, carry):
-            rows = block(i, TB)
-            for c in inputs(i):
-                c.wait()
-            if first:
-                dz = r["dzp"][rows, :]
+
+        def back_chunk(rows, c):
+            cols, part = slice(c * 512, (c + 1) * 512), slice((c % 2) * 512, (c % 2 + 1) * 512)
+            back = lax.dot_general(r["dz_s"][rows, :], r["w2_s"][cols, :], NT, preferred_element_type=F32)
+            val, slope = gelu_pair(r["u_s"][c // 2, rows, part].astype(F32))
+            r["dh_s"][rows, cols] = (slope * back).astype(BF16)
+            r["h_s"][rows, cols] = val.astype(BF16)
+
+        def part_chunk(rows, c):
+            cols = slice(c * 512, (c + 1) * 512)
+            acc = lax.dot_general(r["dh_s"][rows, :Q], r["w1_s"][0, cols, :], NT, preferred_element_type=F32)
+            acc = acc + lax.dot_general(r["dh_s"][rows, Q:], r["w1_s"][1, cols, :], NT, preferred_element_type=F32)
+            r["part_s"][rows, cols] = acc.astype(BF16)
+
+        start_all(inputs(exs[0], blocks[0]) + w2)
+        for j, ex in enumerate(exs):
+            wait_all(inputs(ex, blocks[0]) + (w2 if j == 0 else []))
+            if j == 0:
+                start_all(w1)
+            start_all([c for i in blocks[1:] for c in inputs(ex, i)])
+            if norms and j == 0:
+                start_all(x_copies)
+            if j == 0:
+                start_all(pack_in)
+
+            def rows_step(i, carry):
+                rows = block(i, TB)
+                if len(blocks) > 1:
+
+                    @pl.when(i > blocks[0])
+                    def _():
+                        wait_all(inputs(ex, blocks[1]))
+
+                if first:
+                    r["dz_s"][rows, :] = r["dzp"][rows, :]
+                else:
+                    r["dz_s"][rows, :] = (r["dzp"][rows, :].astype(F32) + (r["po_s"][rows, :].astype(F32) + r["pr_s"][rows, :].astype(F32))).astype(BF16)
+                for c in range(4):
+                    back_chunk(rows, c)
+                if not last:
+                    if j == 0:
+
+                        @pl.when(i == blocks[0])
+                        def _():
+                            wait_all(w1)
+
+                    part_chunk(rows, 0)
+                    part_chunk(rows, 1)
+                start_all(outputs(ex, i))
+                return carry
+
+            lax.fori_loop(blocks[0], blocks[-1] + 1, rows_step, 0)
+            if j + 1 < len(exs):
+                start_all(inputs(exs[j + 1], blocks[0]))
+            if j == 0:
+                for p, q in zip(pack_in, pack_out):
+                    p.wait()
+                    q.start()
+            if norms:
+                x_copies[j].wait()
+                for k in range(4):
+                    gram_x_ring(k, r["x_s"].at[j], r["ring_s"])
+                for k in range(2):
+                    gram_x_single(k, r["x_s"].at[j], r["single_s"])
+                n_ref = r["n_out"] if len(exs) == 1 else r["n_out"].at[j]
+                store_norms(n_ref, r["tok"], *gram_norms(r["ring_s"], r["single_s"], r["dz_s"], r["dh_s"], r["h_s"]))
             else:
-                dz = (r["dzp"][rows, :].astype(F32) + (r["po_s"][rows, :].astype(F32) + r["pr_s"][rows, :].astype(F32))).astype(BF16)
-            r["dz_s"][rows, :] = dz
-            for c in range(4):
-                cols = slice(c * 512, (c + 1) * 512)
-                back = lax.dot_general(dz, r["w2_s"][cols, :], NT, preferred_element_type=F32)
-                val, slope = gelu_pair(r["u_s"][c // 2, rows, (c % 2) * 512:(c % 2 + 1) * 512].astype(F32))
-                r["dh_s"][rows, cols] = (slope * back).astype(BF16)
-                r["h_s"][rows, cols] = val.astype(BF16)
-            if not last:
-
-                @pl.when(i == 0)
-                def _():
-                    for c in w1:
-                        c.wait()
-
-                for c in range(2):
-                    cols = slice(c * 512, (c + 1) * 512)
-                    acc = lax.dot_general(r["dh_s"][rows, :Q], r["w1_s"][0, cols, :], NT, preferred_element_type=F32)
-                    acc = acc + lax.dot_general(r["dh_s"][rows, Q:], r["w1_s"][1, cols, :], NT, preferred_element_type=F32)
-                    r["part_s"][rows, cols] = acc.astype(BF16)
-            for c in outputs(i):
-                c.start()
-            if not last:
-                part_output(i).start()
-            return carry
-
-        lax.fori_loop(0, NB, rows_step, 0)
-        if packs:
-            for a, b in zip(pack_in, pack_out):
-                a.wait()
-                b.start()
-        if norms:
-            x_copy.wait()
-            store_norms(r["n_out"], r["tok"], *gram_norms(r["x_s"], r["dz_s"], r["dh_s"], r["h_s"]))
-        else:
-            r["tok"][...] = jnp.zeros((8, 128), F32)
-        for i in range(NB):
-            for c in outputs(i):
-                c.wait()
-            if not last:
-                part_output(i).wait()
-        if packs:
-            for b in pack_out:
-                b.wait()
+                r["tok"][...] = jnp.zeros((8, 128), F32)
+            for i in blocks:
+                wait_all(outputs(ex, i))
+            if j == 0:
+                wait_all(pack_out)
 
     outs = pl.pallas_call(
         body,
@@ -256,12 +302,16 @@
         grid=(1,),
     )(*args)
     named = dict(zip(out_names, outs))
-    return outs[:3], named.get("n_out", norm_buf), named.get("part_out"), named.get("pack_out", pack_buf), named["tok"]
+    return outs[:3], named.get("n_out", norm_buf), [named[f"part{k}"] for k in range(parts)], named.get("pack_out", pack_buf), named["tok"]
 
 
 def norm_call(layer, ex, scal, x_all, bufs, dep):
-    def body(s_ref, x_ref, dz_ref, dh_ref, h_ref, dep_ref, n_ref, tok_ref):
-        store_norms(n_ref, tok_ref, *gram_norms(x_ref, dz_ref, dh_ref, h_ref))
+    def body(s_ref, x_ref, dz_ref, dh_ref, h_ref, dep_ref, n_ref, tok_ref, ring_ref, single_ref):
+        for k in range(4):
+            gram_x_ring(k, x_ref, ring_ref)
+        for k in range(2):
+            gram_x_single(k, x_ref, single_ref)
+        store_norms(n_ref, tok_ref, *gram_norms(ring_ref, single_ref, dz_ref, dh_ref, h_ref))
 
     def at(width):
         return pl.BlockSpec((None, T, width), lambda i, s: (ex, 0, 0))
@@ -272,7 +322,7 @@
         grid_spec=pltpu.PrefetchScalarGridSpec(
             num_scalar_prefetch=1, grid=(1,),
             in_specs=[pl.BlockSpec((None, None, T, D), lambda i, s: (layer, s[0] * E + ex, 0, 0)), at(D), at(2 * Q), at(2 * Q), ANY],
-            out_specs=[norm_spec(ex), TOKEN_SPEC],
+            out_specs=[norm_spec((ex,)), TOKEN_SPEC], scratch_shapes=GRAM_SCRATCH,
         ),
         compiler_params=PARAMS,
     )(scal, x_all, *bufs, dep)
@@ -281,8 +331,7 @@
 def weight_call(layer, half, x_all, bufs, norms, norms_recv, clip_up, clip_down, scal, recv, dep):
     dz, dh, hid = bufs
     own = half == 0
-    steps = E * T // KB
-    per = T // KB
+    steps = E
 
     def body(*refs):
         refs = list(refs)
@@ -366,12 +415,12 @@
         def _():
             add(False, True)
 
-    norm_in = pl.BlockSpec((None, 2, 8, 128), lambda k, s: (k // per, 0, 0, 0))
+    norm_in = pl.BlockSpec((None, 2, 8, 128), lambda k, s: (k, 0, 0, 0))
     in_specs = [
-        pl.BlockSpec((None, None, KB, D), lambda k, s: (layer, s[0] * E + k // per, k % per, 0)),
-        pl.BlockSpec((None, KB, Q), lambda k, s: (k // per, k % per, half)),
-        pl.BlockSpec((None, KB, Q), lambda k, s: (k // per, k % per, half)),
-        pl.BlockSpec((None, KB, D), lambda k, s: (k // per, k % per, 0)),
+        pl.BlockSpec((None, None, T, D), lambda k, s: (layer, s[0] * E + k, 0, 0)),
+        pl.BlockSpec((None, T, Q), lambda k, s: (k, 0, half)),
+        pl.BlockSpec((None, T, Q), lambda k, s: (k, 0, half)),
+        pl.BlockSpec((None, T, D), lambda k, s: (k, 0, 0)),
         norm_in, norm_in, SMEM, SMEM,
     ]
     args = [x_all, dh, hid, dz, norms, norms_recv, clip_up, clip_down]
@@ -398,8 +447,7 @@
 def weight_piece_call(layer, half, at, x_all, bufs, norms, norms_recv, clip_up, clip_down, scal, recv, dep):
     dz, dh, hid = bufs
     own = half == 0
-    steps = E * T // KB
-    per = T // KB
+    steps = E
 
     def body(*refs):
         refs = list(refs)
@@ -445,13 +493,13 @@
     def d_half(s):
         return 1 - s[1] if at == 0 else s[1]
 
-    norm_in = pl.BlockSpec((None, 2, 8, 128), lambda k, s: (k // per, 0, 0, 0))
+    norm_in = pl.BlockSpec((None, 2, 8, 128), lambda k, s: (k, 0, 0, 0))
     piece = pl.BlockSpec((2, 512, 1024), lambda k, s: (0, 0, 0))
     in_specs = [
-        pl.BlockSpec((None, None, KB, 512), lambda k, s: (layer, s[0] * E + k // per, k % per, d_half(s))),
-        pl.BlockSpec((None, KB, Q), lambda k, s: (k // per, k % per, half)),
-        pl.BlockSpec((None, KB, Q), lambda k, s: (k // per, k % per, half)),
-        pl.BlockSpec((None, KB, 512), lambda k, s: (k // per, k % per, d_half(s))),
+        pl.BlockSpec((None, None, T, 512), lambda k, s: (layer, s[0] * E + k, 0, d_half(s))),
+        pl.BlockSpec((None, T, Q), lambda k, s: (k, 0, half)),
+        pl.BlockSpec((None, T, Q), lambda k, s: (k, 0, half)),
+        pl.BlockSpec((None, T, 512), lambda k, s: (k, 0, d_half(s))),
         norm_in, norm_in, SMEM, SMEM,
     ]
     args = [x_all, dh, hid, dz, norms, norms_recv, clip_up, clip_down]
@@ -528,18 +576,6 @@
     order = [("k", "pack", top, 0), ("p", "u", top, 0), ("p", "w", top, 0), ("p", "w", top, 1)]
     order += [("k", "pack", top, 1), ("p", "u", top, 1), ("p", "w", 0, 0), ("p", "w", 0, 1)]
 
-    def chain(layer, e):
-        steps = [("k", "chain", layer, e)]
-        if e == E - 1:
-            steps.append(("p", "n", layer, 0))
-        if layer > 0 and e != E - 2:
-            steps += [("p", "x", layer, k) for k in ((E - 2, E - 1) if e == E - 1 else (e,))]
-        if layer == top and e == 0:
-            steps.append(("k", "norm", layer, e))
-        if layer > 0 and e == 1:
-            steps.append(("p", "u", layer - 1, E))
-        return steps
-
     def give(layer):
         return [("k", "wgrad", layer, 1), ("p", "c", layer, 0)]
 
@@ -547,17 +583,30 @@
         return [("k", "wgrad", layer, 0), ("p", "y", layer, 0)]
 
     for layer in range(top, 0, -1):
-        order += chain(layer, 0) + chain(layer, 1) + chain(layer, 2)
+        if layer == top:
+            order += [("k", "chaina", layer, 0), ("p", "xa", layer, 0), ("k", "chainb", layer, 0), ("p", "xb", layer, 0), ("k", "norm", layer, 0)]
+        else:
+            order += [("k", "chain", layer, 0), ("p", "x", layer, 0)]
+        order.append(("k", "chain", layer, 1))
+        if layer > 1:
+            order.append(("p", "x", layer, 1))
+        order.append(("p", "u", layer - 1, E))
+        if layer == 1:
+            order.append(("k", "chain", 1, 2))
         if layer < top:
             order += give(layer + 1)
-        order += chain(layer, 3)
-        if layer + 2 <= top:
+        if layer > 1:
+            order += [("k", "pair", layer, 2), ("p", "n", layer, 0)]
+            order += [("p", "x", layer, 2)] if layer > 2 else [("p", "x", 2, 2), ("p", "x", 2, 3)]
+        else:
+            order += [("k", "chain", 1, 3), ("p", "n", 1, 0), ("p", "x", 1, 1), ("p", "x", 1, 2), ("p", "x", 1, 3)]
+        if 1 < layer < top - 1:
             order.append(("k", "final", layer + 2, 0))
         if layer < top:
             order += own(layer + 1)
-    order += chain(0, 0) + give(1) + chain(0, 1) + own(1) + chain(0, 2) + chain(0, 3) + [("k", "final", 2, 0)]
-    order += [("k", "piece1", 0, 0), ("p", "c", 0, 0), ("k", "piece1", 0, 1), ("p", "c", 0, 1)]
-    order += [("k", "piece0", 0, 0), ("p", "y", 0, 0), ("k", "piece0", 0, 1), ("k", "final", 1, 0), ("k", "final", 0, 0)]
+    order += give(1) + [("k", "chain", 0, 0)] + own(1) + [("k", "chain", 0, 1), ("k", "chain", 0, 2), ("k", "final", 3, 0), ("k", "chain", 0, 3), ("p", "n", 0, 0)]
+    order += [("k", "piece1", 0, 0), ("p", "c", 0, 0), ("k", "final", 2, 0), ("k", "piece0", 0, 0), ("p", "y", 0, 0)]
+    order += [("k", "piece1", 0, 1), ("p", "c", 0, 1), ("k", "final", 1, 0), ("k", "piece0", 0, 1), ("k", "final", 0, 0)]
     return order
 
 
@@ -588,8 +637,8 @@
                     w_recv[layer, k] = lax.ppermute(w_pack[k] if first else (w_down, w_up)[k], "tp", swap_core)
                 elif what == "n":
                     norms_recv[layer] = lax.ppermute(norms[layer], "tp", swap_x)
-                elif what == "x":
-                    part_recv[layer, k] = lax.ppermute(part[layer, k], "tp", swap_x)
+                elif what in ("x", "xa", "xb"):
+                    part_recv[layer, what, k] = lax.ppermute(part[layer, what, k], "tp", swap_x)
                 elif what == "c":
                     if last:
                         pieces[2, k] = lax.ppermute(pieces[1, k], "tp", swap_core)
@@ -602,14 +651,31 @@
                     packed[layer, k], w_pack[0], w_pack[1], tok = pack_call(layer, 0, 1, scal, u_stored, tok, (w_down, w_up))
                 else:
                     packed[layer, k], tok = pack_call(layer, 1, E - 1, scal, u_stored, tok)
-            elif what == "chain":
+            elif what in ("chain", "chaina", "chainb", "pair"):
                 w_at = top if first else 0
-                bufs[layer], norms[layer], part[layer, k], packed[layer - 1, E], tok = chain_call(
-                    layer, k, first, last, not (first and k == 0), scal,
-                    d_out if first else bufs[layer + 1][0], None if first else part[layer + 1, k], None if first else part_recv[layer + 1, k],
-                    u_stored, u_recv[layer, min(k, 1) if first else E], x_stored,
+                exs = (2, 3) if what == "pair" else (k,)
+                blocks = {"chaina": (0,), "chainb": (1,)}.get(what, (0, 1))
+                apart = what == "pair" and layer == 2
+                sources = {}
+                for e in exs:
+                    for i in range(NB):
+                        rows = pl.ds(i * TB, TB)
+                        if first:
+                            continue
+                        if (layer + 1, "xa", e) in part:
+                            at, index = (layer + 1, ("xa", "xb")[i], e), pl.ds(0, TB)
+                        elif (layer + 1, "x", e) in part and part[layer + 1, "x", e].ndim == 2:
+                            at, index = (layer + 1, "x", e), rows
+                        else:
+                            at, index = (layer + 1, "x", 2), (e - 2, rows)
+                        sources[e, i] = (f"{at[1]}{at[2]}", part[at], part_recv[at], index)
+                bufs[layer], norms[layer], sent, packed[layer - 1, E], tok = chain_call(
+                    layer, exs, blocks, first, last, len(blocks) == NB, layer > 0 and k < 2 and what != "chainb", apart, scal,
+                    d_out if first else bufs[layer + 1][0], sources, u_stored, u_recv[layer, min(k, 1) if first else E], x_stored,
                     w_down, w_recv[w_at, 0], w_up, w_recv[w_at, 1], bufs.get(layer), norms.get(layer), packed.get((layer - 1, E)), tok,
                 )
+                for j, a in enumerate(sent):
+                    part[layer, {"chaina": "xa", "chainb": "xb"}.get(what, "x"), k + j] = a
             elif what == "norm":
                 norms[layer], tok = norm_call(layer, k, scal, x_stored, bufs[layer], tok)
             elif what == "wgrad":

time: 1690 us -> 1750 us (1.036)
  waiting for transfers between devices: 574 us -> 669 us
  Pallas kernels: 1060 us -> 1030 us
    ppermute x20 -> x18, waiting for transfers between devices: 291 us -> 432 us  [local_step(): part_recv[layer, what, k] = lax.ppermute(part[layer, what, k], 'tp', swap_x)]
    ppermute x6, waiting for transfers between devices: 229 us -> 182 us  [local_step(): y_recv[layer] = lax.ppermute(y_send[layer], 'dp', swap_dp)]
    pallas_call x24 -> x21, Pallas kernels: 646 us -> 628 us  [chain_call(): pl.pallas_call(body, out_shape=out_shape, in_specs=[SMEM] + [ANY] * (len(...]
  transfers between devices with their start and end apart: 50 -> 48, of which waited for: 18 -> 16; matrix products, arithmetic and copies ran while one was open for 0% -> 0% of each run, Pallas kernels for 53% -> 51%
where the time goes in v4:
time: 1750 us; the launch traced here: 1740 us
  Pallas kernels  1030 us (59%)
  waiting for transfers between devices  669 us (38%)
  starting transfers between devices  40.7 us (2%)
    pallas_call x21, Pallas kernels, chain_call(): pl.pallas_call(body, out_shape=out_shape, in_specs=[SMEM] + [ANY] * (len(...  628 us
    ppermute x18, waiting for transfers between devices, local_step(): part_recv[layer, what, k] = lax.ppermute(part[layer, what, k], 'tp', swap_x)  432 us
    pallas_call x10, Pallas kernels, weight_call(): pl.pallas_call(body, out_shape=out_shape, grid_spec=pltpu.PrefetchScalarG...  262 us
    ppermute x6, waiting for transfers between devices, local_step(): y_recv[layer] = lax.ppermute(y_send[layer], 'dp', swap_dp)  182 us
    pallas_call x4, Pallas kernels, weight_piece_call(): pl.pallas_call(body, out_shape=[jax.ShapeDtypeStruct((2, 512, 1024), F32)...  68.8 us
    ppermute x4, waiting for transfers between devices, local_step(): lax.ppermute(w_pack[k] if first else (w_down, w_up)[k], 'tp', swap_core)  50.7 us
    pallas_call x6, Pallas kernels, final_call(): pl.pallas_call(body, out_shape=[jax.ShapeDtypeStruct((num_layers, 512, 10...  41.9 us
  transfers between devices with their start and end apart: 48, of which 16 were waited for; matrix products, arithmetic and copies ran while one was open for 0% of the time, Pallas kernels for 51%

profile of v4, /device:TPU:0, one launch (start us, length us, event | category | flops | bytes accessed | tf_op | source)
XLA Modules:
  0.0 1743.6 jit_solution(10986521727874075695)
XLA Ops:
  29.2 38.6 %collective-permute-done.2.refs_7_.refs_8_ = bf16[1,1024,1024]{2,1,0:T(8,128)(2,1)} collective-permute-done((bf16[1,1024,1024]{2,1,0:T(8,128)(2,1)}, bf16[1,1024,1024]{2,1,0:T(8,128)(2,1)}, u32[]{:S(2)}, u32[]{:S(2)}) %collective-permute-start.2) | collective-permute-done | bytes 2097184 | tf_op jit(solution)/shard_map/ppermute | solution.py:637
  112.0 27.1 %shard_map.118 = (bf16[4,1024,1024]{2,1,0:T(8,128)(2,1)}, bf16[4,1024,2048]{2,1,0:T(8,128)(2,1)}, bf16[4,1024,2048]{2,1,0:T(8,128)(2,1)}, f32[8,128]{1,0:T(8,128...) custom-call(s32[2]{0:T(128)} %pad_add_fusion.refs_0_.s_ref, ...), custom_call_target="tpu_custom_call", output_to_operand_aliasing={{0}: (10, {}), {1}: (11, {}), {2}: (12, {}), {4}: (13, {}),... | custom-call | tf_op jit(solution)/shard_map/pallas_call | solution.py:294
  168.5 49.7 %shard_map.119 = (bf16[4,1024,1024]{2,1,0:T(8,128)(2,1)}, bf16[4,1024,2048]{2,1,0:T(8,128)(2,1)}, bf16[4,1024,2048]{2,1,0:T(8,128)(2,1)}, f32[8,128]{1,0:T(8,128...) custom-call(s32[2]{0:T(128)} %pad_add_fusion.refs_0_.s_ref, ...), custom_call_target="tpu_custom_call", output_to_operand_aliasing={{0}: (10, {}), {1}: (11, {}), {2}: (12, {}), {4}: (13, {})} | custom-call | tf_op jit(solution)/shard_map/pallas_call | solution.py:294
  235.4 28.0 %shard_map.120 = (bf16[4,1024,1024]{2,1,0:T(8,128)(2,1)}, bf16[4,1024,2048]{2,1,0:T(8,128)(2,1)}, bf16[4,1024,2048]{2,1,0:T(8,128)(2,1)}, f32[8,128]{1,0:T(8,128...) custom-call(s32[2]{0:T(128)} %pad_add_fusion.refs_0_.s_ref, ...), custom_call_target="tpu_custom_call" | custom-call | tf_op jit(solution)/shard_map/pallas_call | solution.py:294
  263.4 28.3 %shard_map.121 = (bf16[4,1024,1024]{2,1,0:T(8,128)(2,1)}, bf16[4,1024,2048]{2,1,0:T(8,128)(2,1)}, bf16[4,1024,2048]{2,1,0:T(8,128)(2,1)}, f32[8,128]{1,0:T(8,128...) custom-call(s32[2]{0:T(128)} %pad_add_fusion.refs_0_.s_ref, ...), custom_call_target="tpu_custom_call", output_to_operand_aliasing={{0}: (12, {}), {1}: (13, {}), {2}: (14, {}), {4}: (15, {}),... | custom-call | tf_op jit(solution)/shard_map/pallas_call | solution.py:294
  291.7 25.8 %shard_map.122 = (f32[2,1024,1024]{2,1,0:T(8,128)}, f32[8,128]{1,0:T(8,128)}) custom-call(s32[2]{0:T(128)} %pad_add_fusion.refs_0_.s_ref, bf16[6,8,1024,1024]{3,2,1,0:T(8,128)(2,1)} %refs_1_.39, bf16[4,1024,2048]{2,1,0:T(8,128)(2,1)} %get-tuple-element.216.refs_2_, bf16[4,1024,2048]{2,1,0:T(8,128)(2,1)} %get-tuple-element.217.refs_3_, ...), custom_call_target="tpu_custom_call" | custom-call | tf_op jit(solution)/shard_map/pallas_call | solution.py:437
  320.4 91.4 %collective-permute-done.4.refs_3_ = bf16[2,1024,1024]{2,1,0:T(8,128)(2,1)} collective-permute-done((bf16[2,1024,1024]{2,1,0:T(8,128)(2,1)}, bf16[2,1024,1024]{2,1,0:T(8,128)(2,1)}, u32[]{:S(2)}, u32[]{:S(2)}) %collective-permute-start.4) | collective-permute-done | bytes 4194336 | tf_op jit(solution)/shard_map/ppermute | solution.py:641
  411.8 50.5 %shard_map.123 = (bf16[4,1024,1024]{2,1,0:T(8,128)(2,1)}, bf16[4,1024,2048]{2,1,0:T(8,128)(2,1)}, bf16[4,1024,2048]{2,1,0:T(8,128)(2,1)}, f32[8,128]{1,0:T(8,128...) custom-call(s32[2]{0:T(128)} %pad_add_fusion.refs_0_.s_ref, ...), custom_call_target="tpu_custom_call", output_to_operand_aliasing={{0}: (12, {}), {1}: (13, {}), {2}: (14, {}), {4}: (15, {})} | custom-call | tf_op jit(solution)/shard_map/pallas_call | solution.py:294
  462.7 26.6 %shard_map.124 = (f32[2,512,1024]{2,1,0:T(8,128)}, f32[2,512,1024]{2,1,0:T(8,128)}, f32[8,128]{1,0:T(8,128)}) custom-call(s32[2]{0:T(128)} %pad_add_fusion.refs_0_.s_ref, bf16[6,8,1024,1024]{3,2,1,0:T(8,128)(2,1)} %refs_1_.39, bf16[4,1024,2048]{2,1,0:T(8,128)(2,1)} %get-tuple-element.216.refs_2_, bf16[4,1024,2048]{2,1,0:T(8,128)(2,1)} %get-tuple-element.217.refs_3_, ...), custom_call_target="tpu_custom_call" | custom-call | tf_op jit(solution)/shard_map/pallas_call | solution.py:437
  489.3 28.0 %shard_map.125 = (bf16[4,1024,1024]{2,1,0:T(8,128)(2,1)}, bf16[4,1024,2048]{2,1,0:T(8,128)(2,1)}, bf16[4,1024,2048]{2,1,0:T(8,128)(2,1)}, f32[8,128]{1,0:T(8,128...) custom-call(s32[2]{0:T(128)} %pad_add_fusion.refs_0_.s_ref, ...), custom_call_target="tpu_custom_call" | custom-call | tf_op jit(solution)/shard_map/pallas_call | solution.py:294
  517.3 28.2 %shard_map.126 = (bf16[4,1024,1024]{2,1,0:T(8,128)(2,1)}, bf16[4,1024,2048]{2,1,0:T(8,128)(2,1)}, bf16[4,1024,2048]{2,1,0:T(8,128)(2,1)}, f32[8,128]{1,0:T(8,128...) custom-call(s32[2]{0:T(128)} %pad_add_fusion.refs_0_.s_ref, ...), custom_call_target="tpu_custom_call", output_to_operand_aliasing={{0}: (12, {}), {1}: (13, {}), {2}: (14, {}), {4}: (15, {}),... | custom-call | tf_op jit(solution)/shard_map/pallas_call | solution.py:294
  575.6 89.9 %collective-permute-done.12.refs_3_ = bf16[2,1024,1024]{2,1,0:T(8,128)(2,1)} collective-permute-done((bf16[2,1024,1024]{2,1,0:T(8,128)(2,1)}, bf16[2,1024,1024]{2,1,0:T(8,128)(2,1)}, u32[]{:S(2)}, u32[]{:S(2)}) %collective-permute-start.12) | collective-permute-done | bytes 4194336 | tf_op jit(solution)/shard_map/ppermute | solution.py:641
  667.3 50.6 %shard_map.128 = (bf16[4,1024,1024]{2,1,0:T(8,128)(2,1)}, bf16[4,1024,2048]{2,1,0:T(8,128)(2,1)}, bf16[4,1024,2048]{2,1,0:T(8,128)(2,1)}, f32[8,128]{1,0:T(8,128...) custom-call(s32[2]{0:T(128)} %pad_add_fusion.refs_0_.s_ref, ...), custom_call_target="tpu_custom_call", output_to_operand_aliasing={{0}: (12, {}), {1}: (13, {}), {2}: (14, {}), {4}: (15, {})} | custom-call | tf_op jit(solution)/shard_map/pallas_call | solution.py:294
  725.8 26.5 %shard_map.130 = (f32[2,512,1024]{2,1,0:T(8,128)}, f32[2,512,1024]{2,1,0:T(8,128)}, f32[8,128]{1,0:T(8,128)}) custom-call(s32[2]{0:T(128)} %pad_add_fusion.refs_0_.s_ref, bf16[6,8,1024,1024]{3,2,1,0:T(8,128)(2,1)} %refs_1_.39, bf16[4,1024,2048]{2,1,0:T(8,128)(2,1)} %get-tuple-element.238.refs_2_, bf16[4,1024,2048]{2,1,0:T(8,128)(2,1)} %get-tuple-element.239.refs_3_, ...), custom_call_target="tpu_custom_call" | custom-call | tf_op jit(solution)/shard_map/pallas_call | solution.py:437
  752.4 28.0 %shard_map.131 = (bf16[4,1024,1024]{2,1,0:T(8,128)(2,1)}, bf16[4,1024,2048]{2,1,0:T(8,128)(2,1)}, bf16[4,1024,2048]{2,1,0:T(8,128)(2,1)}, f32[8,128]{1,0:T(8,128...) custom-call(s32[2]{0:T(128)} %pad_add_fusion.refs_0_.s_ref, ...), custom_call_target="tpu_custom_call" | custom-call | tf_op jit(solution)/shard_map/pallas_call | solution.py:294
  780.4 28.2 %shard_map.132 = (bf16[4,1024,1024]{2,1,0:T(8,128)(2,1)}, bf16[4,1024,2048]{2,1,0:T(8,128)(2,1)}, bf16[4,1024,2048]{2,1,0:T(8,128)(2,1)}, f32[8,128]{1,0:T(8,128...) custom-call(s32[2]{0:T(128)} %pad_add_fusion.refs_0_.s_ref, ...), custom_call_target="tpu_custom_call", output_to_operand_aliasing={{0}: (12, {}), {1}: (13, {}), {2}: (14, {}), {4}: (15, {}),... | custom-call | tf_op jit(solution)/shard_map/pallas_call | solution.py:294
  808.6 25.8 %shard_map.133 = (f32[2,1024,1024]{2,1,0:T(8,128)}, f32[8,128]{1,0:T(8,128)}) custom-call(s32[2]{0:T(128)} %pad_add_fusion.refs_0_.s_ref, bf16[6,8,1024,1024]{3,2,1,0:T(8,128)(2,1)} %refs_1_.39, bf16[4,1024,2048]{2,1,0:T(8,128)(2,1)} %get-tuple-element.261.refs_2_, bf16[4,1024,2048]{2,1,0:T(8,128)(2,1)} %get-tuple-element.262.refs_3_, ...), custom_call_target="tpu_custom_call" | custom-call | tf_op jit(solution)/shard_map/pallas_call | solution.py:437
  838.8 89.9 %collective-permute-done.18.refs_3_ = bf16[2,1024,1024]{2,1,0:T(8,128)(2,1)} collective-permute-done((bf16[2,1024,1024]{2,1,0:T(8,128)(2,1)}, bf16[2,1024,1024]{2,1,0:T(8,128)(2,1)}, u32[]{:S(2)}, u32[]{:S(2)}) %collective-permute-start.18) | collective-permute-done | bytes 4194336 | tf_op jit(solution)/shard_map/ppermute | solution.py:641
  930.4 50.5 %shard_map.134 = (bf16[4,1024,1024]{2,1,0:T(8,128)(2,1)}, bf16[4,1024,2048]{2,1,0:T(8,128)(2,1)}, bf16[4,1024,2048]{2,1,0:T(8,128)(2,1)}, f32[8,128]{1,0:T(8,128...) custom-call(s32[2]{0:T(128)} %pad_add_fusion.refs_0_.s_ref, ...), custom_call_target="tpu_custom_call", output_to_operand_aliasing={{0}: (12, {}), {1}: (13, {}), {2}: (14, {}), {4}: (15, {})} | custom-call | tf_op jit(solution)/shard_map/pallas_call | solution.py:294
  990.0 26.5 %shard_map.136 = (f32[2,512,1024]{2,1,0:T(8,128)}, f32[2,512,1024]{2,1,0:T(8,128)}, f32[8,128]{1,0:T(8,128)}) custom-call(s32[2]{0:T(128)} %pad_add_fusion.refs_0_.s_ref, bf16[6,8,1024,1024]{3,2,1,0:T(8,128)(2,1)} %refs_1_.39, bf16[4,1024,2048]{2,1,0:T(8,128)(2,1)} %get-tuple-element.261.refs_2_, bf16[4,1024,2048]{2,1,0:T(8,128)(2,1)} %get-tuple-element.262.refs_3_, ...), custom_call_target="tpu_custom_call" | custom-call | tf_op jit(solution)/shard_map/pallas_call | solution.py:437
  1016.5 28.0 %shard_map.137 = (bf16[4,1024,1024]{2,1,0:T(8,128)(2,1)}, bf16[4,1024,2048]{2,1,0:T(8,128)(2,1)}, bf16[4,1024,2048]{2,1,0:T(8,128)(2,1)}, f32[8,128]{1,0:T(8,128...) custom-call(s32[2]{0:T(128)} %pad_add_fusion.refs_0_.s_ref, ...), custom_call_target="tpu_custom_call" | custom-call | tf_op jit(solution)/shard_map/pallas_call | solution.py:294
  1044.6 28.2 %shard_map.138 = (bf16[4,1024,1024]{2,1,0:T(8,128)(2,1)}, bf16[4,1024,2048]{2,1,0:T(8,128)(2,1)}, bf16[4,1024,2048]{2,1,0:T(8,128)(2,1)}, f32[8,128]{1,0:T(8,128...) custom-call(s32[2]{0:T(128)} %pad_add_fusion.refs_0_.s_ref, ...), custom_call_target="tpu_custom_call", output_to_operand_aliasing={{0}: (12, {}), {1}: (13, {}), {2}: (14, {}), {4}: (15, {}),... | custom-call | tf_op jit(solution)/shard_map/pallas_call | solution.py:294
  1072.8 27.9 %shard_map.139 = (bf16[4,1024,1024]{2,1,0:T(8,128)(2,1)}, bf16[4,1024,2048]{2,1,0:T(8,128)(2,1)}, bf16[4,1024,2048]{2,1,0:T(8,128)(2,1)}, f32[8,128]{1,0:T(8,128...) custom-call(s32[2]{0:T(128)} %pad_add_fusion.refs_0_.s_ref, ...), custom_call_target="tpu_custom_call", output_to_operand_aliasing={{0}: (12, {}), {1}: (13, {}), {2}: (14, {}), {4}: (15, {})} | custom-call | tf_op jit(solution)/shard_map/pallas_call | solution.py:294
  1100.7 25.8 %shard_map.140 = (f32[2,1024,1024]{2,1,0:T(8,128)}, f32[8,128]{1,0:T(8,128)}) custom-call(s32[2]{0:T(128)} %pad_add_fusion.refs_0_.s_ref, bf16[6,8,1024,1024]{3,2,1,0:T(8,128)(2,1)} %refs_1_.39, bf16[4,1024,2048]{2,1,0:T(8,128)(2,1)} %get-tuple-element.287.refs_2_, bf16[4,1024,2048]{2,1,0:T(8,128)(2,1)} %get-tuple-element.288.refs_3_, ...), custom_call_target="tpu_custom_call" | custom-call | tf_op jit(solution)/shard_map/pallas_call | solution.py:437
  1127.1 47.8 %collective-permute-done.25.refs_3_ = bf16[1024,1024]{1,0:T(8,128)(2,1)} collective-permute-done((bf16[1024,1024]{1,0:T(8,128)(2,1)}, bf16[1024,1024]{1,0:T(8,128)(2,1)}, u32[]{:S(2)}, u32[]{:S(2)}) %collective-permute-start.25) | collective-permute-done | bytes 2097184 | tf_op jit(solution)/shard_map/ppermute | solution.py:641
  1174.9 28.1 %shard_map.141 = (bf16[4,1024,1024]{2,1,0:T(8,128)(2,1)}, bf16[4,1024,2048]{2,1,0:T(8,128)(2,1)}, bf16[4,1024,2048]{2,1,0:T(8,128)(2,1)}, f32[8,128]{1,0:T(8,128...) custom-call(s32[2]{0:T(128)} %pad_add_fusion.refs_0_.s_ref, ...), custom_call_target="tpu_custom_call", output_to_operand_aliasing={{0}: (12, {}), {1}: (13, {}), {2}: (14, {}), {4}: (15, {})} | custom-call | tf_op jit(solution)/shard_map/pallas_call | solution.py:294
  1203.3 26.5 %shard_map.142 = (f32[2,512,1024]{2,1,0:T(8,128)}, f32[2,512,1024]{2,1,0:T(8,128)}, f32[8,128]{1,0:T(8,128)}) custom-call(s32[2]{0:T(128)} %pad_add_fusion.refs_0_.s_ref, bf16[6,8,1024,1024]{3,2,1,0:T(8,128)(2,1)} %refs_1_.39, bf16[4,1024,2048]{2,1,0:T(8,128)(2,1)} %get-tuple-element.287.refs_2_, bf16[4,1024,2048]{2,1,0:T(8,128)(2,1)} %get-tuple-element.288.refs_3_, ...), custom_call_target="tpu_custom_call" | custom-call | tf_op jit(solution)/shard_map/pallas_call | solution.py:437
  1260.2 44.9 %collective-permute-done.41.refs_3_ = bf16[1024,1024]{1,0:T(8,128)(2,1)} collective-permute-done((bf16[1024,1024]{1,0:T(8,128)(2,1)}, bf16[1024,1024]{1,0:T(8,128)(2,1)}, u32[]{:S(2)}, u32[]{:S(2)}) %collective-permute-start.41) | collective-permute-done | bytes 2097184 | tf_op jit(solution)/shard_map/ppermute | solution.py:641
  1330.6 26.5 %shard_map.145 = (f32[2,512,1024]{2,1,0:T(8,128)}, f32[2,512,1024]{2,1,0:T(8,128)}, f32[8,128]{1,0:T(8,128)}) custom-call(s32[2]{0:T(128)} %pad_add_fusion.refs_0_.s_ref, bf16[6,8,1024,1024]{3,2,1,0:T(8,128)(2,1)} %refs_1_.39, bf16[4,1024,2048]{2,1,0:T(8,128)(2,1)} %get-tuple-element.325.refs_2_, bf16[4,1024,2048]{2,1,0:T(8,128)(2,1)} %get-tuple-element.326.refs_3_, ...), custom_call_target="tpu_custom_call" | custom-call | tf_op jit(solution)/shard_map/pallas_call | solution.py:437
  1485.3 72.7 %collective-permute-done.44.refs_2_.refs_3_ = f32[2,512,1024]{2,1,0:T(8,128)} collective-permute-done((f32[2,512,1024]{2,1,0:T(8,128)}, f32[2,512,1024]{2,1,0:T(8,128)}, u32[]{:S(2)}, u32[]{:S(2)}) %collective-permute-start.44) | collective-permute-done | bytes 4194336 | tf_op jit(solution)/shard_map/ppermute | solution.py:648
  1601.0 46.9 %collective-permute-done.46.refs_2_.refs_3_ = f32[2,512,1024]{2,1,0:T(8,128)} collective-permute-done((f32[2,512,1024]{2,1,0:T(8,128)}, f32[2,512,1024]{2,1,0:T(8,128)}, u32[]{:S(2)}, u32[]{:S(2)}) %collective-permute-start.46) | collective-permute-done | bytes 4194336 | tf_op jit(solution)/shard_map/ppermute | solution.py:648
  1673.3 62.8 %collective-permute-done.47.refs_2_.refs_3_ = f32[2,512,1024]{2,1,0:T(8,128)} collective-permute-done((f32[2,512,1024]{2,1,0:T(8,128)}, f32[2,512,1024]{2,1,0:T(8,128)}, u32[]{:S(2)}, u32[]{:S(2)}) %collective-permute-start.47) | collective-permute-done | bytes 4194336 | tf_op jit(solution)/shard_map/ppermute | solution.py:648
  (114 shorter events, 436.9 us)
Async XLA Ops:
  14.9 97.1 %collective-permute-start = (bf16[3,1024,1024]{2,1,0:T(8,128)(2,1)}, bf16[3,1024,1024]{2,1,0:T(8,128)(2,1)}, u32[]{:S(2)}, u32[]{:S(2)}) collective-permute-start(bf16[3,1024,1024]{2,1,0:T(8,128)(2,1)} %get-tuple-element.192), channel_id=1, source_target_pairs={{0,1},{1,0},{2,3},{3,2},{4,5},{5,4},{6,7},{7,6}} | collective-permute-start | bytes 18874376 | tf_op jit(solution)/shard_map/ppermute | solution.py:635
  15.7 219.6 %collective-permute-start.6 = (bf16[6,1024,1024]{2,1,0:T(8,128)(2,1)}, bf16[6,1024,1024]{2,1,0:T(8,128)(2,1)}, u32[]{:S(2)}, u32[]{:S(2)}) collective-permute-start(bf16[6,1024,1024]{2,1,0:T(8,128)(2,1)} %refs_6_.50), channel_id=1, source_target_pairs={{0,1},{1,0},{2,3},{3,2},{4,5},{5,4},{6,7},{7,6}} | collective-permute-start | bytes 37748744 | tf_op jit(solution)/shard_map/ppermute | solution.py:637
  16.3 219.1 %collective-permute-start.7 = (bf16[6,1024,1024]{2,1,0:T(8,128)(2,1)}, bf16[6,1024,1024]{2,1,0:T(8,128)(2,1)}, u32[]{:S(2)}, u32[]{:S(2)}) collective-permute-start(bf16[6,1024,1024]{2,1,0:T(8,128)(2,1)} %refs_9_.23), channel_id=1, source_target_pairs={{0,1},{1,0},{2,3},{3,2},{4,5},{5,4},{6,7},{7,6}} | collective-permute-start | bytes 37748744 | tf_op jit(solution)/shard_map/ppermute | solution.py:637
  139.2 96.2 %collective-permute-start.5 = (bf16[4,1024,1024]{2,1,0:T(8,128)(2,1)}, bf16[4,1024,1024]{2,1,0:T(8,128)(2,1)}, u32[]{:S(2)}, u32[]{:S(2)}) collective-permute-start(bf16[4,1024,1024]{2,1,0:T(8,128)(2,1)} %get-tuple-element.215), channel_id=1, source_target_pairs={{0,1},{1,0},{2,3},{3,2},{4,5},{5,4},{6,7},{7,6}} | collective-permute-start | bytes 25165832 | tf_op jit(solution)/shard_map/ppermute | solution.py:635
  142.2 121.2 %collective-permute-start.9 = (bf16[1024,1024]{1,0:T(8,128)(2,1)}, bf16[1024,1024]{1,0:T(8,128)(2,1)}, u32[]{:S(2)}, u32[]{:S(2)}) collective-permute-start(bf16[1024,1024]{1,0:T(8,128)(2,1)} %get-tuple-element.219.refs_2_), channel_id=1, source_target_pairs={{0,2},{2,0},{1,3},{3,1},{4,6},{6,4},{5,7},{7,5}} | collective-permute-start | bytes 6291464 | tf_op jit(solution)/shard_map/ppermute | solution.py:641
  317.5 145.2 %collective-permute-start.17 = (f32[2,1024,1024]{2,1,0:T(8,128)}, f32[2,1024,1024]{2,1,0:T(8,128)}, u32[]{:S(2)}, u32[]{:S(2)}) collective-permute-start(f32[2,1024,1024]{2,1,0:T(8,128)} %get-tuple-element.243), channel_id=1, source_target_pairs={{0,1},{1,0},{2,3},{3,2},{4,5},{5,4},{6,7},{7,6}} | collective-permute-start | bytes 25165832 | tf_op jit(solution)/shard_map/ppermute | solution.py:646
  317.5 171.7 %collective-permute-start.13 = (bf16[4,1024,1024]{2,1,0:T(8,128)(2,1)}, bf16[4,1024,1024]{2,1,0:T(8,128)(2,1)}, u32[]{:S(2)}, u32[]{:S(2)}) collective-permute-start(bf16[4,1024,1024]{2,1,0:T(8,128)(2,1)} %get-tuple-element.237), channel_id=1, source_target_pairs={{0,1},{1,0},{2,3},{3,2},{4,5},{5,4},{6,7},{7,6}} | collective-permute-start | bytes 25165832 | tf_op jit(solution)/shard_map/ppermute | solution.py:635
  318.0 93.8 %collective-permute-start.4 = (bf16[2,1024,1024]{2,1,0:T(8,128)(2,1)}, bf16[2,1024,1024]{2,1,0:T(8,128)(2,1)}, u32[]{:S(2)}, u32[]{:S(2)}) collective-permute-start(bf16[2,1024,1024]{2,1,0:T(8,128)(2,1)} %get-tuple-element.214.refs_2_), channel_id=1, source_target_pairs={{0,2},{2,0},{1,3},{3,1},{4,6},{6,4},{5,7},{7,5}} | collective-permute-start | bytes 12582920 | tf_op jit(solution)/shard_map/ppermute | solution.py:641
  318.3 170.9 %collective-permute-start.16 = (bf16[1024,1024]{1,0:T(8,128)(2,1)}, bf16[1024,1024]{1,0:T(8,128)(2,1)}, u32[]{:S(2)}, u32[]{:S(2)}) collective-permute-start(bf16[1024,1024]{1,0:T(8,128)(2,1)} %get-tuple-element.242.refs_2_), channel_id=1, source_target_pairs={{0,2},{2,0},{1,3},{3,1},{4,6},{6,4},{5,7},{7,5}} | collective-permute-start | bytes 6291464 | tf_op jit(solution)/shard_map/ppermute | solution.py:641
  320.1 197.2 %collective-permute-start.15 = (bf16[1024,1024]{1,0:T(8,128)(2,1)}, bf16[1024,1024]{1,0:T(8,128)(2,1)}, u32[]{:S(2)}, u32[]{:S(2)}) collective-permute-start(bf16[1024,1024]{1,0:T(8,128)(2,1)} %get-tuple-element.241.refs_2_), channel_id=1, source_target_pairs={{0,2},{2,0},{1,3},{3,1},{4,6},{6,4},{5,7},{7,5}} | collective-permute-start | bytes 6291464 | tf_op jit(solution)/shard_map/ppermute | solution.py:641
  571.3 154.6 %collective-permute-start.23 = (f32[2,1024,1024]{2,1,0:T(8,128)}, f32[2,1024,1024]{2,1,0:T(8,128)}, u32[]{:S(2)}, u32[]{:S(2)}) collective-permute-start(f32[2,1024,1024]{2,1,0:T(8,128)} %get-tuple-element.266), channel_id=1, source_target_pairs={{0,1},{1,0},{2,3},{3,2},{4,5},{5,4},{6,7},{7,6}} | collective-permute-start | bytes 25165832 | tf_op jit(solution)/shard_map/ppermute | solution.py:646
  571.3 181.1 %collective-permute-start.19 = (bf16[4,1024,1024]{2,1,0:T(8,128)(2,1)}, bf16[4,1024,1024]{2,1,0:T(8,128)(2,1)}, u32[]{:S(2)}, u32[]{:S(2)}) collective-permute-start(bf16[4,1024,1024]{2,1,0:T(8,128)(2,1)} %get-tuple-element.260), channel_id=1, source_target_pairs={{0,1},{1,0},{2,3},{3,2},{4,5},{5,4},{6,7},{7,6}} | collective-permute-start | bytes 25165832 | tf_op jit(solution)/shard_map/ppermute | solution.py:635
  571.8 93.8 %collective-permute-start.12 = (bf16[2,1024,1024]{2,1,0:T(8,128)(2,1)}, bf16[2,1024,1024]{2,1,0:T(8,128)(2,1)}, u32[]{:S(2)}, u32[]{:S(2)}) collective-permute-start(bf16[2,1024,1024]{2,1,0:T(8,128)(2,1)} %get-tuple-element.236.refs_2_), channel_id=1, source_target_pairs={{0,2},{2,0},{1,3},{3,1},{4,6},{6,4},{5,7},{7,5}} | collective-permute-start | bytes 12582920 | tf_op jit(solution)/shard_map/ppermute | solution.py:641
  573.5 144.3 %collective-permute-start.24 = (f32[2,512,1024]{2,1,0:T(8,128)}, f32[2,512,1024]{2,1,0:T(8,128)}, u32[]{:S(2)}, u32[]{:S(2)}) collective-permute-start(f32[2,512,1024]{2,1,0:T(8,128)} %get-tuple-element.268), channel_id=1, source_target_pairs={{0,4},{4,0},{1,5},{5,1},{2,6},{6,2},{3,7},{7,3}} | collective-permute-start | bytes 12582920 | tf_op jit(solution)/shard_map/ppermute | solution.py:648
  575.1 177.3 %collective-permute-start.22 = (bf16[1024,1024]{1,0:T(8,128)(2,1)}, bf16[1024,1024]{1,0:T(8,128)(2,1)}, u32[]{:S(2)}, u32[]{:S(2)}) collective-permute-start(bf16[1024,1024]{1,0:T(8,128)(2,1)} %get-tuple-element.265.refs_2_), channel_id=1, source_target_pairs={{0,2},{2,0},{1,3},{3,1},{4,6},{6,4},{5,7},{7,5}} | collective-permute-start | bytes 6291464 | tf_op jit(solution)/shard_map/ppermute | solution.py:641
  665.6 114.8 %collective-permute-start.21 = (bf16[1024,1024]{1,0:T(8,128)(2,1)}, bf16[1024,1024]{1,0:T(8,128)(2,1)}, u32[]{:S(2)}, u32[]{:S(2)}) collective-permute-start(bf16[1024,1024]{1,0:T(8,128)(2,1)} %get-tuple-element.264.refs_2_), channel_id=1, source_target_pairs={{0,2},{2,0},{1,3},{3,1},{4,6},{6,4},{5,7},{7,5}} | collective-permute-start | bytes 6291464 | tf_op jit(solution)/shard_map/ppermute | solution.py:641
  717.9 90.7 %collective-permute-start.20 = (f32[4,2,8,128]{3,2,1,0:T(8,128)}, f32[4,2,8,128]{3,2,1,0:T(8,128)}, u32[]{:S(2)}, u32[]{:S(2)}) collective-permute-start(f32[4,2,8,128]{3,2,1,0:T(8,128)} %get-tuple-element.263.refs_5_), channel_id=1, source_target_pairs={{0,2},{2,0},{1,3},{3,1},{4,6},{6,4},{5,7},{7,5}} | collective-permute-start | bytes 98312 | tf_op jit(solution)/shard_map/ppermute | solution.py:639
  834.4 146.9 %collective-permute-start.31 = (f32[2,1024,1024]{2,1,0:T(8,128)}, f32[2,1024,1024]{2,1,0:T(8,128)}, u32[]{:S(2)}, u32[]{:S(2)}) collective-permute-start(f32[2,1024,1024]{2,1,0:T(8,128)} %get-tuple-element.293), channel_id=1, source_target_pairs={{0,1},{1,0},{2,3},{3,2},{4,5},{5,4},{6,7},{7,6}} | collective-permute-start | bytes 25165832 | tf_op jit(solution)/shard_map/ppermute | solution.py:646
  834.5 182.1 %collective-permute-start.26 = (bf16[4,1024,1024]{2,1,0:T(8,128)(2,1)}, bf16[4,1024,1024]{2,1,0:T(8,128)(2,1)}, u32[]{:S(2)}, u32[]{:S(2)}) collective-permute-start(bf16[4,1024,1024]{2,1,0:T(8,128)(2,1)} %get-tuple-element.286), channel_id=1, source_target_pairs={{0,1},{1,0},{2,3},{3,2},{4,5},{5,4},{6,7},{7,6}} | collective-permute-start | bytes 25165832 | tf_op jit(solution)/shard_map/ppermute | solution.py:635
  834.9 93.8 %collective-permute-start.18 = (bf16[2,1024,1024]{2,1,0:T(8,128)(2,1)}, bf16[2,1024,1024]{2,1,0:T(8,128)(2,1)}, u32[]{:S(2)}, u32[]{:S(2)}) collective-permute-start(bf16[2,1024,1024]{2,1,0:T(8,128)(2,1)} %get-tuple-element.259.refs_2_), channel_id=1, source_target_pairs={{0,2},{2,0},{1,3},{3,1},{4,6},{6,4},{5,7},{7,5}} | collective-permute-start | bytes 12582920 | tf_op jit(solution)/shard_map/ppermute | solution.py:641
  836.7 144.3 %collective-permute-start.32 = (f32[2,512,1024]{2,1,0:T(8,128)}, f32[2,512,1024]{2,1,0:T(8,128)}, u32[]{:S(2)}, u32[]{:S(2)}) collective-permute-start(f32[2,512,1024]{2,1,0:T(8,128)} %get-tuple-element.295), channel_id=1, source_target_pairs={{0,4},{4,0},{1,5},{5,1},{2,6},{6,2},{3,7},{7,3}} | collective-permute-start | bytes 12582920 | tf_op jit(solution)/shard_map/ppermute | solution.py:648
  838.3 178.2 %collective-permute-start.30 = (bf16[1024,1024]{1,0:T(8,128)(2,1)}, bf16[1024,1024]{1,0:T(8,128)(2,1)}, u32[]{:S(2)}, u32[]{:S(2)}) collective-permute-start(bf16[1024,1024]{1,0:T(8,128)(2,1)} %get-tuple-element.292.refs_2_), channel_id=1, source_target_pairs={{0,2},{2,0},{1,3},{3,1},{4,6},{6,4},{5,7},{7,5}} | collective-permute-start | bytes 6291464 | tf_op jit(solution)/shard_map/ppermute | solution.py:641
  928.7 115.8 %collective-permute-start.29 = (bf16[1024,1024]{1,0:T(8,128)(2,1)}, bf16[1024,1024]{1,0:T(8,128)(2,1)}, u32[]{:S(2)}, u32[]{:S(2)}) collective-permute-start(bf16[1024,1024]{1,0:T(8,128)(2,1)} %get-tuple-element.291.refs_2_), channel_id=1, source_target_pairs={{0,2},{2,0},{1,3},{3,1},{4,6},{6,4},{5,7},{7,5}} | collective-permute-start | bytes 6291464 | tf_op jit(solution)/shard_map/ppermute | solution.py:641
  981.0 91.8 %collective-permute-start.28 = (bf16[1024,1024]{1,0:T(8,128)(2,1)}, bf16[1024,1024]{1,0:T(8,128)(2,1)}, u32[]{:S(2)}, u32[]{:S(2)}) collective-permute-start(bf16[1024,1024]{1,0:T(8,128)(2,1)} %get-tuple-element.290.refs_2_), channel_id=1, source_target_pairs={{0,2},{2,0},{1,3},{3,1},{4,6},{6,4},{5,7},{7,5}} | collective-permute-start | bytes 6291464 | tf_op jit(solution)/shard_map/ppermute | solution.py:641
  981.3 119.3 %collective-permute-start.27 = (f32[4,2,8,128]{3,2,1,0:T(8,128)}, f32[4,2,8,128]{3,2,1,0:T(8,128)}, u32[]{:S(2)}, u32[]{:S(2)}) collective-permute-start(f32[4,2,8,128]{3,2,1,0:T(8,128)} %get-tuple-element.289.refs_5_), channel_id=1, source_target_pairs={{0,2},{2,0},{1,3},{3,1},{4,6},{6,4},{5,7},{7,5}} | collective-permute-start | bytes 98312 | tf_op jit(solution)/shard_map/ppermute | solution.py:639
  1126.9 180.0 %collective-permute-start.34 = (bf16[4,1024,1024]{2,1,0:T(8,128)(2,1)}, bf16[4,1024,1024]{2,1,0:T(8,128)(2,1)}, u32[]{:S(2)}, u32[]{:S(2)}) collective-permute-start(bf16[4,1024,1024]{2,1,0:T(8,128)(2,1)} %get-tuple-element.320), channel_id=1, source_target_pairs={{0,1},{1,0},{2,3},{3,2},{4,5},{5,4},{6,7},{7,6}} | collective-permute-start | bytes 25165832 | tf_op jit(solution)/shard_map/ppermute | solution.py:635
  1258.0 160.4 %collective-permute-start.35 = (f32[2,512,1024]{2,1,0:T(8,128)}, f32[2,512,1024]{2,1,0:T(8,128)}, u32[]{:S(2)}, u32[]{:S(2)}) collective-permute-start(f32[2,512,1024]{2,1,0:T(8,128)} %get-tuple-element.322), channel_id=1, source_target_pairs={{0,4},{4,0},{1,5},{5,1},{2,6},{6,2},{3,7},{7,3}} | collective-permute-start | bytes 12582920 | tf_op jit(solution)/shard_map/ppermute | solution.py:648
  1259.7 97.4 %collective-permute-start.37 = (bf16[1024,1024]{1,0:T(8,128)(2,1)}, bf16[1024,1024]{1,0:T(8,128)(2,1)}, u32[]{:S(2)}, u32[]{:S(2)}) collective-permute-start(bf16[1024,1024]{1,0:T(8,128)(2,1)} %get-tuple-element.324.refs_2_), channel_id=1, source_target_pairs={{0,2},{2,0},{1,3},{3,1},{4,6},{6,4},{5,7},{7,5}} | collective-permute-start | bytes 6291464 | tf_op jit(solution)/shard_map/ppermute | solution.py:641
  1306.8 132.6 %collective-permute-start.33 = (bf16[1024,1024]{1,0:T(8,128)(2,1)}, bf16[1024,1024]{1,0:T(8,128)(2,1)}, u32[]{:S(2)}, u32[]{:S(2)}) collective-permute-start(bf16[1024,1024]{1,0:T(8,128)(2,1)} %get-tuple-element.319.refs_2_), channel_id=1, source_target_pairs={{0,2},{2,0},{1,3},{3,1},{4,6},{6,4},{5,7},{7,5}} | collective-permute-start | bytes 6291464 | tf_op jit(solution)/shard_map/ppermute | solution.py:641
  1464.2 93.8 %collective-permute-start.44 = (f32[2,512,1024]{2,1,0:T(8,128)}, f32[2,512,1024]{2,1,0:T(8,128)}, u32[]{:S(2)}, u32[]{:S(2)}) collective-permute-start(f32[2,512,1024]{2,1,0:T(8,128)} %get-tuple-element.360), channel_id=1, source_target_pairs={{0,4},{4,0},{1,5},{5,1},{2,6},{6,2},{3,7},{7,3}} | collective-permute-start | bytes 12582920 | tf_op jit(solution)/shard_map/ppermute | solution.py:648
  1483.2 164.6 %collective-permute-start.46 = (f32[2,512,1024]{2,1,0:T(8,128)}, f32[2,512,1024]{2,1,0:T(8,128)}, u32[]{:S(2)}, u32[]{:S(2)}) collective-permute-start(f32[2,512,1024]{2,1,0:T(8,128)} %get-tuple-element.368), channel_id=1, source_target_pairs={{0,4},{4,0},{1,5},{5,1},{2,6},{6,2},{3,7},{7,3}} | collective-permute-start | bytes 12582920 | tf_op jit(solution)/shard_map/ppermute | solution.py:648
  1599.3 136.8 %collective-permute-start.47 = (f32[2,512,1024]{2,1,0:T(8,128)}, f32[2,512,1024]{2,1,0:T(8,128)}, u32[]{:S(2)}, u32[]{:S(2)}) collective-permute-start(f32[2,512,1024]{2,1,0:T(8,128)} %get-tuple-element.374), channel_id=1, source_target_pairs={{0,4},{4,0},{1,5},{5,1},{2,6},{6,2},{3,7},{7,3}} | collective-permute-start | bytes 12582920 | tf_op jit(solution)/shard_map/ppermute | solution.py:648
  (18 other events, 849.7 us)
